TPU v7x, 256 devices: a whole 4x4x8 slice. The times are simulated.
256 devices in a mesh: row: 8 (over x, y_lo), blk: 32 (over y_hi, z, core).
Axes of the slice: x: 4, y: 4 (y_hi: 2, y_lo: 2; y = y_hi * 2 + y_lo), z: 8, core: 2. Of those that a mesh axis runs over, the one named last changes fastest.
Arguments:
- elastic_kernel: bfloat16 [32, 1024, 8, 4096], P('blk', None, 'row'), may hold values from -0.046875 to 0.046875
- slip_deficit: float32 [32, 8, 128, 512], P('blk', 'row'), may hold values from -6 to 6
- state_variable: float32 [32, 8, 128, 512], P('blk', 'row'), may hold values from 0.2 to 5
- step_size: float32 [512], replicated, may hold values from 0.02 to 0.1
- load_stress: float32 [32, 8, 128], P('blk', 'row'), may hold values from -6 to 6
- normal_stress: float32 [32, 8, 128], P('blk', 'row'), may hold values from 0.5 to 2
- rate_table: float32 [16], replicated, may hold values from 0.3 to 1
- evolve_table: float32 [16], replicated, may hold values from 0.3 to 1.5
- patch_region: int32 [32, 8, 128], P('blk', 'row'), may hold values from 0 to 15
- creep_flag: int32 [32, 8, 128], P('blk', 'row'), may hold values 0 or 1
Outputs:
- velocity: float32 [32, 8, 128, 512], P('blk', 'row')
- deficit_out: float32 [32, 8, 128, 512], P('blk', 'row')
- state_out: float32 [32, 8, 128, 512], P('blk', 'row')
- step_next: float32 [512], replicated
All inputs are finite; a program needn't handle non-finite values. Where the computation divides by a largest or mean magnitude, that divisor is 1e-20 or more. No bound on the sum of `creep_flag` on one device may be relied on, other than what follows from the above.
Results may differ from a plain program's by a relative error of at most 0.0035.
Values may be sent and summed in bfloat16 or wider, within the bound.
No kernel may reach another device: no remote copies, remote signals or barrier semaphores. Data moves between devices by JAX's collectives and lax.ppermute only.
A program may use at most 64 MiB of HBM per device.

v0:
```python
import functools

import jax
import jax.numpy as jnp
from jax import lax
from jax.sharding import Mesh
from jax.sharding import PartitionSpec as P

NEWTON = 3
BLK = ("blk_0", "blk_1", "blk_2")
ROW = ("row_0", "row_1")
ROW_BLK = ("row_0", "row_1", "blk_0", "blk_1", "blk_2")


DAMPING = 0.5
PLATE_RATE = 1.0
STEP_CAP = 0.5


def in_order(parts, dim):
    dims = list(parts.shape[1:])
    dims[dim] *= parts.shape[0]
    return jnp.moveaxis(parts, 0, dim).reshape(dims)


def gather_in_order(x, axes, order):
    parts = x
    for k in order:
        parts = lax.all_gather(parts, axes[k])
    done = order[::-1]
    back = [done.index(k) for k in range(len(axes))]
    parts = parts.transpose(*back, *range(len(axes), parts.ndim))
    return parts.reshape(-1, *x.shape)


def whole_of(x, axes, order, dim):
    return in_order(gather_in_order(x, axes, order), dim)


def cut_along(x, dim, count):
    dims = x.shape
    parts = x.reshape(*dims[:dim], count, dims[dim] // count, *dims[dim + 1 :])
    return jnp.moveaxis(parts, dim, 0)


def summed_on_arrival(x, axis, dim):
    count = lax.axis_size(axis)
    parts = lax.all_to_all(cut_along(x, dim, count), axis, 0, 0, tiled=True)
    return jnp.sum(parts.astype(jnp.float32), axis=0)


def over_axes(x, axes):
    return functools.reduce(lax.pmax, axes, x)


def inverse_sinh(value):
    magnitude = jnp.abs(value)
    result = jnp.log(magnitude + jnp.sqrt(magnitude * magnitude + 1.0))
    return jnp.where(value < 0.0, -result, result)


def solve_rate(stress, pressure, rate_coef, state_coef, state, creeping):
    factor = 0.5 * jnp.exp(state_coef * jnp.log(state) / rate_coef)
    strength = pressure * rate_coef
    speed = stress / (strength * factor + DAMPING)
    for repeat in range(NEWTON):
        scaled = factor * speed
        mismatch = strength * inverse_sinh(scaled) + DAMPING * speed - stress
        gradient = strength * factor / jnp.sqrt(1.0 + scaled * scaled) + DAMPING
        speed = speed - mismatch / gradient
    return jnp.where(creeping, jnp.float32(PLATE_RATE), speed)


def advance(state, deficit, velocity, step_now):
    new_state = state * jnp.exp(step_now * (1.0 / state - jnp.abs(velocity)))
    new_deficit = deficit + step_now * (velocity - PLATE_RATE)
    return (new_state, new_deficit)


def body(
    elastic_kernel,
    slip_deficit,
    state_variable,
    step_size,
    load_stress,
    normal_stress,
    rate_table,
    evolve_table,
    patch_region,
    creep_flag,
):
    kernel_tile = elastic_kernel.reshape(elastic_kernel.shape[1], elastic_kernel.shape[3])
    elements = slip_deficit.shape[2]
    members = slip_deficit.shape[3]
    levels = jnp.arange(rate_table.shape[0], dtype=jnp.int32)
    onehot = (patch_region[..., None] == levels).astype(jnp.float32)
    rate_coef = jnp.sum(onehot * rate_table, axis=-1)[..., None]
    state_coef = jnp.sum(onehot * evolve_table, axis=-1)[..., None]
    pressure = normal_stress[..., None]
    loading = load_stress[..., None]
    creeping = (creep_flag == 1)[..., None]

    def traction_of(deficit):
        slip = deficit.astype(jnp.bfloat16)
        shards = whole_of(slip, BLK, (0, 1, 2), 0)
        breadth = shards.shape[0] * elements
        partial_sum = jnp.dot(
            kernel_tile, shards.reshape(breadth, members), preferred_element_type=jnp.float32
        )
        owned = summed_on_arrival(partial_sum.astype(jnp.bfloat16), ROW, 0)
        return owned.reshape(slip.shape)

    def velocity_of(deficit, state):
        stress = loading + traction_of(deficit)
        return solve_rate(stress, pressure, rate_coef, state_coef, state, creeping)

    deficit = slip_deficit
    state = state_variable
    step_now = step_size
    velocity = velocity_of(deficit, state)
    local_first = jnp.max(jnp.abs(velocity), axis=(0, 1, 2))
    state, deficit = advance(state, deficit, velocity, step_now)
    velocity = velocity_of(deficit, state)
    local_second = jnp.max(jnp.abs(velocity), axis=(0, 1, 2))
    maxima = over_axes(jnp.stack([local_first, local_second]), ROW_BLK)
    state, deficit = advance(state, deficit, velocity, STEP_CAP / (1.0 + maxima[0]))
    step_now = STEP_CAP / (1.0 + maxima[1])
    return (velocity, deficit, state, step_now)


def solution(mesh):
    torus = Mesh(mesh.devices.reshape(4, 2, 2, 8, 2), ("row_0", "row_1", "blk_0", "blk_1", "blk_2"))
    in_specs = (
        P(BLK, None, ROW, None),
        P(BLK, ROW, None, None),
        P(BLK, ROW, None, None),
        P(),
        P(BLK, ROW, None),
        P(BLK, ROW, None),
        P(),
        P(),
        P(BLK, ROW, None),
        P(BLK, ROW, None),
    )
    out_specs = (P(BLK, ROW, None, None), P(BLK, ROW, None, None), P(BLK, ROW, None, None), P())
    return jax.shard_map(body, mesh=torus, in_specs=in_specs, out_specs=out_specs, check_vma=False)
```

profile of v0, /device:TPU:1, one launch (start us, length us, event | category | flops | bytes accessed | tf_op | source)
XLA Modules:
  0.0 260.3 jit_solution(6911714111795193618)
XLA Ops:
  7.2 0.0 all-gather.11.cloned.1.call-start
  7.2 1.0 convert_element_type.22
  8.2 6.8 %all-gather = bf16[2,1,128,512]{3,2,1,0:T(8,128)(2,1)} all-gather(bf16[1,1,128,512]{3,2,1,0:T(8,128)(2,1)S(1)} %convert_element_type.22), channel_id=2, replica_groups=mesh['row_0'=4,'row_1'=2,'blk_0'=2,'blk_1'=8,'blk_2'=2] {'blk_0'}, dimensions={0}, use_global_device_ids=true | all-gather | bytes 393216 | tf_op jit(solution)/shard_map/all_gather | solution.py:29
  15.0 0.0 all-gather.11.cloned.1.call-update
  15.1 0.0 all-gather.13.cloned.1.call-start
  15.1 41.2 %all-gather.11.cloned.1.call-done = bf16[16,1,128,512]{3,2,1,0:T(8,128)(2,1)} async-done(((bf16[2,1,128,512]{3,2,1,0:T(8,128)(2,1)}), bf16[16,1,128,512]{3,2,1,0:T(8,128)(2,1)}) %all-gather.11.cloned.1.call-update) | async-done | bytes 2097168 | tf_op jit(solution)/shard_map/all_gather | solution.py:29
  56.3 0.0 all-gather.13.cloned.1.call-update
  56.4 24.3 %all-gather.13.cloned.1.call-done = bf16[16,2,1,1,128,512]{5,4,3,2,1,0:T(8,128)(2,1)} async-done(((bf16[8,2,1,1,128,512]{5,4,3,2,1,0:T(8,128)(2,1)}), bf16[16,2,1,1,128,512]{5,4,3,2,1,0:T(8,128)(2,1)}) %all-gather.13.cloned.1.call-update) | async-done | bytes 4194320 | tf_op jit(solution)/shard_map/all_gather | solution.py:29
  80.6 0.0 copy-start.8
  80.6 2.8 %copy.38 = bf16[2,8,2,1,1,128,512]{6,5,2,1,0,4,3:T(8,128)(2,1)S(1)} copy(bf16[2,8,2,1,1,128,512]{6,5,0,1,2,4,3:T(8,128)(2,1)} %bitcast.55) | data formatting | bytes 8388608 | tf_op jit(solution)/shard_map/transpose | solution.py:32
  83.4 1.8 copy-done.8
  85.3 0.0 copy-start.4
  85.3 0.0 copy-start.5
  85.3 0.0 copy-start.6
  85.3 0.0 copy-start.9
  85.3 0.0 copy-start.7
  85.3 0.0 copy-start.1
  85.3 0.0 copy-start.10
  85.3 5.5 %fusion.4 = bf16[1024,512]{1,0:T(8,128)(2,1)} fusion(bf16[4096,512]{1,0:T(8,128)(2,1)S(1)} %bitcast.57, bf16[1,1024,1,4096]{3,1,2,0:T(8,128)(2,1)S(1)} %copy-done.8), kind=kOutput, calls=%fused_computation.6 | convolution fusion | flops 4295491584 | bytes 13631488 | tf_op jit(solution)/shard_map/dot_general | solution.py:107
  90.8 0.0 copy-start
  90.8 0.0 copy-start.3
  90.8 4.8 %all-to-all-start = ((bf16[8,128,512]{2,1,0:T(8,128)(2,1)}), bf16[8,128,512]{2,1,0:T(8,128)(2,1)S(1)}, u32[]{:S(2)}, u32[]{:S(2)}) async-start(bf16[8,128,512]{2,1,0:T(8,128)(2,1)} %bitcast.8), calls=%async_computation | async-start | bytes 2097152 | tf_op jit(solution)/shard_map/all_to_all | solution.py:48
  95.6 0.0 all-gather.15.cloned.1.call-start
  95.6 0.0 copy-done.4
  95.6 0.0 copy-done.5
  95.6 0.0 copy-done.6
  95.6 0.1 select_reduce_fusion.1
  95.7 0.0 copy-done.9
  95.7 0.0 copy-done.7
  95.8 15.8 %all-to-all-done = bf16[8,128,512]{2,1,0:T(8,128)(2,1)S(1)} async-done(((bf16[8,128,512]{2,1,0:T(8,128)(2,1)}), bf16[8,128,512]{2,1,0:T(8,128)(2,1)S(1)}, u32[]{:S(2)}, u32[]{:S(2)}) %all-to-all-start) | async-done | bytes 1048608 | tf_op jit(solution)/shard_map/all_to_all | solution.py:48
  111.5 0.2 convert_reduce_fusion.1
  111.7 0.0 copy-done.1
  111.7 0.0 copy-done.10
  111.7 1.0 abs_reduce_fusion.1
  112.7 0.0 copy-done
  112.7 0.0 copy-done.3
  112.7 0.1 fusion.45
  112.8 6.1 %all-gather.3 = bf16[2,1,128,512]{3,2,1,0:T(8,128)(2,1)} all-gather(bf16[1,1,128,512]{3,2,1,0:T(8,128)(2,1)S(1)} %fusion.45), channel_id=5, replica_groups=mesh['row_0'=4,'row_1'=2,'blk_0'=2,'blk_1'=8,'blk_2'=2] {'blk_0'}, dimensions={0}, use_global_device_ids=true | all-gather | bytes 393216 | tf_op jit(solution)/shard_map/all_gather | solution.py:29
  118.9 0.0 all-gather.15.cloned.1.call-update
  118.9 0.0 all-gather.17.cloned.1.call-start
  119.0 37.6 %all-gather.15.cloned.1.call-done = bf16[16,1,128,512]{3,2,1,0:T(8,128)(2,1)} async-done(((bf16[2,1,128,512]{3,2,1,0:T(8,128)(2,1)}), bf16[16,1,128,512]{3,2,1,0:T(8,128)(2,1)}) %all-gather.15.cloned.1.call-update) | async-done | bytes 2097168 | tf_op jit(solution)/shard_map/all_gather | solution.py:29
  156.5 0.0 all-gather.17.cloned.1.call-update
  156.6 24.1 %all-gather.17.cloned.1.call-done = bf16[16,2,1,1,128,512]{5,4,3,2,1,0:T(8,128)(2,1)} async-done(((bf16[8,2,1,1,128,512]{5,4,3,2,1,0:T(8,128)(2,1)}), bf16[16,2,1,1,128,512]{5,4,3,2,1,0:T(8,128)(2,1)}) %all-gather.17.cloned.1.call-update) | async-done | bytes 4194320 | tf_op jit(solution)/shard_map/all_gather | solution.py:29
  180.7 2.5 copy.40
  183.2 7.1 %fusion.10 = bf16[64,8,8,128]{3,2,1,0:T(8,128)(2,1)S(1)} fusion(bf16[4096,512]{1,0:T(8,128)(2,1)S(1)} %bitcast.58, bf16[1,1024,1,4096]{3,1,2,0:T(8,128)(2,1)} %param.10), kind=kOutput, calls=%fused_computation.8 | convolution fusion | flops 4295491584 | bytes 13631488 | tf_op jit(solution)/shard_map/dot_general | solution.py:107
  190.3 0.2 copy.47
  190.5 18.8 %all_to_all.10 = bf16[8,128,512]{1,2,0:T(8,128)(2,1)S(1)} all-to-all(bf16[8,128,512]{1,2,0:T(8,128)(2,1)S(1)} %bitcast.59), channel_id=1, replica_groups=mesh['row_0'=4,'row_1'=2,'blk_0'=2,'blk_1'=8,'blk_2'=2] {'row_0','row_1'}, dimensions={0} | all-to-all | bytes 2097152 | tf_op jit(solution)/shard_map/all_to_all | solution.py:48
  209.3 0.1 convert_reduce_fusion
  209.5 0.1 copy.43
  209.6 1.0 abs_reduce_fusion
  210.7 0.0 copy-start.2
  210.7 7.0 %pmax.35 = f32[2,512]{1,0:T(2,128)S(1)} all-reduce(f32[2,512]{1,0:T(2,128)S(1)} %pad_maximum_fusion), channel_id=1, replica_groups=mesh['row_0'=4,'row_1'=2,'blk_0'=2,'blk_1'=8,'blk_2'=2] {'row_0'}, use_global_device_ids=true, to_apply=%region_6.7 | all-reduce | flops 1024 | bytes 8192 | tf_op jit(solution)/shard_map/pmax | solution.py:53
  217.7 3.8 %pmax.36 = f32[2,512]{1,0:T(2,128)S(1)} all-reduce(f32[2,512]{1,0:T(2,128)S(1)} %pmax.35), channel_id=1, replica_groups=mesh['row_0'=4,'row_1'=2,'blk_0'=2,'blk_1'=8,'blk_2'=2] {'row_1'}, use_global_device_ids=true, to_apply=%region_7.8 | all-reduce | flops 1024 | bytes 8192 | tf_op jit(solution)/shard_map/pmax | solution.py:53
  221.4 5.3 %pmax.37 = f32[2,512]{1,0:T(2,128)S(1)} all-reduce(f32[2,512]{1,0:T(2,128)S(1)} %pmax.36), channel_id=1, replica_groups=mesh['row_0'=4,'row_1'=2,'blk_0'=2,'blk_1'=8,'blk_2'=2] {'blk_0'}, use_global_device_ids=true, to_apply=%region_8.9 | all-reduce | flops 1024 | bytes 8192 | tf_op jit(solution)/shard_map/pmax | solution.py:53
  226.7 14.0 %pmax.38 = f32[2,512]{1,0:T(2,128)S(1)} all-reduce(f32[2,512]{1,0:T(2,128)S(1)} %pmax.37), channel_id=1, replica_groups=mesh['row_0'=4,'row_1'=2,'blk_0'=2,'blk_1'=8,'blk_2'=2] {'blk_1'}, use_global_device_ids=true, to_apply=%region_9.10 | all-reduce | flops 1024 | bytes 8192 | tf_op jit(solution)/shard_map/pmax | solution.py:53
  240.7 11.5 %pmax.39 = f32[2,512]{1,0:T(2,128)S(1)} all-reduce(f32[2,512]{1,0:T(2,128)S(1)} %pmax.38), channel_id=1, replica_groups=mesh['row_0'=4,'row_1'=2,'blk_0'=2,'blk_1'=8,'blk_2'=2] {'blk_2'}, use_global_device_ids=true, to_apply=%region_10.11 | all-reduce | flops 1024 | bytes 8192 | tf_op jit(solution)/shard_map/pmax | solution.py:53
  252.2 0.6 fusion.46
  252.8 1.0 exponential_multiply_fusion
  253.7 0.0 copy-done.2
  (3 shorter events, 0.0 us)
Async XLA Ops:
  7.2 49.2 %all-gather.11.cloned.1.call-start = ((), (), s32[]{:S(2)}) async-start(), calls=%async_computation.2 | async-start | bytes 2359296 | tf_op jit(solution)/shard_map/all_gather | solution.py:29
  15.1 65.6 %all-gather.13.cloned.1.call-start = ((), (), s32[]{:S(2)}) async-start(), calls=%async_computation.3 | async-start | bytes 6291456 | tf_op jit(solution)/shard_map/all_gather | solution.py:29
  80.6 4.6 %copy-start.8 = (bf16[1,1024,1,4096]{3,1,2,0:T(8,128)(2,1)S(1)}, bf16[1,1024,1,4096]{3,1,2,0:T(8,128)(2,1)}, u32[]{:S(2)}) copy-start(bf16[1,1024,1,4096]{3,1,2,0:T(8,128)(2,1)} %param.10) | copy-start | bytes 25165828
  85.3 10.3 %copy-start.4 = (f32[16]{0:T(128)S(1)}, f32[16]{0:T(128)}, u32[]{:S(2)}) copy-start(f32[16]{0:T(128)} %param.17) | copy-start | bytes 196
  85.3 10.3 %copy-start.5 = (s32[1,1,128]{2,1,0:T(1,128)S(1)}, s32[1,1,128]{2,1,0:T(1,128)}, u32[]{:S(2)}) copy-start(s32[1,1,128]{2,1,0:T(1,128)} %param.18) | copy-start | bytes 1540
  85.3 10.4 %copy-start.6 = (f32[16]{0:T(128)S(1)}, f32[16]{0:T(128)}, u32[]{:S(2)}) copy-start(f32[16]{0:T(128)} %param.16) | copy-start | bytes 196
  85.3 10.5 %copy-start.9 = (s32[1,1,128]{2,1,0:T(1,128)S(1)}, s32[1,1,128]{2,1,0:T(1,128)}, u32[]{:S(2)}) copy-start(s32[1,1,128]{2,1,0:T(1,128)} %param.19) | copy-start | bytes 1540
  85.3 10.5 %copy-start.7 = (f32[1,1,128]{2,1,0:T(1,128)S(1)}, f32[1,1,128]{2,1,0:T(1,128)}, u32[]{:S(2)}) copy-start(f32[1,1,128]{2,1,0:T(1,128)} %param.15) | copy-start | bytes 1540
  85.3 26.4 %copy-start.1 = (f32[1,1,128,512]{3,2,1,0:T(8,128)S(1)}, f32[1,1,128,512]{3,2,1,0:T(8,128)}, u32[]{:S(2)}) copy-start(f32[1,1,128,512]{3,2,1,0:T(8,128)} %param.12) | copy-start | bytes 786436
  85.3 26.4 %copy-start.10 = (f32[1,1,128]{2,1,0:T(1,128)S(1)}, f32[1,1,128]{2,1,0:T(1,128)}, u32[]{:S(2)}) copy-start(f32[1,1,128]{2,1,0:T(1,128)} %param.14) | copy-start | bytes 1540
  90.8 21.9 %copy-start = (f32[1,1,128,512]{3,2,1,0:T(8,128)S(1)}, f32[1,1,128,512]{3,2,1,0:T(8,128)}, u32[]{:S(2)}) copy-start(f32[1,1,128,512]{3,2,1,0:T(8,128)} %param.11) | copy-start | bytes 786436
  90.8 21.9 %copy-start.3 = (f32[512]{0:T(512)S(1)}, f32[512]{0:T(512)}, u32[]{:S(2)}) copy-start(f32[512]{0:T(512)} %param.13) | copy-start | bytes 6148
  90.8 20.7 %all-to-all-start = ((bf16[8,128,512]{2,1,0:T(8,128)(2,1)}), bf16[8,128,512]{2,1,0:T(8,128)(2,1)S(1)}, u32[]{:S(2)}, u32[]{:S(2)}) async-start(bf16[8,128,512]{2,1,0:T(8,128)(2,1)} %bitcast.8), calls=%async_computation | async-start | bytes 2097152 | tf_op jit(solution)/shard_map/all_to_all | solution.py:48
  95.6 61.0 %all-gather.15.cloned.1.call-start = ((), (), s32[]{:S(2)}) async-start(), calls=%async_computation.4 | async-start | bytes 2359296 | tf_op jit(solution)/shard_map/all_gather | solution.py:29
  118.9 61.8 %all-gather.17.cloned.1.call-start = ((), (), s32[]{:S(2)}) async-start(), calls=%async_computation.5 | async-start | bytes 6291456 | tf_op jit(solution)/shard_map/all_gather | solution.py:29
  210.7 43.1 %copy-start.2 = (f32[1,1,128,512]{3,2,1,0:T(8,128)}, f32[1,1,128,512]{3,2,1,0:T(8,128)S(1)}, u32[]{:S(2)}) copy-start(f32[1,1,128,512]{3,2,1,0:T(8,128)S(1)} %get-tuple-element.13) | copy-start | bytes 786436
Sparse Core Ops, SparseCore 0:
  15.2 41.1 all-gather.10
  58.1 22.4 all-gather.12
  119.0 37.4 all-gather.14
  158.2 22.4 all-gather.16
where the time goes:
time: 261 us; the launch traced here: 260 us
  waiting for transfers between devices  143 us (55%)
  blocking collectives  73.2 us (28%)
  between operations  13.9 us (5%)
  matrix products  12.6 us (5%)
  local copies, waits for them, and re-layouts  7.45 us (3%)
  other arithmetic  5.04 us (2%)
  starting transfers between devices  4.93 us (2%)
    all_gather x4, waiting for transfers between devices, gather_in_order(): parts = lax.all_gather(parts, axes[k])  127 us
    pmax x5, blocking collectives, over_axes(): return functools.reduce(lax.pmax, axes, x)  41.5 us
    all_to_all x1, blocking collectives, summed_on_arrival(): parts = lax.all_to_all(cut_along(x, dim, count), axis, 0, 0, tiled=True)  18.8 us
    all_to_all x1, waiting for transfers between devices, summed_on_arrival(): parts = lax.all_to_all(cut_along(x, dim, count), axis, 0, 0, tiled=True)  15.8 us
    all_gather x2, blocking collectives, gather_in_order(): parts = lax.all_gather(parts, axes[k])  12.9 us
    dot_general x2, matrix products, traction_of(): jnp.dot(kernel_tile, shards.reshape(breadth, members), preferred_element_...  12.6 us
    transpose x2, local copies, waits for them, and re-layouts, gather_in_order(): parts = parts.transpose(*back, *range(len(axes), parts.ndim))  5.24 us
  transfers between devices with their start and end apart: 5, of which 5 were waited for; matrix products, arithmetic and copies ran while one was open for 0% of the time, Pallas kernels for 0%

commit v1 on v0

v1 whole, which is shorter than its diff:
```python
import functools

import jax
import jax.numpy as jnp
from jax import lax
from jax.sharding import Mesh
from jax.sharding import PartitionSpec as P


NEWTON = 3
STEPS = 2
BLK = ("yh", "z", "c")
ROW = ("x", "yl")
CHIPS = ("x", "yl", "yh", "z")

DAMPING = 0.5
PLATE_RATE = 1.0
STEP_CAP = 0.5


def inverse_sinh(value):
    magnitude = jnp.abs(value)
    result = jnp.log(magnitude + jnp.sqrt(magnitude * magnitude + 1.0))
    return jnp.where(value < 0.0, -result, result)


def solve_rate(stress, pressure, rate_coef, state_coef, state, creeping):
    factor = 0.5 * jnp.exp(state_coef * jnp.log(state) / rate_coef)
    strength = pressure * rate_coef
    speed = stress / (strength * factor + DAMPING)
    for _ in range(NEWTON):
        scaled = factor * speed
        mismatch = strength * inverse_sinh(scaled) + DAMPING * speed - stress
        gradient = strength * factor / jnp.sqrt(1.0 + scaled * scaled) + DAMPING
        speed = speed - mismatch / gradient
    return jnp.where(creeping, jnp.float32(PLATE_RATE), speed)


def advance(state, deficit, velocity, step_now):
    new_state = state * jnp.exp(step_now * (1.0 / state - jnp.abs(velocity)))
    new_deficit = deficit + step_now * (velocity - PLATE_RATE)
    return (new_state, new_deficit)


def swap_cores(x):
    return lax.ppermute(x, "c", ((0, 1), (1, 0)))


def swap_far(x):
    return lax.ppermute(x, "yh", ((0, 1), (1, 0)))


def shifted(x, by):
    depth = lax.axis_size("z")
    return lax.ppermute(x, "z", [(z, (z + by) % depth) for z in range(depth)])


def body(
    elastic_kernel,
    slip_deficit,
    state_variable,
    step_size,
    load_stress,
    normal_stress,
    rate_table,
    evolve_table,
    patch_region,
    creep_flag,
):
    kernel_tile = elastic_kernel.reshape(elastic_kernel.shape[1], elastic_kernel.shape[3])
    elements = slip_deficit.shape[2]
    members = slip_deficit.shape[3]
    core = lax.axis_index("c")
    depth = lax.axis_size("z")
    here = lax.axis_index("z")
    near = lax.axis_index("yh")
    first = core == 0

    fault = (rate_table, evolve_table, patch_region, creep_flag, normal_stress, load_stress)

    def coefs_of(fault):
        rate_table, evolve_table, patch_region, creep_flag, normal_stress, load_stress = fault
        levels = jnp.arange(rate_table.shape[0], dtype=jnp.int32)
        onehot = (patch_region.reshape(elements)[:, None] == levels).astype(jnp.float32)
        rate_coef = jnp.sum(onehot * rate_table, axis=-1)[:, None]
        state_coef = jnp.sum(onehot * evolve_table, axis=-1)[:, None]
        pressure = normal_stress.reshape(elements, 1)
        loading = load_stress.reshape(elements, 1)
        creeping = creep_flag.reshape(elements, 1)
        return (rate_coef, state_coef, pressure, loading, creeping)

    half = depth * 2 * elements

    def tile_of(side):
        return lax.dynamic_slice(kernel_tile, (0, side * half), (kernel_tile.shape[0], half))

    def swapped(blocks):
        both = swap_cores(jnp.concatenate([block for _, block in blocks]))
        span = blocks[0][1].shape[0]
        return [(shift, both[i * span : (i + 1) * span]) for i, (shift, _) in enumerate(blocks)]

    def after(blocks, token):
        held, _ = lax.optimization_barrier(([block for _, block in blocks], token))
        return [(shift, block) for (shift, _), block in zip(blocks, held)]

    def joined(rows):
        return rows[0].astype(jnp.float32) + rows[1].astype(jnp.float32)

    def gathered(block):
        found = [joined(block[elements:])]

        def marked(block, by):
            block = shifted(block, by)
            found.append(joined(block[elements:]))
            return block

        far = swap_far(block)
        found.append(joined(far[elements:]))
        start = [[(0, block)], [(0, far)]]
        up, down = [block, far], [block, far]
        hops = [[], []]
        for hop in (1, 2, 3):
            for side in (0, 1):
                up[side] = marked(up[side], 1)
                down[side] = marked(down[side], -1)
                hops[side].append([(-hop, up[side]), (hop, down[side])])
        last = [[(4, marked(up[0], 1))], [(4, marked(down[1], -1))]]
        mine = [start[side] + sum(hops[side], []) + last[side] for side in (0, 1)]
        token = (up[0], down[0], up[1], down[1])
        other = [
            swapped(after(start[side] + hops[side][0] + hops[side][1], token))
            for side in (0, 1)
        ]
        other[0] += swapped(hops[0][2] + last[0])
        other[1] += swapped(hops[1][2]) + swapped(last[1])
        found += [joined(block[elements:]) for side in other for _, block in side]
        return mine, other, found

    def placed(mine, other):
        slips = jnp.zeros((half, members), jnp.bfloat16)
        for owner_core, blocks in ((core, mine), (1 - core, other)):
            for shift, block in blocks:
                owner = 2 * lax.rem(here + shift + depth, depth) + owner_core
                slips = lax.dynamic_update_slice(slips, block[:elements], (owner * elements, 0))
        return slips

    def partial_of(mine, other, side):
        slips = placed(mine[0], other[0])
        partial = jnp.dot(tile_of(side), slips, preferred_element_type=jnp.float32)
        (shift, block) = other[1][-1]
        partial, block = lax.optimization_barrier((partial, block))
        slips = placed(mine[1], [*other[1][:-1], (shift, block)])
        partial += jnp.dot(tile_of(1 - side), slips, preferred_element_type=jnp.float32)
        return partial.astype(jnp.bfloat16).reshape(-1, elements, members)

    def summed(parts):
        return jnp.sum(parts.astype(jnp.float32), axis=0)

    def exchanged(parts):
        return lax.all_to_all(parts, ROW, 0, 0, tiled=True)

    def solved(traction, state, coefs):
        rate_coef, state_coef, pressure, loading, creeping = coefs
        stress = loading + traction
        return solve_rate(stress, pressure, rate_coef, state_coef, state, creeping == 1)

    spare = 8

    def split_rows(largest):
        high = largest.astype(jnp.bfloat16)
        rest = largest - high.astype(jnp.float32)
        low = rest.astype(jnp.bfloat16)
        return jnp.concatenate(
            [high[None], low[None], jnp.zeros((spare - 2, members), jnp.bfloat16)]
        )

    def largest_of(local):
        count = members // 2
        mine = jnp.where(first, local[:count], local[count:])
        other = jnp.where(first, local[count:], local[:count])
        mine = jnp.maximum(mine, swap_cores(other))
        chips = functools.reduce(lambda n, axis: n * lax.axis_size(axis), CHIPS, 1)
        everyone = lax.all_to_all(
            jnp.broadcast_to(mine, (chips, count)), CHIPS, 0, 0, tiled=True
        )
        mine = jnp.max(everyone, axis=0)
        other = swap_cores(mine)
        return jnp.where(first, jnp.concatenate([mine, other]), jnp.concatenate([other, mine]))

    def step(carry):
        index, deficit, state, _, local = carry
        deficit = jnp.where(index == 0, slip_deficit.reshape(elements, members), deficit)
        state = jnp.where(index == 0, state_variable.reshape(elements, members), state)
        block = jnp.concatenate([deficit.astype(jnp.bfloat16), split_rows(local)])
        mine, other, found = gathered(block)
        side, held, _ = lax.optimization_barrier((near, fault, index))
        coefs = coefs_of(held)
        parts = partial_of(mine, other, side)
        rows = split_rows(functools.reduce(jnp.maximum, found))
        rows = jnp.broadcast_to(rows, (parts.shape[0], *rows.shape))
        parts = jnp.concatenate([parts, rows], axis=1)
        held = (coefs, deficit, state, index)
        parts, held = lax.optimization_barrier((parts, held))
        parts, held = lax.optimization_barrier((exchanged(parts), held))
        coefs, deficit, state, index = held
        velocity = solved(summed(parts[:, :elements]), state, coefs)
        local = jnp.max(jnp.abs(velocity), axis=0)
        found = [joined(parts[row, elements:]) for row in range(parts.shape[0])]
        largest = functools.reduce(jnp.maximum, found)
        step_now = jnp.where(index == 0, step_size, STEP_CAP / (1.0 + largest))
        state, deficit = advance(state, deficit, velocity, step_now)
        return index + 1, deficit, state, velocity, local

    blank = jnp.zeros((elements, members), jnp.float32)
    carry = (jnp.int32(0), blank, blank, blank, jnp.zeros((members,), jnp.float32))
    carry = lax.while_loop(lambda carry: carry[0] < STEPS, step, carry)
    _, deficit, state, velocity, local = carry
    step_next = STEP_CAP / (1.0 + largest_of(local))
    shape = slip_deficit.shape
    return (velocity.reshape(shape), deficit.reshape(shape), state.reshape(shape), step_next)


def solution(mesh):
    torus = Mesh(mesh.devices.reshape(4, 2, 2, 8, 2), ("x", "yl", "yh", "z", "c"))
    in_specs = (
        P(BLK, None, ROW, None),
        P(BLK, ROW, None, None),
        P(BLK, ROW, None, None),
        P(),
        P(BLK, ROW, None),
        P(BLK, ROW, None),
        P(),
        P(),
        P(BLK, ROW, None),
        P(BLK, ROW, None),
    )
    out_specs = (P(BLK, ROW, None, None), P(BLK, ROW, None, None), P(BLK, ROW, None, None), P())
    return jax.shard_map(body, mesh=torus, in_specs=in_specs, out_specs=out_specs, check_vma=False)
```

time: 261 us -> 184 us (0.70)
  waiting for transfers between devices: 143 us -> 26.6 us
  starting transfers between devices: 4.93 us -> 68.6 us
  blocking collectives: 73.2 us -> 59.9 us
  between operations: 13.9 us -> 0.78 us
    all_gather x4 -> x0, waiting for transfers between devices: 127 us -> none  [gather_in_order(): parts = lax.all_gather(parts, axes[k])]
    ppermute x0 -> x42, starting transfers between devices: none -> 68.6 us  [the longest x28 42.9 us: shifted(): return lax.ppermute(x, 'z', [(z, (z + by) % depth) for z in range(depth)])]
    pmax x5 -> x0, blocking collectives: 41.5 us -> none  [over_axes(): return functools.reduce(lax.pmax, axes, x)]
    all_to_all x1 -> x3, blocking collectives: 18.8 us -> 59.9 us  [the longest x2 38.8 us: exchanged(): return lax.all_to_all(parts, ROW, 0, 0, tiled=True)]
    ppermute x0 -> x42, waiting for transfers between devices: none -> 26.6 us  [the longest x28 23 us: shifted(): return lax.ppermute(x, 'z', [(z, (z + by) % depth) for z in range(depth)])]
    all_to_all x1 -> x0, waiting for transfers between devices: 15.8 us -> none  [summed_on_arrival(): parts = lax.all_to_all(cut_along(x, dim, count), axis, 0, 0, tiled=True)]
    all_gather x2 -> x0, blocking collectives: 12.9 us -> none  [gather_in_order(): parts = lax.all_gather(parts, axes[k])]
    transpose x2 -> x0, local copies, waits for them, and re-layouts: 5.24 us -> none  [gather_in_order(): parts = parts.transpose(*back, *range(len(axes), parts.ndim))]
  transfers between devices with their start and end apart: 5 -> 42, of which waited for: 5 -> 15; matrix products, arithmetic and copies ran while one was open for 0% -> 1% of each run, Pallas kernels for 0% -> 0%
where the time goes in v1:
time: 184 us
  starting transfers between devices  68.6 us (37%)
  blocking collectives  59.9 us (33%)
  waiting for transfers between devices  26.6 us (14%)
  matrix products  14 us (8%)
  other arithmetic  7.08 us (4%)
  local copies, waits for them, and re-layouts  4.93 us (3%)
    ppermute x28, starting transfers between devices, shifted(): return lax.ppermute(x, 'z', [(z, (z + by) % depth) for z in range(depth)])  42.9 us
    all_to_all x2, blocking collectives, exchanged(): return lax.all_to_all(parts, ROW, 0, 0, tiled=True)  38.8 us
    ppermute x28, waiting for transfers between devices, shifted(): return lax.ppermute(x, 'z', [(z, (z + by) % depth) for z in range(depth)])  23 us
    all_to_all x1, blocking collectives, largest_of(): lax.all_to_all(jnp.broadcast_to(mine, (chips, count)), CHIPS, 0, 0, tiled...  21.1 us
    ppermute x12, starting transfers between devices, swap_cores(): return lax.ppermute(x, 'c', ((0, 1), (1, 0)))  20.1 us
    dot_general x2, matrix products, partial_of(): partial = jnp.dot(tile_of(side), slips, preferred_element_type=jnp.float32)  9.36 us
    ppermute x2, starting transfers between devices, swap_far(): return lax.ppermute(x, 'yh', ((0, 1), (1, 0)))  5.53 us
    dot_general x2, matrix products, partial_of(): jnp.dot(tile_of(1 - side), slips, preferred_element_type=jnp.float32)  4.64 us
  transfers between devices with their start and end apart: 42, of which 15 were waited for; matrix products, arithmetic and copies ran while one was open for 1% of the time, Pallas kernels for 0%

profile of v1, /device:TPU:1, one launch (start us, length us, event | category | flops | bytes accessed | tf_op | source)
XLA Modules:
  0.0 183.5 jit_solution(11218046532362161877)
XLA Ops:
  0.8 0.7 broadcast.102.clone.1
  1.5 0.7 broadcast.102.clone
  2.3 154.3 %while.18 = (s32[]{:T(128)}, f32[128,512]{1,0:T(8,128)S(1)}, f32[128,512]{1,0:T(8,128)}, f32[128,512]{1,0:T(8,128)}, f32[512]{0:T(512)S(1)}, /*index=5*/s32[]{:T...) while((s32[]{:T(128)}, f32[128,512]{1,0:T(8,128)S(1)}, ...), condition=%wide.region_5.6_spmd, body=%wide.region_0.5_spmd.sunk | while | flops 4306238976 | bytes 95482936 | solution.py:216
  2.4 0.1 broadcast.132.clone
  2.5 0.7 copy-done.3
  3.3 6.5 %collective-permute-start.13 = (bf16[136,512]{1,0:T(8,128)(2,1)S(1)}, bf16[136,512]{1,0:T(8,128)(2,1)S(1)}, u32[]{:S(2)}, u32[]{:S(2)}) collective-permute-start(bf16[136,512]{1,0:T(8,128)(2,1)S(1)} %pad_maximum_fusion.10), channel_id=1, source_target_pairs={{0,14},{2,0},{4,2},{6,4},{8,6},{10,8},{12,10},{14,12},{1,15},{3,1}... | collective-permute-start | bytes 417800 | tf_op jit(solution)/shard_map/while/body/ppermute | solution.py:55
  9.8 2.9 %collective-permute-start = (bf16[136,512]{1,0:T(8,128)(2,1)S(1)}, bf16[136,512]{1,0:T(8,128)(2,1)S(1)}, u32[]{:S(2)}, u32[]{:S(2)}) collective-permute-start(bf16[136,512]{1,0:T(8,128)(2,1)S(1)} %pad_maximum_fusion.10), channel_id=1, source_target_pairs={{0,16},{16,0},{1,17},{17,1},{2,18},{18,2},{3,19},{19,3},{4,20},{20... | collective-permute-start | bytes 417800 | tf_op jit(solution)/shard_map/while/body/ppermute | solution.py:50
  12.9 2.7 %collective-permute-start.14 = (bf16[136,512]{1,0:T(8,128)(2,1)S(1)}, bf16[136,512]{1,0:T(8,128)(2,1)S(1)}, u32[]{:S(2)}, u32[]{:S(2)}) collective-permute-start(bf16[136,512]{1,0:T(8,128)(2,1)S(1)} %collective-permute-done.13), channel_id=1, source_target_pairs={{0,14},{2,0},{4,2},{6,4},{8,6},{10,8},{12,10},{14,12},{1,15},{3,1}... | collective-permute-start | bytes 417800 | tf_op jit(solution)/shard_map/while/body/ppermute | solution.py:55
  15.8 2.7 %collective-permute-start.1 = (bf16[136,512]{1,0:T(8,128)(2,1)S(1)}, bf16[136,512]{1,0:T(8,128)(2,1)S(1)}, u32[]{:S(2)}, u32[]{:S(2)}) collective-permute-start(bf16[136,512]{1,0:T(8,128)(2,1)S(1)} %collective-permute-done), channel_id=1, source_target_pairs={{0,14},{2,0},{4,2},{6,4},{8,6},{10,8},{12,10},{14,12},{1,15},{3,1}... | collective-permute-start | bytes 417800 | tf_op jit(solution)/shard_map/while/body/ppermute | solution.py:55
  18.6 0.1 broadcast.132
  18.8 1.9 %collective-permute-start.15 = (bf16[136,512]{1,0:T(8,128)(2,1)S(1)}, bf16[136,512]{1,0:T(8,128)(2,1)S(1)}, u32[]{:S(2)}, u32[]{:S(2)}) collective-permute-start(bf16[136,512]{1,0:T(8,128)(2,1)S(1)} %collective-permute-done.14), channel_id=1, source_target_pairs={{0,14},{2,0},{4,2},{6,4},{8,6},{10,8},{12,10},{14,12},{1,15},{3,1}... | collective-permute-start | bytes 417800 | tf_op jit(solution)/shard_map/while/body/ppermute | solution.py:55
  20.8 2.5 %collective-permute-done.6 = bf16[136,512]{1,0:T(8,128)(2,1)S(1)} collective-permute-done((bf16[136,512]{1,0:T(8,128)(2,1)S(1)}, bf16[136,512]{1,0:T(8,128)(2,1)S(1)}, u32[]{:S(2)}, u32[]{:S(2)}) %collective-permute-start.6) | collective-permute-done | bytes 139296 | tf_op jit(solution)/shard_map/while/body/ppermute | solution.py:55
  23.3 2.7 %collective-permute-start.2 = (bf16[136,512]{1,0:T(8,128)(2,1)S(1)}, bf16[136,512]{1,0:T(8,128)(2,1)S(1)}, u32[]{:S(2)}, u32[]{:S(2)}) collective-permute-start(bf16[136,512]{1,0:T(8,128)(2,1)S(1)} %collective-permute-done.1), channel_id=1, source_target_pairs={{0,14},{2,0},{4,2},{6,4},{8,6},{10,8},{12,10},{14,12},{1,15},{3,1}... | collective-permute-start | bytes 417800 | tf_op jit(solution)/shard_map/while/body/ppermute | solution.py:55
  26.2 0.6 collective-permute-done.12
  26.8 1.6 collective-permute-done.7
  28.5 2.7 %collective-permute-start.3 = (bf16[136,512]{1,0:T(8,128)(2,1)S(1)}, bf16[136,512]{1,0:T(8,128)(2,1)S(1)}, u32[]{:S(2)}, u32[]{:S(2)}) collective-permute-start(bf16[136,512]{1,0:T(8,128)(2,1)S(1)} %collective-permute-done.2), channel_id=1, source_target_pairs={{0,14},{2,0},{4,2},{6,4},{8,6},{10,8},{12,10},{14,12},{1,15},{3,1}... | collective-permute-start | bytes 417800 | tf_op jit(solution)/shard_map/while/body/ppermute | solution.py:55
  31.3 3.9 %collective-permute-done.8 = bf16[136,512]{1,0:T(8,128)(2,1)S(1)} collective-permute-done((bf16[136,512]{1,0:T(8,128)(2,1)S(1)}, bf16[136,512]{1,0:T(8,128)(2,1)S(1)}, u32[]{:S(2)}, u32[]{:S(2)}) %collective-permute-start.8) | collective-permute-done | bytes 139296 | tf_op jit(solution)/shard_map/while/body/ppermute | solution.py:55
  35.3 5.7 %collective-permute-start.9 = (bf16[272,512]{1,0:T(8,128)(2,1)S(1)}, bf16[272,512]{1,0:T(8,128)(2,1)S(1)}, u32[]{:S(2)}, u32[]{:S(2)}) collective-permute-start(bf16[272,512]{1,0:T(8,128)(2,1)S(1)} %pad_maximum_fusion.11), channel_id=1, source_target_pairs={{0,1},{1,0},{2,3},{3,2},{4,5},{5,4},{6,7},{7,6},{8,9},{9,8},{10,11... | collective-permute-start | bytes 835592 | tf_op jit(solution)/shard_map/while/body/ppermute | solution.py:46
  41.2 0.6 collective-permute-start.16
  42.0 3.1 %collective-permute-start.4 = (bf16[136,512]{1,0:T(8,128)(2,1)S(1)}, bf16[136,512]{1,0:T(8,128)(2,1)S(1)}, u32[]{:S(2)}, u32[]{:S(2)}) collective-permute-start(bf16[136,512]{1,0:T(8,128)(2,1)S(1)} %collective-permute-done.3), channel_id=1, source_target_pairs={{0,14},{2,0},{4,2},{6,4},{8,6},{10,8},{12,10},{14,12},{1,15},{3,1}... | collective-permute-start | bytes 417800 | tf_op jit(solution)/shard_map/while/body/ppermute | solution.py:55
  45.2 2.5 %collective-permute-done.4 = bf16[136,512]{1,0:T(8,128)(2,1)S(1)} collective-permute-done((bf16[136,512]{1,0:T(8,128)(2,1)S(1)}, bf16[136,512]{1,0:T(8,128)(2,1)S(1)}, u32[]{:S(2)}, u32[]{:S(2)}) %collective-permute-start.4) | collective-permute-done | bytes 139296 | tf_op jit(solution)/shard_map/while/body/ppermute | solution.py:55
  47.7 1.3 collective-permute-start.5
  49.1 1.0 collective-permute-done.5
  50.6 4.7 %fusion.125 = f32[1024,512]{1,0:T(8,128)S(1)} fusion(bf16[2048,512]{1,0:T(8,128)(2,1)S(1)} %slice_dynamic-update-slice_fusion.89, bf16[1024,4096]{1,0:T(8,128)(2,1)} %get-tuple-element.986, s32[]{:T(128)S(6)} %select_n.283), kind=kOutput, calls=%fused_computation.2.clone.1 | convolution fusion | flops 2147483648 | bytes 8388612 | tf_op jit(solution)/shard_map/while/body/dot_general | solution.py:149
  55.4 2.3 %fusion.126 = f32[1024,512]{1,0:T(8,128)S(1)} fusion(bf16[2048,512]{1,0:T(8,128)(2,1)S(1)} %slice_dynamic-update-slice_fusion.90, bf16[1024,4096]{1,0:T(8,128)(2,1)S(1)} %bitcast.191, s32[]{:T(128)S(6)} %select_n.284), kind=kOutput, calls=%fused_computation.clone.1 | convolution fusion | flops 2147483648 | bytes 8388612 | tf_op jit(solution)/shard_map/while/body/dot_general | solution.py:153
  57.7 0.6 add_convert_fusion.2
  58.4 20.4 %all_to_all.16 = bf16[8,136,512]{2,1,0:T(8,128)(2,1)S(1)} all-to-all(bf16[8,136,512]{2,1,0:T(8,128)(2,1)S(1)} %pad_maximum_fusion.14), channel_id=1, replica_groups=mesh['x'=4,'yl'=2,'yh'=2,'z'=8,'c'=2] {'x','yl'}, dimensions={0} | all-to-all | bytes 2228224 | tf_op jit(solution)/shard_map/while/body/all_to_all | solution.py:160
  78.9 0.2 convert_reduce_fusion.2
  79.1 1.0 abs_reduce_fusion.2
  80.1 0.8 exponential_multiply_fusion.2
  81.1 0.1 broadcast.132.clone
  81.2 0.7 copy-done.3
  82.0 3.5 %collective-permute-start.13 = (bf16[136,512]{1,0:T(8,128)(2,1)S(1)}, bf16[136,512]{1,0:T(8,128)(2,1)S(1)}, u32[]{:S(2)}, u32[]{:S(2)}) collective-permute-start(bf16[136,512]{1,0:T(8,128)(2,1)S(1)} %pad_maximum_fusion.10), channel_id=1, source_target_pairs={{0,14},{2,0},{4,2},{6,4},{8,6},{10,8},{12,10},{14,12},{1,15},{3,1}... | collective-permute-start | bytes 417800 | tf_op jit(solution)/shard_map/while/body/ppermute | solution.py:55
  85.5 2.6 %collective-permute-start = (bf16[136,512]{1,0:T(8,128)(2,1)S(1)}, bf16[136,512]{1,0:T(8,128)(2,1)S(1)}, u32[]{:S(2)}, u32[]{:S(2)}) collective-permute-start(bf16[136,512]{1,0:T(8,128)(2,1)S(1)} %pad_maximum_fusion.10), channel_id=1, source_target_pairs={{0,16},{16,0},{1,17},{17,1},{2,18},{18,2},{3,19},{19,3},{4,20},{20... | collective-permute-start | bytes 417800 | tf_op jit(solution)/shard_map/while/body/ppermute | solution.py:50
  88.3 2.7 %collective-permute-start.14 = (bf16[136,512]{1,0:T(8,128)(2,1)S(1)}, bf16[136,512]{1,0:T(8,128)(2,1)S(1)}, u32[]{:S(2)}, u32[]{:S(2)}) collective-permute-start(bf16[136,512]{1,0:T(8,128)(2,1)S(1)} %collective-permute-done.13), channel_id=1, source_target_pairs={{0,14},{2,0},{4,2},{6,4},{8,6},{10,8},{12,10},{14,12},{1,15},{3,1}... | collective-permute-start | bytes 417800 | tf_op jit(solution)/shard_map/while/body/ppermute | solution.py:55
  91.3 2.7 %collective-permute-start.1 = (bf16[136,512]{1,0:T(8,128)(2,1)S(1)}, bf16[136,512]{1,0:T(8,128)(2,1)S(1)}, u32[]{:S(2)}, u32[]{:S(2)}) collective-permute-start(bf16[136,512]{1,0:T(8,128)(2,1)S(1)} %collective-permute-done), channel_id=1, source_target_pairs={{0,14},{2,0},{4,2},{6,4},{8,6},{10,8},{12,10},{14,12},{1,15},{3,1}... | collective-permute-start | bytes 417800 | tf_op jit(solution)/shard_map/while/body/ppermute | solution.py:55
  94.0 0.1 broadcast.132
  94.2 2.2 %collective-permute-start.15 = (bf16[136,512]{1,0:T(8,128)(2,1)S(1)}, bf16[136,512]{1,0:T(8,128)(2,1)S(1)}, u32[]{:S(2)}, u32[]{:S(2)}) collective-permute-start(bf16[136,512]{1,0:T(8,128)(2,1)S(1)} %collective-permute-done.14), channel_id=1, source_target_pairs={{0,14},{2,0},{4,2},{6,4},{8,6},{10,8},{12,10},{14,12},{1,15},{3,1}... | collective-permute-start | bytes 417800 | tf_op jit(solution)/shard_map/while/body/ppermute | solution.py:55
  96.6 1.2 collective-permute-done.6
  97.8 2.9 %collective-permute-start.2 = (bf16[136,512]{1,0:T(8,128)(2,1)S(1)}, bf16[136,512]{1,0:T(8,128)(2,1)S(1)}, u32[]{:S(2)}, u32[]{:S(2)}) collective-permute-start(bf16[136,512]{1,0:T(8,128)(2,1)S(1)} %collective-permute-done.1), channel_id=1, source_target_pairs={{0,14},{2,0},{4,2},{6,4},{8,6},{10,8},{12,10},{14,12},{1,15},{3,1}... | collective-permute-start | bytes 417800 | tf_op jit(solution)/shard_map/while/body/ppermute | solution.py:55
  100.8 1.8 %collective-permute-done.12 = bf16[136,512]{1,0:T(8,128)(2,1)S(1)} collective-permute-done((bf16[136,512]{1,0:T(8,128)(2,1)S(1)}, bf16[136,512]{1,0:T(8,128)(2,1)S(1)}, u32[]{:S(2)}, u32[]{:S(2)}) %collective-permute-start.12) | collective-permute-done | bytes 139296 | tf_op jit(solution)/shard_map/while/body/ppermute | solution.py:55
  102.7 1.5 collective-permute-done.7
  104.2 2.7 %collective-permute-start.3 = (bf16[136,512]{1,0:T(8,128)(2,1)S(1)}, bf16[136,512]{1,0:T(8,128)(2,1)S(1)}, u32[]{:S(2)}, u32[]{:S(2)}) collective-permute-start(bf16[136,512]{1,0:T(8,128)(2,1)S(1)} %collective-permute-done.2), channel_id=1, source_target_pairs={{0,14},{2,0},{4,2},{6,4},{8,6},{10,8},{12,10},{14,12},{1,15},{3,1}... | collective-permute-start | bytes 417800 | tf_op jit(solution)/shard_map/while/body/ppermute | solution.py:55
  107.0 4.9 %collective-permute-done.8 = bf16[136,512]{1,0:T(8,128)(2,1)S(1)} collective-permute-done((bf16[136,512]{1,0:T(8,128)(2,1)S(1)}, bf16[136,512]{1,0:T(8,128)(2,1)S(1)}, u32[]{:S(2)}, u32[]{:S(2)}) %collective-permute-start.8) | collective-permute-done | bytes 139296 | tf_op jit(solution)/shard_map/while/body/ppermute | solution.py:55
  111.9 6.7 %collective-permute-start.9 = (bf16[272,512]{1,0:T(8,128)(2,1)S(1)}, bf16[272,512]{1,0:T(8,128)(2,1)S(1)}, u32[]{:S(2)}, u32[]{:S(2)}) collective-permute-start(bf16[272,512]{1,0:T(8,128)(2,1)S(1)} %pad_maximum_fusion.11), channel_id=1, source_target_pairs={{0,1},{1,0},{2,3},{3,2},{4,5},{5,4},{6,7},{7,6},{8,9},{9,8},{10,11... | collective-permute-start | bytes 835592 | tf_op jit(solution)/shard_map/while/body/ppermute | solution.py:46
  118.9 0.6 collective-permute-start.16
  119.6 3.1 %collective-permute-start.4 = (bf16[136,512]{1,0:T(8,128)(2,1)S(1)}, bf16[136,512]{1,0:T(8,128)(2,1)S(1)}, u32[]{:S(2)}, u32[]{:S(2)}) collective-permute-start(bf16[136,512]{1,0:T(8,128)(2,1)S(1)} %collective-permute-done.3), channel_id=1, source_target_pairs={{0,14},{2,0},{4,2},{6,4},{8,6},{10,8},{12,10},{14,12},{1,15},{3,1}... | collective-permute-start | bytes 417800 | tf_op jit(solution)/shard_map/while/body/ppermute | solution.py:55
  122.9 2.5 %collective-permute-done.4 = bf16[136,512]{1,0:T(8,128)(2,1)S(1)} collective-permute-done((bf16[136,512]{1,0:T(8,128)(2,1)S(1)}, bf16[136,512]{1,0:T(8,128)(2,1)S(1)}, u32[]{:S(2)}, u32[]{:S(2)}) %collective-permute-start.4) | collective-permute-done | bytes 139296 | tf_op jit(solution)/shard_map/while/body/ppermute | solution.py:55
  125.3 1.3 collective-permute-start.5
  126.7 1.0 collective-permute-done.5
  128.2 4.7 %fusion.125 = f32[1024,512]{1,0:T(8,128)S(1)} fusion(bf16[2048,512]{1,0:T(8,128)(2,1)S(1)} %slice_dynamic-update-slice_fusion.89, bf16[1024,4096]{1,0:T(8,128)(2,1)} %get-tuple-element.986, s32[]{:T(128)S(6)} %select_n.283), kind=kOutput, calls=%fused_computation.2.clone.1 | convolution fusion | flops 2147483648 | bytes 8388612 | tf_op jit(solution)/shard_map/while/body/dot_general | solution.py:149
  133.0 2.3 %fusion.126 = f32[1024,512]{1,0:T(8,128)S(1)} fusion(bf16[2048,512]{1,0:T(8,128)(2,1)S(1)} %slice_dynamic-update-slice_fusion.90, bf16[1024,4096]{1,0:T(8,128)(2,1)S(1)} %bitcast.191, s32[]{:T(128)S(6)} %select_n.284), kind=kOutput, calls=%fused_computation.clone.1 | convolution fusion | flops 2147483648 | bytes 8388612 | tf_op jit(solution)/shard_map/while/body/dot_general | solution.py:153
  135.3 0.6 add_convert_fusion.2
  136.0 18.4 %all_to_all.16 = bf16[8,136,512]{2,1,0:T(8,128)(2,1)S(1)} all-to-all(bf16[8,136,512]{2,1,0:T(8,128)(2,1)S(1)} %pad_maximum_fusion.14), channel_id=1, replica_groups=mesh['x'=4,'yl'=2,'yh'=2,'z'=8,'c'=2] {'x','yl'}, dimensions={0} | all-to-all | bytes 2228224 | tf_op jit(solution)/shard_map/while/body/all_to_all | solution.py:160
  154.4 0.2 convert_reduce_fusion.2
  154.7 1.0 abs_reduce_fusion.2
  155.7 0.8 exponential_multiply_fusion.2
  156.5 1.6 collective-permute-start.20
  158.2 0.8 collective-permute-done.20
  159.1 21.1 %all_to_all.15 = f32[128,1,256]{2,1,0:T(1,128)S(1)} all-to-all(f32[128,1,256]{2,1,0:T(1,128)S(1)} %broadcast_in_dim.77), channel_id=1, replica_groups=mesh['x'=4,'yl'=2,'yh'=2,'z'=8,'c'=2] {'x','yl','yh','z'}, dimensions={0} | all-to-all | bytes 262144 | tf_op jit(solution)/shard_map/all_to_all | solution.py:183
  180.2 0.2 reduce_max.21
  180.3 1.8 collective-permute-start.21
  182.1 0.8 collective-permute-done.21
  182.9 0.6 fusion.68
  (265 shorter events, 3.8 us)
Async XLA Ops:
  2.3 10.4 %copy-start.2 = (f32[128,512]{1,0:T(8,128)S(1)}, f32[128,512]{1,0:T(8,128)}, u32[]{:S(2)}) copy-start(f32[128,512]{1,0:T(8,128)} %get-tuple-element.939) | copy-start | bytes 786436 | tf_op jit(solution)/shard_map/while
  2.3 10.4 %copy-start.4 = (f32[1,1,128,512]{3,2,1,0:T(8,128)S(1)}, f32[1,1,128,512]{3,2,1,0:T(8,128)}, u32[]{:S(2)}) copy-start(f32[1,1,128,512]{3,2,1,0:T(8,128)} %get-tuple-element.1004) | copy-start | bytes 786436 | tf_op jit(solution)/shard_map/while
  2.3 10.4 %copy-start.6 = (f32[16]{0:T(128)S(1)}, f32[16]{0:T(128)}, u32[]{:S(2)}) copy-start(f32[16]{0:T(128)} %get-tuple-element.869) | copy-start | bytes 196 | tf_op jit(solution)/shard_map/while
  2.4 10.4 %copy-start.7 = (f32[16]{0:T(128)S(1)}, f32[16]{0:T(128)}, u32[]{:S(2)}) copy-start(f32[16]{0:T(128)} %get-tuple-element.867) | copy-start | bytes 196 | tf_op jit(solution)/shard_map/while
  2.4 10.4 %copy-start.8 = (s32[1,1,128]{2,1,0:T(1,128)S(1)}, s32[1,1,128]{2,1,0:T(1,128)}, u32[]{:S(2)}) copy-start(s32[1,1,128]{2,1,0:T(1,128)} %get-tuple-element.868) | copy-start | bytes 1540 | tf_op jit(solution)/shard_map/while
  3.3 9.6 %collective-permute-start.13 = (bf16[136,512]{1,0:T(8,128)(2,1)S(1)}, bf16[136,512]{1,0:T(8,128)(2,1)S(1)}, u32[]{:S(2)}, u32[]{:S(2)}) collective-permute-start(bf16[136,512]{1,0:T(8,128)(2,1)S(1)} %pad_maximum_fusion.10), channel_id=1, source_target_pairs={{0,14},{2,0},{4,2},{6,4},{8,6},{10,8},{12,10},{14,12},{1,15},{3,1}... | collective-permute-start | bytes 417800 | tf_op jit(solution)/shard_map/while/body/ppermute | solution.py:55
  9.8 5.8 %collective-permute-start.10 = (bf16[136,512]{1,0:T(8,128)(2,1)S(1)}, bf16[136,512]{1,0:T(8,128)(2,1)S(1)}, u32[]{:S(2)}, u32[]{:S(2)}) collective-permute-start(bf16[136,512]{1,0:T(8,128)(2,1)S(1)} %pad_maximum_fusion.10), channel_id=1, source_target_pairs={{0,2},{2,4},{4,6},{6,8},{8,10},{10,12},{12,14},{14,0},{1,3},{3,5},... | collective-permute-start | bytes 417800 | tf_op jit(solution)/shard_map/while/body/ppermute | solution.py:55
  9.8 6.0 %collective-permute-start = (bf16[136,512]{1,0:T(8,128)(2,1)S(1)}, bf16[136,512]{1,0:T(8,128)(2,1)S(1)}, u32[]{:S(2)}, u32[]{:S(2)}) collective-permute-start(bf16[136,512]{1,0:T(8,128)(2,1)S(1)} %pad_maximum_fusion.10), channel_id=1, source_target_pairs={{0,16},{16,0},{1,17},{17,1},{2,18},{18,2},{3,19},{19,3},{4,20},{20... | collective-permute-start | bytes 417800 | tf_op jit(solution)/shard_map/while/body/ppermute | solution.py:50
  12.9 5.9 %collective-permute-start.14 = (bf16[136,512]{1,0:T(8,128)(2,1)S(1)}, bf16[136,512]{1,0:T(8,128)(2,1)S(1)}, u32[]{:S(2)}, u32[]{:S(2)}) collective-permute-start(bf16[136,512]{1,0:T(8,128)(2,1)S(1)} %collective-permute-done.13), channel_id=1, source_target_pairs={{0,14},{2,0},{4,2},{6,4},{8,6},{10,8},{12,10},{14,12},{1,15},{3,1}... | collective-permute-start | bytes 417800 | tf_op jit(solution)/shard_map/while/body/ppermute | solution.py:55
  15.6 5.2 %collective-permute-start.11 = (bf16[136,512]{1,0:T(8,128)(2,1)S(1)}, bf16[136,512]{1,0:T(8,128)(2,1)S(1)}, u32[]{:S(2)}, u32[]{:S(2)}) collective-permute-start(bf16[136,512]{1,0:T(8,128)(2,1)S(1)} %collective-permute-done.10), channel_id=1, source_target_pairs={{0,2},{2,4},{4,6},{6,8},{8,10},{10,12},{12,14},{14,0},{1,3},{3,5},... | collective-permute-start | bytes 417800 | tf_op jit(solution)/shard_map/while/body/ppermute | solution.py:55
  15.7 7.6 %collective-permute-start.6 = (bf16[136,512]{1,0:T(8,128)(2,1)S(1)}, bf16[136,512]{1,0:T(8,128)(2,1)S(1)}, u32[]{:S(2)}, u32[]{:S(2)}) collective-permute-start(bf16[136,512]{1,0:T(8,128)(2,1)S(1)} %collective-permute-done), channel_id=1, source_target_pairs={{0,2},{2,4},{4,6},{6,8},{8,10},{10,12},{12,14},{14,0},{1,3},{3,5},... | collective-permute-start | bytes 417800 | tf_op jit(solution)/shard_map/while/body/ppermute | solution.py:55
  15.8 7.5 %collective-permute-start.1 = (bf16[136,512]{1,0:T(8,128)(2,1)S(1)}, bf16[136,512]{1,0:T(8,128)(2,1)S(1)}, u32[]{:S(2)}, u32[]{:S(2)}) collective-permute-start(bf16[136,512]{1,0:T(8,128)(2,1)S(1)} %collective-permute-done), channel_id=1, source_target_pairs={{0,14},{2,0},{4,2},{6,4},{8,6},{10,8},{12,10},{14,12},{1,15},{3,1}... | collective-permute-start | bytes 417800 | tf_op jit(solution)/shard_map/while/body/ppermute | solution.py:55
  18.8 9.7 %collective-permute-start.15 = (bf16[136,512]{1,0:T(8,128)(2,1)S(1)}, bf16[136,512]{1,0:T(8,128)(2,1)S(1)}, u32[]{:S(2)}, u32[]{:S(2)}) collective-permute-start(bf16[136,512]{1,0:T(8,128)(2,1)S(1)} %collective-permute-done.14), channel_id=1, source_target_pairs={{0,14},{2,0},{4,2},{6,4},{8,6},{10,8},{12,10},{14,12},{1,15},{3,1}... | collective-permute-start | bytes 417800 | tf_op jit(solution)/shard_map/while/body/ppermute | solution.py:55
  20.8 6.0 %collective-permute-start.12 = (bf16[136,512]{1,0:T(8,128)(2,1)S(1)}, bf16[136,512]{1,0:T(8,128)(2,1)S(1)}, u32[]{:S(2)}, u32[]{:S(2)}) collective-permute-start(bf16[136,512]{1,0:T(8,128)(2,1)S(1)} %collective-permute-done.11), channel_id=1, source_target_pairs={{0,2},{2,4},{4,6},{6,8},{8,10},{10,12},{12,14},{14,0},{1,3},{3,5},... | collective-permute-start | bytes 417800 | tf_op jit(solution)/shard_map/while/body/ppermute | solution.py:55
  23.3 5.1 %collective-permute-start.7 = (bf16[136,512]{1,0:T(8,128)(2,1)S(1)}, bf16[136,512]{1,0:T(8,128)(2,1)S(1)}, u32[]{:S(2)}, u32[]{:S(2)}) collective-permute-start(bf16[136,512]{1,0:T(8,128)(2,1)S(1)} %collective-permute-done.6), channel_id=1, source_target_pairs={{0,2},{2,4},{4,6},{6,8},{8,10},{10,12},{12,14},{14,0},{1,3},{3,5},... | collective-permute-start | bytes 417800 | tf_op jit(solution)/shard_map/while/body/ppermute | solution.py:55
  23.3 5.1 %collective-permute-start.2 = (bf16[136,512]{1,0:T(8,128)(2,1)S(1)}, bf16[136,512]{1,0:T(8,128)(2,1)S(1)}, u32[]{:S(2)}, u32[]{:S(2)}) collective-permute-start(bf16[136,512]{1,0:T(8,128)(2,1)S(1)} %collective-permute-done.1), channel_id=1, source_target_pairs={{0,14},{2,0},{4,2},{6,4},{8,6},{10,8},{12,10},{14,12},{1,15},{3,1}... | collective-permute-start | bytes 417800 | tf_op jit(solution)/shard_map/while/body/ppermute | solution.py:55
  26.8 14.2 %collective-permute-start.17 = (bf16[136,512]{1,0:T(8,128)(2,1)S(1)}, bf16[136,512]{1,0:T(8,128)(2,1)S(1)}, u32[]{:S(2)}, u32[]{:S(2)}) collective-permute-start(bf16[136,512]{1,0:T(8,128)(2,1)S(1)} %collective-permute-done.12), channel_id=1, source_target_pairs={{0,2},{2,4},{4,6},{6,8},{8,10},{10,12},{12,14},{14,0},{1,3},{3,5},... | collective-permute-start | bytes 417800 | tf_op jit(solution)/shard_map/while/body/ppermute | solution.py:55
  28.4 6.8 %collective-permute-start.8 = (bf16[136,512]{1,0:T(8,128)(2,1)S(1)}, bf16[136,512]{1,0:T(8,128)(2,1)S(1)}, u32[]{:S(2)}, u32[]{:S(2)}) collective-permute-start(bf16[136,512]{1,0:T(8,128)(2,1)S(1)} %collective-permute-done.7), channel_id=1, source_target_pairs={{0,2},{2,4},{4,6},{6,8},{8,10},{10,12},{12,14},{14,0},{1,3},{3,5},... | collective-permute-start | bytes 417800 | tf_op jit(solution)/shard_map/while/body/ppermute | solution.py:55
  28.5 6.7 %collective-permute-start.3 = (bf16[136,512]{1,0:T(8,128)(2,1)S(1)}, bf16[136,512]{1,0:T(8,128)(2,1)S(1)}, u32[]{:S(2)}, u32[]{:S(2)}) collective-permute-start(bf16[136,512]{1,0:T(8,128)(2,1)S(1)} %collective-permute-done.2), channel_id=1, source_target_pairs={{0,14},{2,0},{4,2},{6,4},{8,6},{10,8},{12,10},{14,12},{1,15},{3,1}... | collective-permute-start | bytes 417800 | tf_op jit(solution)/shard_map/while/body/ppermute | solution.py:55
  35.3 14.8 %collective-permute-start.9 = (bf16[272,512]{1,0:T(8,128)(2,1)S(1)}, bf16[272,512]{1,0:T(8,128)(2,1)S(1)}, u32[]{:S(2)}, u32[]{:S(2)}) collective-permute-start(bf16[272,512]{1,0:T(8,128)(2,1)S(1)} %pad_maximum_fusion.11), channel_id=1, source_target_pairs={{0,1},{1,0},{2,3},{3,2},{4,5},{5,4},{6,7},{7,6},{8,9},{9,8},{10,11... | collective-permute-start | bytes 835592 | tf_op jit(solution)/shard_map/while/body/ppermute | solution.py:46
  41.0 9.0 %collective-permute-start.18 = (bf16[408,512]{1,0:T(8,128)(2,1)S(1)}, bf16[408,512]{1,0:T(8,128)(2,1)S(1)}, u32[]{:S(2)}, u32[]{:S(2)}) collective-permute-start(bf16[408,512]{1,0:T(8,128)(2,1)S(1)} %pad_maximum_fusion.12), channel_id=1, source_target_pairs={{0,1},{1,0},{2,3},{3,2},{4,5},{5,4},{6,7},{7,6},{8,9},{9,8},{10,11... | collective-permute-start | bytes 1253384 | tf_op jit(solution)/shard_map/while/body/ppermute | solution.py:46
  41.2 8.9 %collective-permute-start.16 = (bf16[680,512]{1,0:T(8,128)(2,1)S(1)}, bf16[680,512]{1,0:T(8,128)(2,1)S(1)}, u32[]{:S(2)}, u32[]{:S(2)}) collective-permute-start(bf16[680,512]{1,0:T(8,128)(2,1)S(1)} %constant_dynamic-update-slice_fusion.27), channel_id=1, source_target_pairs={{0,1},{1,0},{2,3},{3,2},{4,5},{5,4},{6,7},{7,6},{8,9},{9,8},{10,11... | collective-permute-start | bytes 2088968 | tf_op jit(solution)/shard_map/while/body/ppermute | solution.py:46
  41.9 8.2 %collective-permute-start.19 = (bf16[680,512]{1,0:T(8,128)(2,1)S(1)}, bf16[680,512]{1,0:T(8,128)(2,1)S(1)}, u32[]{:S(2)}, u32[]{:S(2)}) collective-permute-start(bf16[680,512]{1,0:T(8,128)(2,1)S(1)} %constant_dynamic-update-slice_fusion.32), channel_id=1, source_target_pairs={{0,1},{1,0},{2,3},{3,2},{4,5},{5,4},{6,7},{7,6},{8,9},{9,8},{10,11... | collective-permute-start | bytes 2088968 | tf_op jit(solution)/shard_map/while/body/ppermute | solution.py:46
  42.0 5.7 %collective-permute-start.4 = (bf16[136,512]{1,0:T(8,128)(2,1)S(1)}, bf16[136,512]{1,0:T(8,128)(2,1)S(1)}, u32[]{:S(2)}, u32[]{:S(2)}) collective-permute-start(bf16[136,512]{1,0:T(8,128)(2,1)S(1)} %collective-permute-done.3), channel_id=1, source_target_pairs={{0,14},{2,0},{4,2},{6,4},{8,6},{10,8},{12,10},{14,12},{1,15},{3,1}... | collective-permute-start | bytes 417800 | tf_op jit(solution)/shard_map/while/body/ppermute | solution.py:55
  47.7 2.3 %collective-permute-start.5 = (bf16[136,512]{1,0:T(8,128)(2,1)S(1)}, bf16[136,512]{1,0:T(8,128)(2,1)S(1)}, u32[]{:S(2)}, u32[]{:S(2)}) collective-permute-start(bf16[136,512]{1,0:T(8,128)(2,1)S(1)} %collective-permute-done.4), channel_id=1, source_target_pairs={{0,1},{1,0},{2,3},{3,2},{4,5},{5,4},{6,7},{7,6},{8,9},{9,8},{10,11... | collective-permute-start | bytes 417800 | tf_op jit(solution)/shard_map/while/body/ppermute | solution.py:46
  50.5 4.8 %slice-start = ((s8[8388608]{0:T(1024)(128)(4,1)}), s8[4194304]{0:T(1024)(128)(4,1)S(1)}, s32[]{:S(2)}) async-start(s8[8388608]{0:T(1024)(128)(4,1)} %bitcast.190), calls=%async_computation.2 | async-start | bytes 8388608 | tf_op jit(solution)/shard_map/while
  50.6 4.8 %slice-start.1 = ((s8[8388608]{0:T(1024)(128)(4,1)}), s8[4194304]{0:T(1024)(128)(4,1)S(1)}, s32[]{:S(2)}) async-start(s8[8388608]{0:T(1024)(128)(4,1)} %bitcast.190), calls=%async_computation.3 | async-start | bytes 8388608 | tf_op jit(solution)/shard_map/while
  58.3 20.7 %copy-start.10 = (s32[1,1,128]{2,1,0:T(1,128)S(1)}, s32[1,1,128]{2,1,0:T(1,128)}, u32[]{:S(2)}) copy-start(s32[1,1,128]{2,1,0:T(1,128)} %get-tuple-element.874) | copy-start | bytes 1540 | tf_op jit(solution)/shard_map/while
  58.4 20.7 %copy-start.9 = (f32[1,1,128]{2,1,0:T(1,128)S(1)}, f32[1,1,128]{2,1,0:T(1,128)}, u32[]{:S(2)}) copy-start(f32[1,1,128]{2,1,0:T(1,128)} %get-tuple-element.872) | copy-start | bytes 1540 | tf_op jit(solution)/shard_map/while
  58.4 20.7 %copy-start.5 = (f32[512]{0:T(512)S(1)}, f32[512]{0:T(512)}, u32[]{:S(2)}) copy-start(f32[512]{0:T(512)} %get-tuple-element.1005) | copy-start | bytes 6148 | tf_op jit(solution)/shard_map/while
  58.4 20.7 %copy-start.11 = (f32[1,1,128]{2,1,0:T(1,128)S(1)}, f32[1,1,128]{2,1,0:T(1,128)}, u32[]{:S(2)}) copy-start(f32[1,1,128]{2,1,0:T(1,128)} %get-tuple-element.873) | copy-start | bytes 1540 | tf_op jit(solution)/shard_map/while
  81.0 7.1 %copy-start.2 = (f32[128,512]{1,0:T(8,128)S(1)}, f32[128,512]{1,0:T(8,128)}, u32[]{:S(2)}) copy-start(f32[128,512]{1,0:T(8,128)} %get-tuple-element.939) | copy-start | bytes 786436 | tf_op jit(solution)/shard_map/while
  81.0 7.1 %copy-start.4 = (f32[1,1,128,512]{3,2,1,0:T(8,128)S(1)}, f32[1,1,128,512]{3,2,1,0:T(8,128)}, u32[]{:S(2)}) copy-start(f32[1,1,128,512]{3,2,1,0:T(8,128)} %get-tuple-element.1004) | copy-start | bytes 786436 | tf_op jit(solution)/shard_map/while
  81.0 7.1 %copy-start.6 = (f32[16]{0:T(128)S(1)}, f32[16]{0:T(128)}, u32[]{:S(2)}) copy-start(f32[16]{0:T(128)} %get-tuple-element.869) | copy-start | bytes 196 | tf_op jit(solution)/shard_map/while
  81.0 7.1 %copy-start.7 = (f32[16]{0:T(128)S(1)}, f32[16]{0:T(128)}, u32[]{:S(2)}) copy-start(f32[16]{0:T(128)} %get-tuple-element.867) | copy-start | bytes 196 | tf_op jit(solution)/shard_map/while
  81.1 7.1 %copy-start.8 = (s32[1,1,128]{2,1,0:T(1,128)S(1)}, s32[1,1,128]{2,1,0:T(1,128)}, u32[]{:S(2)}) copy-start(s32[1,1,128]{2,1,0:T(1,128)} %get-tuple-element.868) | copy-start | bytes 1540 | tf_op jit(solution)/shard_map/while
  82.0 6.3 %collective-permute-start.13 = (bf16[136,512]{1,0:T(8,128)(2,1)S(1)}, bf16[136,512]{1,0:T(8,128)(2,1)S(1)}, u32[]{:S(2)}, u32[]{:S(2)}) collective-permute-start(bf16[136,512]{1,0:T(8,128)(2,1)S(1)} %pad_maximum_fusion.10), channel_id=1, source_target_pairs={{0,14},{2,0},{4,2},{6,4},{8,6},{10,8},{12,10},{14,12},{1,15},{3,1}... | collective-permute-start | bytes 417800 | tf_op jit(solution)/shard_map/while/body/ppermute | solution.py:55
  85.5 5.6 %collective-permute-start.10 = (bf16[136,512]{1,0:T(8,128)(2,1)S(1)}, bf16[136,512]{1,0:T(8,128)(2,1)S(1)}, u32[]{:S(2)}, u32[]{:S(2)}) collective-permute-start(bf16[136,512]{1,0:T(8,128)(2,1)S(1)} %pad_maximum_fusion.10), channel_id=1, source_target_pairs={{0,2},{2,4},{4,6},{6,8},{8,10},{10,12},{12,14},{14,0},{1,3},{3,5},... | collective-permute-start | bytes 417800 | tf_op jit(solution)/shard_map/while/body/ppermute | solution.py:55
  85.5 5.7 %collective-permute-start = (bf16[136,512]{1,0:T(8,128)(2,1)S(1)}, bf16[136,512]{1,0:T(8,128)(2,1)S(1)}, u32[]{:S(2)}, u32[]{:S(2)}) collective-permute-start(bf16[136,512]{1,0:T(8,128)(2,1)S(1)} %pad_maximum_fusion.10), channel_id=1, source_target_pairs={{0,16},{16,0},{1,17},{17,1},{2,18},{18,2},{3,19},{19,3},{4,20},{20... | collective-permute-start | bytes 417800 | tf_op jit(solution)/shard_map/while/body/ppermute | solution.py:50
  88.3 5.9 %collective-permute-start.14 = (bf16[136,512]{1,0:T(8,128)(2,1)S(1)}, bf16[136,512]{1,0:T(8,128)(2,1)S(1)}, u32[]{:S(2)}, u32[]{:S(2)}) collective-permute-start(bf16[136,512]{1,0:T(8,128)(2,1)S(1)} %collective-permute-done.13), channel_id=1, source_target_pairs={{0,14},{2,0},{4,2},{6,4},{8,6},{10,8},{12,10},{14,12},{1,15},{3,1}... | collective-permute-start | bytes 417800 | tf_op jit(solution)/shard_map/while/body/ppermute | solution.py:55
  91.0 5.4 %collective-permute-start.11 = (bf16[136,512]{1,0:T(8,128)(2,1)S(1)}, bf16[136,512]{1,0:T(8,128)(2,1)S(1)}, u32[]{:S(2)}, u32[]{:S(2)}) collective-permute-start(bf16[136,512]{1,0:T(8,128)(2,1)S(1)} %collective-permute-done.10), channel_id=1, source_target_pairs={{0,2},{2,4},{4,6},{6,8},{8,10},{10,12},{12,14},{14,0},{1,3},{3,5},... | collective-permute-start | bytes 417800 | tf_op jit(solution)/shard_map/while/body/ppermute | solution.py:55
  91.2 6.6 %collective-permute-start.6 = (bf16[136,512]{1,0:T(8,128)(2,1)S(1)}, bf16[136,512]{1,0:T(8,128)(2,1)S(1)}, u32[]{:S(2)}, u32[]{:S(2)}) collective-permute-start(bf16[136,512]{1,0:T(8,128)(2,1)S(1)} %collective-permute-done), channel_id=1, source_target_pairs={{0,2},{2,4},{4,6},{6,8},{8,10},{10,12},{12,14},{14,0},{1,3},{3,5},... | collective-permute-start | bytes 417800 | tf_op jit(solution)/shard_map/while/body/ppermute | solution.py:55
  91.3 6.5 %collective-permute-start.1 = (bf16[136,512]{1,0:T(8,128)(2,1)S(1)}, bf16[136,512]{1,0:T(8,128)(2,1)S(1)}, u32[]{:S(2)}, u32[]{:S(2)}) collective-permute-start(bf16[136,512]{1,0:T(8,128)(2,1)S(1)} %collective-permute-done), channel_id=1, source_target_pairs={{0,14},{2,0},{4,2},{6,4},{8,6},{10,8},{12,10},{14,12},{1,15},{3,1}... | collective-permute-start | bytes 417800 | tf_op jit(solution)/shard_map/while/body/ppermute | solution.py:55
  94.2 9.9 %collective-permute-start.15 = (bf16[136,512]{1,0:T(8,128)(2,1)S(1)}, bf16[136,512]{1,0:T(8,128)(2,1)S(1)}, u32[]{:S(2)}, u32[]{:S(2)}) collective-permute-start(bf16[136,512]{1,0:T(8,128)(2,1)S(1)} %collective-permute-done.14), channel_id=1, source_target_pairs={{0,14},{2,0},{4,2},{6,4},{8,6},{10,8},{12,10},{14,12},{1,15},{3,1}... | collective-permute-start | bytes 417800 | tf_op jit(solution)/shard_map/while/body/ppermute | solution.py:55
  96.5 6.2 %collective-permute-start.12 = (bf16[136,512]{1,0:T(8,128)(2,1)S(1)}, bf16[136,512]{1,0:T(8,128)(2,1)S(1)}, u32[]{:S(2)}, u32[]{:S(2)}) collective-permute-start(bf16[136,512]{1,0:T(8,128)(2,1)S(1)} %collective-permute-done.11), channel_id=1, source_target_pairs={{0,2},{2,4},{4,6},{6,8},{8,10},{10,12},{12,14},{14,0},{1,3},{3,5},... | collective-permute-start | bytes 417800 | tf_op jit(solution)/shard_map/while/body/ppermute | solution.py:55
  97.7 6.4 %collective-permute-start.7 = (bf16[136,512]{1,0:T(8,128)(2,1)S(1)}, bf16[136,512]{1,0:T(8,128)(2,1)S(1)}, u32[]{:S(2)}, u32[]{:S(2)}) collective-permute-start(bf16[136,512]{1,0:T(8,128)(2,1)S(1)} %collective-permute-done.6), channel_id=1, source_target_pairs={{0,2},{2,4},{4,6},{6,8},{8,10},{10,12},{12,14},{14,0},{1,3},{3,5},... | collective-permute-start | bytes 417800 | tf_op jit(solution)/shard_map/while/body/ppermute | solution.py:55
  97.8 6.4 %collective-permute-start.2 = (bf16[136,512]{1,0:T(8,128)(2,1)S(1)}, bf16[136,512]{1,0:T(8,128)(2,1)S(1)}, u32[]{:S(2)}, u32[]{:S(2)}) collective-permute-start(bf16[136,512]{1,0:T(8,128)(2,1)S(1)} %collective-permute-done.1), channel_id=1, source_target_pairs={{0,14},{2,0},{4,2},{6,4},{8,6},{10,8},{12,10},{14,12},{1,15},{3,1}... | collective-permute-start | bytes 417800 | tf_op jit(solution)/shard_map/while/body/ppermute | solution.py:55
  102.6 16.0 %collective-permute-start.17 = (bf16[136,512]{1,0:T(8,128)(2,1)S(1)}, bf16[136,512]{1,0:T(8,128)(2,1)S(1)}, u32[]{:S(2)}, u32[]{:S(2)}) collective-permute-start(bf16[136,512]{1,0:T(8,128)(2,1)S(1)} %collective-permute-done.12), channel_id=1, source_target_pairs={{0,2},{2,4},{4,6},{6,8},{8,10},{10,12},{12,14},{14,0},{1,3},{3,5},... | collective-permute-start | bytes 417800 | tf_op jit(solution)/shard_map/while/body/ppermute | solution.py:55
  104.1 7.8 %collective-permute-start.8 = (bf16[136,512]{1,0:T(8,128)(2,1)S(1)}, bf16[136,512]{1,0:T(8,128)(2,1)S(1)}, u32[]{:S(2)}, u32[]{:S(2)}) collective-permute-start(bf16[136,512]{1,0:T(8,128)(2,1)S(1)} %collective-permute-done.7), channel_id=1, source_target_pairs={{0,2},{2,4},{4,6},{6,8},{8,10},{10,12},{12,14},{14,0},{1,3},{3,5},... | collective-permute-start | bytes 417800 | tf_op jit(solution)/shard_map/while/body/ppermute | solution.py:55
  104.2 7.7 %collective-permute-start.3 = (bf16[136,512]{1,0:T(8,128)(2,1)S(1)}, bf16[136,512]{1,0:T(8,128)(2,1)S(1)}, u32[]{:S(2)}, u32[]{:S(2)}) collective-permute-start(bf16[136,512]{1,0:T(8,128)(2,1)S(1)} %collective-permute-done.2), channel_id=1, source_target_pairs={{0,14},{2,0},{4,2},{6,4},{8,6},{10,8},{12,10},{14,12},{1,15},{3,1}... | collective-permute-start | bytes 417800 | tf_op jit(solution)/shard_map/while/body/ppermute | solution.py:55
  111.9 15.8 %collective-permute-start.9 = (bf16[272,512]{1,0:T(8,128)(2,1)S(1)}, bf16[272,512]{1,0:T(8,128)(2,1)S(1)}, u32[]{:S(2)}, u32[]{:S(2)}) collective-permute-start(bf16[272,512]{1,0:T(8,128)(2,1)S(1)} %pad_maximum_fusion.11), channel_id=1, source_target_pairs={{0,1},{1,0},{2,3},{3,2},{4,5},{5,4},{6,7},{7,6},{8,9},{9,8},{10,11... | collective-permute-start | bytes 835592 | tf_op jit(solution)/shard_map/while/body/ppermute | solution.py:46
  118.7 9.0 %collective-permute-start.18 = (bf16[408,512]{1,0:T(8,128)(2,1)S(1)}, bf16[408,512]{1,0:T(8,128)(2,1)S(1)}, u32[]{:S(2)}, u32[]{:S(2)}) collective-permute-start(bf16[408,512]{1,0:T(8,128)(2,1)S(1)} %pad_maximum_fusion.12), channel_id=1, source_target_pairs={{0,1},{1,0},{2,3},{3,2},{4,5},{5,4},{6,7},{7,6},{8,9},{9,8},{10,11... | collective-permute-start | bytes 1253384 | tf_op jit(solution)/shard_map/while/body/ppermute | solution.py:46
  118.9 8.9 %collective-permute-start.16 = (bf16[680,512]{1,0:T(8,128)(2,1)S(1)}, bf16[680,512]{1,0:T(8,128)(2,1)S(1)}, u32[]{:S(2)}, u32[]{:S(2)}) collective-permute-start(bf16[680,512]{1,0:T(8,128)(2,1)S(1)} %constant_dynamic-update-slice_fusion.27), channel_id=1, source_target_pairs={{0,1},{1,0},{2,3},{3,2},{4,5},{5,4},{6,7},{7,6},{8,9},{9,8},{10,11... | collective-permute-start | bytes 2088968 | tf_op jit(solution)/shard_map/while/body/ppermute | solution.py:46
  119.5 8.2 %collective-permute-start.19 = (bf16[680,512]{1,0:T(8,128)(2,1)S(1)}, bf16[680,512]{1,0:T(8,128)(2,1)S(1)}, u32[]{:S(2)}, u32[]{:S(2)}) collective-permute-start(bf16[680,512]{1,0:T(8,128)(2,1)S(1)} %constant_dynamic-update-slice_fusion.32), channel_id=1, source_target_pairs={{0,1},{1,0},{2,3},{3,2},{4,5},{5,4},{6,7},{7,6},{8,9},{9,8},{10,11... | collective-permute-start | bytes 2088968 | tf_op jit(solution)/shard_map/while/body/ppermute | solution.py:46
  119.6 5.7 %collective-permute-start.4 = (bf16[136,512]{1,0:T(8,128)(2,1)S(1)}, bf16[136,512]{1,0:T(8,128)(2,1)S(1)}, u32[]{:S(2)}, u32[]{:S(2)}) collective-permute-start(bf16[136,512]{1,0:T(8,128)(2,1)S(1)} %collective-permute-done.3), channel_id=1, source_target_pairs={{0,14},{2,0},{4,2},{6,4},{8,6},{10,8},{12,10},{14,12},{1,15},{3,1}... | collective-permute-start | bytes 417800 | tf_op jit(solution)/shard_map/while/body/ppermute | solution.py:55
  125.3 2.3 %collective-permute-start.5 = (bf16[136,512]{1,0:T(8,128)(2,1)S(1)}, bf16[136,512]{1,0:T(8,128)(2,1)S(1)}, u32[]{:S(2)}, u32[]{:S(2)}) collective-permute-start(bf16[136,512]{1,0:T(8,128)(2,1)S(1)} %collective-permute-done.4), channel_id=1, source_target_pairs={{0,1},{1,0},{2,3},{3,2},{4,5},{5,4},{6,7},{7,6},{8,9},{9,8},{10,11... | collective-permute-start | bytes 417800 | tf_op jit(solution)/shard_map/while/body/ppermute | solution.py:46
  128.2 4.8 %slice-start = ((s8[8388608]{0:T(1024)(128)(4,1)}), s8[4194304]{0:T(1024)(128)(4,1)S(1)}, s32[]{:S(2)}) async-start(s8[8388608]{0:T(1024)(128)(4,1)} %bitcast.190), calls=%async_computation.2 | async-start | bytes 8388608 | tf_op jit(solution)/shard_map/while
  136.0 18.6 %copy-start.10 = (s32[1,1,128]{2,1,0:T(1,128)S(1)}, s32[1,1,128]{2,1,0:T(1,128)}, u32[]{:S(2)}) copy-start(s32[1,1,128]{2,1,0:T(1,128)} %get-tuple-element.874) | copy-start | bytes 1540 | tf_op jit(solution)/shard_map/while
  136.0 18.6 %copy-start.9 = (f32[1,1,128]{2,1,0:T(1,128)S(1)}, f32[1,1,128]{2,1,0:T(1,128)}, u32[]{:S(2)}) copy-start(f32[1,1,128]{2,1,0:T(1,128)} %get-tuple-element.872) | copy-start | bytes 1540 | tf_op jit(solution)/shard_map/while
  136.0 18.6 %copy-start.5 = (f32[512]{0:T(512)S(1)}, f32[512]{0:T(512)}, u32[]{:S(2)}) copy-start(f32[512]{0:T(512)} %get-tuple-element.1005) | copy-start | bytes 6148 | tf_op jit(solution)/shard_map/while
  136.0 18.6 %copy-start.11 = (f32[1,1,128]{2,1,0:T(1,128)S(1)}, f32[1,1,128]{2,1,0:T(1,128)}, u32[]{:S(2)}) copy-start(f32[1,1,128]{2,1,0:T(1,128)} %get-tuple-element.873) | copy-start | bytes 1540 | tf_op jit(solution)/shard_map/while
  156.5 27.0 %copy-start.1 = (f32[128,512]{1,0:T(8,128)}, f32[128,512]{1,0:T(8,128)S(1)}, u32[]{:S(2)}) copy-start(f32[128,512]{1,0:T(8,128)S(1)} %get-tuple-element.472) | copy-start | bytes 786436
  156.5 2.5 %collective-permute-start.20 = (f32[256]{0:T(256)S(1)}, f32[256]{0:T(256)S(1)}, u32[]{:S(2)}, u32[]{:S(2)}) collective-permute-start(f32[256]{0:T(256)S(1)} %broadcast_select_fusion.1), channel_id=1, source_target_pairs={{0,1},{1,0},{2,3},{3,2},{4,5},{5,4},{6,7},{7,6},{8,9},{9,8},{10,11... | collective-permute-start | bytes 3080 | tf_op jit(solution)/shard_map/ppermute | solution.py:46
  180.3 2.6 %collective-permute-start.21 = (f32[256]{0:T(256)S(1)}, f32[256]{0:T(256)S(1)}, u32[]{:S(2)}, u32[]{:S(2)}) collective-permute-start(f32[256]{0:T(256)S(1)} %reduce_max.21), channel_id=1, source_target_pairs={{0,1},{1,0},{2,3},{3,2},{4,5},{5,4},{6,7},{7,6},{8,9},{9,8},{10,11... | collective-permute-start | bytes 3080 | tf_op jit(solution)/shard_map/ppermute | solution.py:46
  (5 other events, 8.4 us)

commit v2 on v1

--- a/solution.py
+++ b/solution.py
@@ -74,7 +74,6 @@
     depth = lax.axis_size("z")
     here = lax.axis_index("z")
     near = lax.axis_index("yh")
-    first = core == 0
 
     fault = (rate_table, evolve_table, patch_region, creep_flag, normal_stress, load_stress)
 
@@ -136,20 +135,23 @@
         found += [joined(block[elements:]) for side in other for _, block in side]
         return mine, other, found
 
-    def placed(mine, other):
-        slips = jnp.zeros((half, members), jnp.bfloat16)
+    def placed(mine, other, blank):
+        slips = blank
         for owner_core, blocks in ((core, mine), (1 - core, other)):
             for shift, block in blocks:
                 owner = 2 * lax.rem(here + shift + depth, depth) + owner_core
-                slips = lax.dynamic_update_slice(slips, block[:elements], (owner * elements, 0))
-        return slips
+                block = block[:elements].reshape(-1, *blank.shape[1:])
+                start = (owner * block.shape[0], *(0 for _ in blank.shape[1:]))
+                slips = lax.dynamic_update_slice(slips, block, start)
+        return slips.reshape(half, members)
 
     def partial_of(mine, other, side):
-        slips = placed(mine[0], other[0])
+        near_blank = jnp.zeros((half, members), jnp.bfloat16)
+        far_blank = jnp.zeros((half // elements, elements, members), jnp.bfloat16)
+        slips = placed(mine[0], other[0], near_blank)
         partial = jnp.dot(tile_of(side), slips, preferred_element_type=jnp.float32)
-        (shift, block) = other[1][-1]
-        partial, block = lax.optimization_barrier((partial, block))
-        slips = placed(mine[1], [*other[1][:-1], (shift, block)])
+        partial = lax.optimization_barrier(partial)
+        slips = placed(mine[1], other[1], far_blank)
         partial += jnp.dot(tile_of(1 - side), slips, preferred_element_type=jnp.float32)
         return partial.astype(jnp.bfloat16).reshape(-1, elements, members)
 
@@ -175,22 +177,13 @@
         )
 
     def largest_of(local):
-        count = members // 2
-        mine = jnp.where(first, local[:count], local[count:])
-        other = jnp.where(first, local[count:], local[:count])
-        mine = jnp.maximum(mine, swap_cores(other))
+        local = jnp.maximum(local, swap_cores(local))
         chips = functools.reduce(lambda n, axis: n * lax.axis_size(axis), CHIPS, 1)
-        everyone = lax.all_to_all(
-            jnp.broadcast_to(mine, (chips, count)), CHIPS, 0, 0, tiled=True
-        )
-        mine = jnp.max(everyone, axis=0)
-        other = swap_cores(mine)
-        return jnp.where(first, jnp.concatenate([mine, other]), jnp.concatenate([other, mine]))
+        everyone = jnp.broadcast_to(local, (chips, members))
+        return jnp.max(lax.all_to_all(everyone, CHIPS, 0, 0, tiled=True), axis=0)
 
     def step(carry):
         index, deficit, state, _, local = carry
-        deficit = jnp.where(index == 0, slip_deficit.reshape(elements, members), deficit)
-        state = jnp.where(index == 0, state_variable.reshape(elements, members), state)
         block = jnp.concatenate([deficit.astype(jnp.bfloat16), split_rows(local)])
         mine, other, found = gathered(block)
         side, held, _ = lax.optimization_barrier((near, fault, index))
@@ -199,10 +192,11 @@
         rows = split_rows(functools.reduce(jnp.maximum, found))
         rows = jnp.broadcast_to(rows, (parts.shape[0], *rows.shape))
         parts = jnp.concatenate([parts, rows], axis=1)
-        held = (coefs, deficit, state, index)
+        held = (coefs, deficit, state, state_variable, index)
         parts, held = lax.optimization_barrier((parts, held))
         parts, held = lax.optimization_barrier((exchanged(parts), held))
-        coefs, deficit, state, index = held
+        coefs, deficit, state, begin, index = held
+        state = jnp.where(index == 0, begin.reshape(elements, members), state)
         velocity = solved(summed(parts[:, :elements]), state, coefs)
         local = jnp.max(jnp.abs(velocity), axis=0)
         found = [joined(parts[row, elements:]) for row in range(parts.shape[0])]
@@ -212,7 +206,8 @@
         return index + 1, deficit, state, velocity, local
 
     blank = jnp.zeros((elements, members), jnp.float32)
-    carry = (jnp.int32(0), blank, blank, blank, jnp.zeros((members,), jnp.float32))
+    deficit = slip_deficit.reshape(elements, members)
+    carry = (jnp.int32(0), deficit, blank, blank, jnp.zeros((members,), jnp.float32))
     carry = lax.while_loop(lambda carry: carry[0] < STEPS, step, carry)
     _, deficit, state, velocity, local = carry
     step_next = STEP_CAP / (1.0 + largest_of(local))

time: 184 us -> 176 us (0.957)
  matrix products: 14 us -> 9.31 us
  blocking collectives: 59.9 us -> 62.6 us
  other arithmetic: 7.08 us -> 4.66 us
  starting transfers between devices: 68.6 us -> 66.7 us
    dot_general x2, matrix products: 9.36 us -> 4.64 us  [partial_of(): partial = jnp.dot(tile_of(side), slips, preferred_element_type=jnp.float32)]
    all_to_all x1, blocking collectives: 21.1 us -> 23.8 us  [largest_of(): return jnp.max(lax.all_to_all(everyone, CHIPS, 0, 0, tiled=True), axis=0)]
    ppermute x12 -> x11, starting transfers between devices: 20.1 us -> 18.3 us  [swap_cores(): return lax.ppermute(x, 'c', ((0, 1), (1, 0)))]
  transfers between devices with their start and end apart: 42 -> 41, of which waited for: 15 -> 14; matrix products, arithmetic and copies ran while one was open for 1% -> 4% of each run, Pallas kernels for 0% -> 0%
where the time goes in v2:
time: 176 us
  starting transfers between devices  66.7 us (38%)
  blocking collectives  62.6 us (36%)
  waiting for transfers between devices  25.8 us (15%)
  matrix products  9.31 us (5%)
  local copies, waits for them, and re-layouts  4.82 us (3%)
  other arithmetic  4.66 us (3%)
    ppermute x28, starting transfers between devices, shifted(): return lax.ppermute(x, 'z', [(z, (z + by) % depth) for z in range(depth)])  42.8 us
    all_to_all x2, blocking collectives, exchanged(): return lax.all_to_all(parts, ROW, 0, 0, tiled=True)  38.8 us
    all_to_all x1, blocking collectives, largest_of(): return jnp.max(lax.all_to_all(everyone, CHIPS, 0, 0, tiled=True), axis=0)  23.8 us
    ppermute x28, waiting for transfers between devices, shifted(): return lax.ppermute(x, 'z', [(z, (z + by) % depth) for z in range(depth)])  23 us
    ppermute x11, starting transfers between devices, swap_cores(): return lax.ppermute(x, 'c', ((0, 1), (1, 0)))  18.3 us
    ppermute x2, starting transfers between devices, swap_far(): return lax.ppermute(x, 'yh', ((0, 1), (1, 0)))  5.53 us
    dot_general x2, matrix products, partial_of(): jnp.dot(tile_of(1 - side), slips, preferred_element_type=jnp.float32)  4.67 us
    dot_general x2, matrix products, partial_of(): partial = jnp.dot(tile_of(side), slips, preferred_element_type=jnp.float32)  4.64 us
  transfers between devices with their start and end apart: 41, of which 14 were waited for; matrix products, arithmetic and copies ran while one was open for 4% of the time, Pallas kernels for 0%

profile of v2, /device:TPU:1, one launch (start us, length us, event | category | flops | bytes accessed | tf_op | source)
XLA Modules:
  0.0 176.0 jit_solution(9177474769006697578)
XLA Ops:
  0.6 1.0 copy.72
  1.6 0.7 broadcast.108.clone
  2.3 146.5 %while.18 = (s32[]{:T(128)}, f32[128,512]{1,0:T(8,128)S(1)}, f32[128,512]{1,0:T(8,128)S(1)}, f32[128,512]{1,0:T(8,128)}, f32[512]{0:T(512)S(1)}, /*index=5*/s32[...) while((s32[]{:T(128)}, f32[128,512]{1,0:T(8,128)S(1)}, ...), condition=%wide.region_5.6_spmd, body=%wide.region_0.5_spmd.sunk | while | flops 4306238976 | bytes 96793648 | solution.py:211
  2.4 0.1 broadcast.139
  2.6 6.5 %collective-permute-start.13 = (bf16[136,512]{1,0:T(8,128)(2,1)S(1)}, bf16[136,512]{1,0:T(8,128)(2,1)S(1)}, u32[]{:S(2)}, u32[]{:S(2)}) collective-permute-start(bf16[136,512]{1,0:T(8,128)(2,1)S(1)} %pad_maximum_fusion.10), channel_id=1, source_target_pairs={{0,14},{2,0},{4,2},{6,4},{8,6},{10,8},{12,10},{14,12},{1,15},{3,1}... | collective-permute-start | bytes 417800 | tf_op jit(solution)/shard_map/while/body/ppermute | solution.py:55
  9.1 2.9 %collective-permute-start = (bf16[136,512]{1,0:T(8,128)(2,1)S(1)}, bf16[136,512]{1,0:T(8,128)(2,1)S(1)}, u32[]{:S(2)}, u32[]{:S(2)}) collective-permute-start(bf16[136,512]{1,0:T(8,128)(2,1)S(1)} %pad_maximum_fusion.10), channel_id=1, source_target_pairs={{0,16},{16,0},{1,17},{17,1},{2,18},{18,2},{3,19},{19,3},{4,20},{20... | collective-permute-start | bytes 417800 | tf_op jit(solution)/shard_map/while/body/ppermute | solution.py:50
  12.1 2.8 %collective-permute-start.14 = (bf16[136,512]{1,0:T(8,128)(2,1)S(1)}, bf16[136,512]{1,0:T(8,128)(2,1)S(1)}, u32[]{:S(2)}, u32[]{:S(2)}) collective-permute-start(bf16[136,512]{1,0:T(8,128)(2,1)S(1)} %collective-permute-done.13), channel_id=1, source_target_pairs={{0,14},{2,0},{4,2},{6,4},{8,6},{10,8},{12,10},{14,12},{1,15},{3,1}... | collective-permute-start | bytes 417800 | tf_op jit(solution)/shard_map/while/body/ppermute | solution.py:55
  15.1 2.7 %collective-permute-start.1 = (bf16[136,512]{1,0:T(8,128)(2,1)S(1)}, bf16[136,512]{1,0:T(8,128)(2,1)S(1)}, u32[]{:S(2)}, u32[]{:S(2)}) collective-permute-start(bf16[136,512]{1,0:T(8,128)(2,1)S(1)} %collective-permute-done), channel_id=1, source_target_pairs={{0,14},{2,0},{4,2},{6,4},{8,6},{10,8},{12,10},{14,12},{1,15},{3,1}... | collective-permute-start | bytes 417800 | tf_op jit(solution)/shard_map/while/body/ppermute | solution.py:55
  17.9 0.2 broadcast.140
  18.1 1.9 %collective-permute-start.15 = (bf16[136,512]{1,0:T(8,128)(2,1)S(1)}, bf16[136,512]{1,0:T(8,128)(2,1)S(1)}, u32[]{:S(2)}, u32[]{:S(2)}) collective-permute-start(bf16[136,512]{1,0:T(8,128)(2,1)S(1)} %collective-permute-done.14), channel_id=1, source_target_pairs={{0,14},{2,0},{4,2},{6,4},{8,6},{10,8},{12,10},{14,12},{1,15},{3,1}... | collective-permute-start | bytes 417800 | tf_op jit(solution)/shard_map/while/body/ppermute | solution.py:55
  20.1 2.5 %collective-permute-done.6 = bf16[136,512]{1,0:T(8,128)(2,1)S(1)} collective-permute-done((bf16[136,512]{1,0:T(8,128)(2,1)S(1)}, bf16[136,512]{1,0:T(8,128)(2,1)S(1)}, u32[]{:S(2)}, u32[]{:S(2)}) %collective-permute-start.6) | collective-permute-done | bytes 139296 | tf_op jit(solution)/shard_map/while/body/ppermute | solution.py:55
  22.6 2.7 %collective-permute-start.2 = (bf16[136,512]{1,0:T(8,128)(2,1)S(1)}, bf16[136,512]{1,0:T(8,128)(2,1)S(1)}, u32[]{:S(2)}, u32[]{:S(2)}) collective-permute-start(bf16[136,512]{1,0:T(8,128)(2,1)S(1)} %collective-permute-done.1), channel_id=1, source_target_pairs={{0,14},{2,0},{4,2},{6,4},{8,6},{10,8},{12,10},{14,12},{1,15},{3,1}... | collective-permute-start | bytes 417800 | tf_op jit(solution)/shard_map/while/body/ppermute | solution.py:55
  25.4 0.6 collective-permute-done.12
  26.1 1.6 collective-permute-done.7
  27.7 2.7 %collective-permute-start.3 = (bf16[136,512]{1,0:T(8,128)(2,1)S(1)}, bf16[136,512]{1,0:T(8,128)(2,1)S(1)}, u32[]{:S(2)}, u32[]{:S(2)}) collective-permute-start(bf16[136,512]{1,0:T(8,128)(2,1)S(1)} %collective-permute-done.2), channel_id=1, source_target_pairs={{0,14},{2,0},{4,2},{6,4},{8,6},{10,8},{12,10},{14,12},{1,15},{3,1}... | collective-permute-start | bytes 417800 | tf_op jit(solution)/shard_map/while/body/ppermute | solution.py:55
  30.6 3.9 %collective-permute-done.8 = bf16[136,512]{1,0:T(8,128)(2,1)S(1)} collective-permute-done((bf16[136,512]{1,0:T(8,128)(2,1)S(1)}, bf16[136,512]{1,0:T(8,128)(2,1)S(1)}, u32[]{:S(2)}, u32[]{:S(2)}) %collective-permute-start.8) | collective-permute-done | bytes 139296 | tf_op jit(solution)/shard_map/while/body/ppermute | solution.py:55
  34.5 5.7 %collective-permute-start.9 = (bf16[272,512]{1,0:T(8,128)(2,1)S(1)}, bf16[272,512]{1,0:T(8,128)(2,1)S(1)}, u32[]{:S(2)}, u32[]{:S(2)}) collective-permute-start(bf16[272,512]{1,0:T(8,128)(2,1)S(1)} %pad_maximum_fusion.11), channel_id=1, source_target_pairs={{0,1},{1,0},{2,3},{3,2},{4,5},{5,4},{6,7},{7,6},{8,9},{9,8},{10,11... | collective-permute-start | bytes 835592 | tf_op jit(solution)/shard_map/while/body/ppermute | solution.py:46
  40.3 0.1 collective-permute-start.18
  40.5 0.6 collective-permute-start.19
  41.1 0.1 collective-permute-start.16
  41.3 3.1 %collective-permute-start.4 = (bf16[136,512]{1,0:T(8,128)(2,1)S(1)}, bf16[136,512]{1,0:T(8,128)(2,1)S(1)}, u32[]{:S(2)}, u32[]{:S(2)}) collective-permute-start(bf16[136,512]{1,0:T(8,128)(2,1)S(1)} %collective-permute-done.3), channel_id=1, source_target_pairs={{0,14},{2,0},{4,2},{6,4},{8,6},{10,8},{12,10},{14,12},{1,15},{3,1}... | collective-permute-start | bytes 417800 | tf_op jit(solution)/shard_map/while/body/ppermute | solution.py:55
  44.5 2.5 %collective-permute-done.4 = bf16[136,512]{1,0:T(8,128)(2,1)S(1)} collective-permute-done((bf16[136,512]{1,0:T(8,128)(2,1)S(1)}, bf16[136,512]{1,0:T(8,128)(2,1)S(1)}, u32[]{:S(2)}, u32[]{:S(2)}) %collective-permute-start.4) | collective-permute-done | bytes 139296 | tf_op jit(solution)/shard_map/while/body/ppermute | solution.py:55
  47.0 1.3 collective-permute-start.5
  48.3 1.0 collective-permute-done.5
  49.6 2.3 %fusion.156 = f32[1024,512]{1,0:T(8,128)S(1)} fusion(bf16[2048,512]{1,0:T(8,128)(2,1)S(1)} %slice_dynamic-update-slice_fusion.44, bf16[1024,4096]{1,0:T(8,128)(2,1)S(1)} %copy-done.9, s32[]{:T(128)S(6)} %select_n.327), kind=kOutput, calls=%fused_computation.2.clone.1 | convolution fusion | flops 2147483648 | bytes 8388612 | tf_op jit(solution)/shard_map/while/body/dot_general | solution.py:152
  52.2 2.3 %add_convert_fusion.2 = bf16[1024,512]{1,0:T(8,128)(2,1)S(1)} fusion(f32[1024,512]{1,0:T(8,128)S(1)} %fusion.156, bf16[2048,512]{1,0:T(8,128)(2,1)S(1)} %bitcast.252, bf16[1024,4096]{1,0:T(8,128)(2,1)S(1)} %copy-done.9, s32[]{:T(128)S(6)} %select_n.328), kind=kOutput, calls=%fused_computation.5.clone.1 | convolution fusion | flops 2148532224 | bytes 9437188 | tf_op jit(solution)/shard_map/while/body/dot_general | solution.py:155
  54.7 20.5 %all_to_all.16 = bf16[8,136,512]{2,1,0:T(8,128)(2,1)S(1)} all-to-all(bf16[8,136,512]{2,1,0:T(8,128)(2,1)S(1)} %pad_maximum_fusion.14), channel_id=1, replica_groups=mesh['x'=4,'yl'=2,'yh'=2,'z'=8,'c'=2] {'x','yl'}, dimensions={0} | all-to-all | bytes 2228224 | tf_op jit(solution)/shard_map/while/body/all_to_all | solution.py:162
  75.3 0.1 convert_reduce_fusion.2
  75.5 1.0 abs_reduce_fusion.2
  76.5 0.2 exponential_multiply_fusion.2
  76.8 0.5 copy-done.1
  77.3 0.1 broadcast.139
  77.5 3.5 %collective-permute-start.13 = (bf16[136,512]{1,0:T(8,128)(2,1)S(1)}, bf16[136,512]{1,0:T(8,128)(2,1)S(1)}, u32[]{:S(2)}, u32[]{:S(2)}) collective-permute-start(bf16[136,512]{1,0:T(8,128)(2,1)S(1)} %pad_maximum_fusion.10), channel_id=1, source_target_pairs={{0,14},{2,0},{4,2},{6,4},{8,6},{10,8},{12,10},{14,12},{1,15},{3,1}... | collective-permute-start | bytes 417800 | tf_op jit(solution)/shard_map/while/body/ppermute | solution.py:55
  81.0 2.6 %collective-permute-start = (bf16[136,512]{1,0:T(8,128)(2,1)S(1)}, bf16[136,512]{1,0:T(8,128)(2,1)S(1)}, u32[]{:S(2)}, u32[]{:S(2)}) collective-permute-start(bf16[136,512]{1,0:T(8,128)(2,1)S(1)} %pad_maximum_fusion.10), channel_id=1, source_target_pairs={{0,16},{16,0},{1,17},{17,1},{2,18},{18,2},{3,19},{19,3},{4,20},{20... | collective-permute-start | bytes 417800 | tf_op jit(solution)/shard_map/while/body/ppermute | solution.py:50
  83.7 2.7 %collective-permute-start.14 = (bf16[136,512]{1,0:T(8,128)(2,1)S(1)}, bf16[136,512]{1,0:T(8,128)(2,1)S(1)}, u32[]{:S(2)}, u32[]{:S(2)}) collective-permute-start(bf16[136,512]{1,0:T(8,128)(2,1)S(1)} %collective-permute-done.13), channel_id=1, source_target_pairs={{0,14},{2,0},{4,2},{6,4},{8,6},{10,8},{12,10},{14,12},{1,15},{3,1}... | collective-permute-start | bytes 417800 | tf_op jit(solution)/shard_map/while/body/ppermute | solution.py:55
  86.7 2.7 %collective-permute-start.1 = (bf16[136,512]{1,0:T(8,128)(2,1)S(1)}, bf16[136,512]{1,0:T(8,128)(2,1)S(1)}, u32[]{:S(2)}, u32[]{:S(2)}) collective-permute-start(bf16[136,512]{1,0:T(8,128)(2,1)S(1)} %collective-permute-done), channel_id=1, source_target_pairs={{0,14},{2,0},{4,2},{6,4},{8,6},{10,8},{12,10},{14,12},{1,15},{3,1}... | collective-permute-start | bytes 417800 | tf_op jit(solution)/shard_map/while/body/ppermute | solution.py:55
  89.4 0.2 broadcast.140
  89.7 2.2 %collective-permute-start.15 = (bf16[136,512]{1,0:T(8,128)(2,1)S(1)}, bf16[136,512]{1,0:T(8,128)(2,1)S(1)}, u32[]{:S(2)}, u32[]{:S(2)}) collective-permute-start(bf16[136,512]{1,0:T(8,128)(2,1)S(1)} %collective-permute-done.14), channel_id=1, source_target_pairs={{0,14},{2,0},{4,2},{6,4},{8,6},{10,8},{12,10},{14,12},{1,15},{3,1}... | collective-permute-start | bytes 417800 | tf_op jit(solution)/shard_map/while/body/ppermute | solution.py:55
  92.0 1.2 collective-permute-done.6
  93.2 2.9 %collective-permute-start.2 = (bf16[136,512]{1,0:T(8,128)(2,1)S(1)}, bf16[136,512]{1,0:T(8,128)(2,1)S(1)}, u32[]{:S(2)}, u32[]{:S(2)}) collective-permute-start(bf16[136,512]{1,0:T(8,128)(2,1)S(1)} %collective-permute-done.1), channel_id=1, source_target_pairs={{0,14},{2,0},{4,2},{6,4},{8,6},{10,8},{12,10},{14,12},{1,15},{3,1}... | collective-permute-start | bytes 417800 | tf_op jit(solution)/shard_map/while/body/ppermute | solution.py:55
  96.2 1.8 %collective-permute-done.12 = bf16[136,512]{1,0:T(8,128)(2,1)S(1)} collective-permute-done((bf16[136,512]{1,0:T(8,128)(2,1)S(1)}, bf16[136,512]{1,0:T(8,128)(2,1)S(1)}, u32[]{:S(2)}, u32[]{:S(2)}) %collective-permute-start.12) | collective-permute-done | bytes 139296 | tf_op jit(solution)/shard_map/while/body/ppermute | solution.py:55
  98.1 1.5 collective-permute-done.7
  99.6 2.7 %collective-permute-start.3 = (bf16[136,512]{1,0:T(8,128)(2,1)S(1)}, bf16[136,512]{1,0:T(8,128)(2,1)S(1)}, u32[]{:S(2)}, u32[]{:S(2)}) collective-permute-start(bf16[136,512]{1,0:T(8,128)(2,1)S(1)} %collective-permute-done.2), channel_id=1, source_target_pairs={{0,14},{2,0},{4,2},{6,4},{8,6},{10,8},{12,10},{14,12},{1,15},{3,1}... | collective-permute-start | bytes 417800 | tf_op jit(solution)/shard_map/while/body/ppermute | solution.py:55
  102.4 4.9 %collective-permute-done.8 = bf16[136,512]{1,0:T(8,128)(2,1)S(1)} collective-permute-done((bf16[136,512]{1,0:T(8,128)(2,1)S(1)}, bf16[136,512]{1,0:T(8,128)(2,1)S(1)}, u32[]{:S(2)}, u32[]{:S(2)}) %collective-permute-start.8) | collective-permute-done | bytes 139296 | tf_op jit(solution)/shard_map/while/body/ppermute | solution.py:55
  107.3 6.7 %collective-permute-start.9 = (bf16[272,512]{1,0:T(8,128)(2,1)S(1)}, bf16[272,512]{1,0:T(8,128)(2,1)S(1)}, u32[]{:S(2)}, u32[]{:S(2)}) collective-permute-start(bf16[272,512]{1,0:T(8,128)(2,1)S(1)} %pad_maximum_fusion.11), channel_id=1, source_target_pairs={{0,1},{1,0},{2,3},{3,2},{4,5},{5,4},{6,7},{7,6},{8,9},{9,8},{10,11... | collective-permute-start | bytes 835592 | tf_op jit(solution)/shard_map/while/body/ppermute | solution.py:46
  114.1 0.1 collective-permute-start.18
  114.3 0.6 collective-permute-start.19
  115.1 3.1 %collective-permute-start.4 = (bf16[136,512]{1,0:T(8,128)(2,1)S(1)}, bf16[136,512]{1,0:T(8,128)(2,1)S(1)}, u32[]{:S(2)}, u32[]{:S(2)}) collective-permute-start(bf16[136,512]{1,0:T(8,128)(2,1)S(1)} %collective-permute-done.3), channel_id=1, source_target_pairs={{0,14},{2,0},{4,2},{6,4},{8,6},{10,8},{12,10},{14,12},{1,15},{3,1}... | collective-permute-start | bytes 417800 | tf_op jit(solution)/shard_map/while/body/ppermute | solution.py:55
  118.3 2.5 %collective-permute-done.4 = bf16[136,512]{1,0:T(8,128)(2,1)S(1)} collective-permute-done((bf16[136,512]{1,0:T(8,128)(2,1)S(1)}, bf16[136,512]{1,0:T(8,128)(2,1)S(1)}, u32[]{:S(2)}, u32[]{:S(2)}) %collective-permute-start.4) | collective-permute-done | bytes 139296 | tf_op jit(solution)/shard_map/while/body/ppermute | solution.py:55
  120.7 1.3 collective-permute-start.5
  122.1 1.0 collective-permute-done.5
  123.3 2.3 %fusion.156 = f32[1024,512]{1,0:T(8,128)S(1)} fusion(bf16[2048,512]{1,0:T(8,128)(2,1)S(1)} %slice_dynamic-update-slice_fusion.44, bf16[1024,4096]{1,0:T(8,128)(2,1)S(1)} %copy-done.9, s32[]{:T(128)S(6)} %select_n.327), kind=kOutput, calls=%fused_computation.2.clone.1 | convolution fusion | flops 2147483648 | bytes 8388612 | tf_op jit(solution)/shard_map/while/body/dot_general | solution.py:152
  126.0 2.3 %add_convert_fusion.2 = bf16[1024,512]{1,0:T(8,128)(2,1)S(1)} fusion(f32[1024,512]{1,0:T(8,128)S(1)} %fusion.156, bf16[2048,512]{1,0:T(8,128)(2,1)S(1)} %bitcast.252, bf16[1024,4096]{1,0:T(8,128)(2,1)S(1)} %copy-done.9, s32[]{:T(128)S(6)} %select_n.328), kind=kOutput, calls=%fused_computation.5.clone.1 | convolution fusion | flops 2148532224 | bytes 9437188 | tf_op jit(solution)/shard_map/while/body/dot_general | solution.py:155
  128.5 18.3 %all_to_all.16 = bf16[8,136,512]{2,1,0:T(8,128)(2,1)S(1)} all-to-all(bf16[8,136,512]{2,1,0:T(8,128)(2,1)S(1)} %pad_maximum_fusion.14), channel_id=1, replica_groups=mesh['x'=4,'yl'=2,'yh'=2,'z'=8,'c'=2] {'x','yl'}, dimensions={0} | all-to-all | bytes 2228224 | tf_op jit(solution)/shard_map/while/body/all_to_all | solution.py:162
  146.8 0.1 convert_reduce_fusion.2
  147.1 1.0 abs_reduce_fusion.2
  148.1 0.2 exponential_multiply_fusion.2
  148.3 0.5 copy-done.1
  148.8 1.6 collective-permute-start.20
  150.4 0.8 collective-permute-done.20
  151.2 0.1 broadcast_in_dim.77
  151.4 23.8 %all_to_all.15 = f32[128,1,512]{2,1,0:T(1,128)S(1)} all-to-all(f32[128,1,512]{2,1,0:T(1,128)S(1)} %broadcast_in_dim.77), channel_id=1, replica_groups=mesh['x'=4,'yl'=2,'yh'=2,'z'=8,'c'=2] {'x','yl','yh','z'}, dimensions={0} | all-to-all | bytes 524288 | tf_op jit(solution)/shard_map/all_to_all | solution.py:183
  175.2 0.2 reduce_max.21
  175.4 0.6 add_divide_fusion.2
  (248 shorter events, 3.2 us)
Async XLA Ops:
  2.4 9.7 %copy-start.5 = (f32[16]{0:T(128)S(1)}, f32[16]{0:T(128)}, u32[]{:S(2)}) copy-start(f32[16]{0:T(128)} %get-tuple-element.1079) | copy-start | bytes 196 | tf_op jit(solution)/shard_map/while
  2.4 9.7 %copy-start.6 = (f32[16]{0:T(128)S(1)}, f32[16]{0:T(128)}, u32[]{:S(2)}) copy-start(f32[16]{0:T(128)} %get-tuple-element.1077) | copy-start | bytes 196 | tf_op jit(solution)/shard_map/while
  2.4 9.7 %copy-start.7 = (s32[1,1,128]{2,1,0:T(1,128)S(1)}, s32[1,1,128]{2,1,0:T(1,128)}, u32[]{:S(2)}) copy-start(s32[1,1,128]{2,1,0:T(1,128)} %get-tuple-element.1078) | copy-start | bytes 1540 | tf_op jit(solution)/shard_map/while
  2.6 9.5 %collective-permute-start.13 = (bf16[136,512]{1,0:T(8,128)(2,1)S(1)}, bf16[136,512]{1,0:T(8,128)(2,1)S(1)}, u32[]{:S(2)}, u32[]{:S(2)}) collective-permute-start(bf16[136,512]{1,0:T(8,128)(2,1)S(1)} %pad_maximum_fusion.10), channel_id=1, source_target_pairs={{0,14},{2,0},{4,2},{6,4},{8,6},{10,8},{12,10},{14,12},{1,15},{3,1}... | collective-permute-start | bytes 417800 | tf_op jit(solution)/shard_map/while/body/ppermute | solution.py:55
  9.1 5.8 %collective-permute-start.10 = (bf16[136,512]{1,0:T(8,128)(2,1)S(1)}, bf16[136,512]{1,0:T(8,128)(2,1)S(1)}, u32[]{:S(2)}, u32[]{:S(2)}) collective-permute-start(bf16[136,512]{1,0:T(8,128)(2,1)S(1)} %pad_maximum_fusion.10), channel_id=1, source_target_pairs={{0,2},{2,4},{4,6},{6,8},{8,10},{10,12},{12,14},{14,0},{1,3},{3,5},... | collective-permute-start | bytes 417800 | tf_op jit(solution)/shard_map/while/body/ppermute | solution.py:55
  9.1 5.9 %collective-permute-start = (bf16[136,512]{1,0:T(8,128)(2,1)S(1)}, bf16[136,512]{1,0:T(8,128)(2,1)S(1)}, u32[]{:S(2)}, u32[]{:S(2)}) collective-permute-start(bf16[136,512]{1,0:T(8,128)(2,1)S(1)} %pad_maximum_fusion.10), channel_id=1, source_target_pairs={{0,16},{16,0},{1,17},{17,1},{2,18},{18,2},{3,19},{19,3},{4,20},{20... | collective-permute-start | bytes 417800 | tf_op jit(solution)/shard_map/while/body/ppermute | solution.py:50
  12.1 6.0 %collective-permute-start.14 = (bf16[136,512]{1,0:T(8,128)(2,1)S(1)}, bf16[136,512]{1,0:T(8,128)(2,1)S(1)}, u32[]{:S(2)}, u32[]{:S(2)}) collective-permute-start(bf16[136,512]{1,0:T(8,128)(2,1)S(1)} %collective-permute-done.13), channel_id=1, source_target_pairs={{0,14},{2,0},{4,2},{6,4},{8,6},{10,8},{12,10},{14,12},{1,15},{3,1}... | collective-permute-start | bytes 417800 | tf_op jit(solution)/shard_map/while/body/ppermute | solution.py:55
  14.9 5.2 %collective-permute-start.11 = (bf16[136,512]{1,0:T(8,128)(2,1)S(1)}, bf16[136,512]{1,0:T(8,128)(2,1)S(1)}, u32[]{:S(2)}, u32[]{:S(2)}) collective-permute-start(bf16[136,512]{1,0:T(8,128)(2,1)S(1)} %collective-permute-done.10), channel_id=1, source_target_pairs={{0,2},{2,4},{4,6},{6,8},{8,10},{10,12},{12,14},{14,0},{1,3},{3,5},... | collective-permute-start | bytes 417800 | tf_op jit(solution)/shard_map/while/body/ppermute | solution.py:55
  15.0 7.6 %collective-permute-start.6 = (bf16[136,512]{1,0:T(8,128)(2,1)S(1)}, bf16[136,512]{1,0:T(8,128)(2,1)S(1)}, u32[]{:S(2)}, u32[]{:S(2)}) collective-permute-start(bf16[136,512]{1,0:T(8,128)(2,1)S(1)} %collective-permute-done), channel_id=1, source_target_pairs={{0,2},{2,4},{4,6},{6,8},{8,10},{10,12},{12,14},{14,0},{1,3},{3,5},... | collective-permute-start | bytes 417800 | tf_op jit(solution)/shard_map/while/body/ppermute | solution.py:55
  15.1 7.5 %collective-permute-start.1 = (bf16[136,512]{1,0:T(8,128)(2,1)S(1)}, bf16[136,512]{1,0:T(8,128)(2,1)S(1)}, u32[]{:S(2)}, u32[]{:S(2)}) collective-permute-start(bf16[136,512]{1,0:T(8,128)(2,1)S(1)} %collective-permute-done), channel_id=1, source_target_pairs={{0,14},{2,0},{4,2},{6,4},{8,6},{10,8},{12,10},{14,12},{1,15},{3,1}... | collective-permute-start | bytes 417800 | tf_op jit(solution)/shard_map/while/body/ppermute | solution.py:55
  18.1 9.6 %collective-permute-start.15 = (bf16[136,512]{1,0:T(8,128)(2,1)S(1)}, bf16[136,512]{1,0:T(8,128)(2,1)S(1)}, u32[]{:S(2)}, u32[]{:S(2)}) collective-permute-start(bf16[136,512]{1,0:T(8,128)(2,1)S(1)} %collective-permute-done.14), channel_id=1, source_target_pairs={{0,14},{2,0},{4,2},{6,4},{8,6},{10,8},{12,10},{14,12},{1,15},{3,1}... | collective-permute-start | bytes 417800 | tf_op jit(solution)/shard_map/while/body/ppermute | solution.py:55
  20.1 6.0 %collective-permute-start.12 = (bf16[136,512]{1,0:T(8,128)(2,1)S(1)}, bf16[136,512]{1,0:T(8,128)(2,1)S(1)}, u32[]{:S(2)}, u32[]{:S(2)}) collective-permute-start(bf16[136,512]{1,0:T(8,128)(2,1)S(1)} %collective-permute-done.11), channel_id=1, source_target_pairs={{0,2},{2,4},{4,6},{6,8},{8,10},{10,12},{12,14},{14,0},{1,3},{3,5},... | collective-permute-start | bytes 417800 | tf_op jit(solution)/shard_map/while/body/ppermute | solution.py:55
  22.6 5.1 %collective-permute-start.7 = (bf16[136,512]{1,0:T(8,128)(2,1)S(1)}, bf16[136,512]{1,0:T(8,128)(2,1)S(1)}, u32[]{:S(2)}, u32[]{:S(2)}) collective-permute-start(bf16[136,512]{1,0:T(8,128)(2,1)S(1)} %collective-permute-done.6), channel_id=1, source_target_pairs={{0,2},{2,4},{4,6},{6,8},{8,10},{10,12},{12,14},{14,0},{1,3},{3,5},... | collective-permute-start | bytes 417800 | tf_op jit(solution)/shard_map/while/body/ppermute | solution.py:55
  22.6 5.1 %collective-permute-start.2 = (bf16[136,512]{1,0:T(8,128)(2,1)S(1)}, bf16[136,512]{1,0:T(8,128)(2,1)S(1)}, u32[]{:S(2)}, u32[]{:S(2)}) collective-permute-start(bf16[136,512]{1,0:T(8,128)(2,1)S(1)} %collective-permute-done.1), channel_id=1, source_target_pairs={{0,14},{2,0},{4,2},{6,4},{8,6},{10,8},{12,10},{14,12},{1,15},{3,1}... | collective-permute-start | bytes 417800 | tf_op jit(solution)/shard_map/while/body/ppermute | solution.py:55
  26.1 14.2 %collective-permute-start.17 = (bf16[136,512]{1,0:T(8,128)(2,1)S(1)}, bf16[136,512]{1,0:T(8,128)(2,1)S(1)}, u32[]{:S(2)}, u32[]{:S(2)}) collective-permute-start(bf16[136,512]{1,0:T(8,128)(2,1)S(1)} %collective-permute-done.12), channel_id=1, source_target_pairs={{0,2},{2,4},{4,6},{6,8},{8,10},{10,12},{12,14},{14,0},{1,3},{3,5},... | collective-permute-start | bytes 417800 | tf_op jit(solution)/shard_map/while/body/ppermute | solution.py:55
  27.7 6.8 %collective-permute-start.8 = (bf16[136,512]{1,0:T(8,128)(2,1)S(1)}, bf16[136,512]{1,0:T(8,128)(2,1)S(1)}, u32[]{:S(2)}, u32[]{:S(2)}) collective-permute-start(bf16[136,512]{1,0:T(8,128)(2,1)S(1)} %collective-permute-done.7), channel_id=1, source_target_pairs={{0,2},{2,4},{4,6},{6,8},{8,10},{10,12},{12,14},{14,0},{1,3},{3,5},... | collective-permute-start | bytes 417800 | tf_op jit(solution)/shard_map/while/body/ppermute | solution.py:55
  27.7 6.7 %collective-permute-start.3 = (bf16[136,512]{1,0:T(8,128)(2,1)S(1)}, bf16[136,512]{1,0:T(8,128)(2,1)S(1)}, u32[]{:S(2)}, u32[]{:S(2)}) collective-permute-start(bf16[136,512]{1,0:T(8,128)(2,1)S(1)} %collective-permute-done.2), channel_id=1, source_target_pairs={{0,14},{2,0},{4,2},{6,4},{8,6},{10,8},{12,10},{14,12},{1,15},{3,1}... | collective-permute-start | bytes 417800 | tf_op jit(solution)/shard_map/while/body/ppermute | solution.py:55
  30.5 19.1 %copy-start.9 = (bf16[1024,4096]{1,0:T(8,128)(2,1)S(1)}, bf16[1024,4096]{1,0:T(8,128)(2,1)}, u32[]{:S(2)}) copy-start(bf16[1024,4096]{1,0:T(8,128)(2,1)} %get-tuple-element.1227) | copy-start | bytes 25165828 | tf_op jit(solution)/shard_map/while
  34.5 14.8 %collective-permute-start.9 = (bf16[272,512]{1,0:T(8,128)(2,1)S(1)}, bf16[272,512]{1,0:T(8,128)(2,1)S(1)}, u32[]{:S(2)}, u32[]{:S(2)}) collective-permute-start(bf16[272,512]{1,0:T(8,128)(2,1)S(1)} %pad_maximum_fusion.11), channel_id=1, source_target_pairs={{0,1},{1,0},{2,3},{3,2},{4,5},{5,4},{6,7},{7,6},{8,9},{9,8},{10,11... | collective-permute-start | bytes 835592 | tf_op jit(solution)/shard_map/while/body/ppermute | solution.py:46
  40.3 9.0 %collective-permute-start.18 = (bf16[408,512]{1,0:T(8,128)(2,1)S(1)}, bf16[408,512]{1,0:T(8,128)(2,1)S(1)}, u32[]{:S(2)}, u32[]{:S(2)}) collective-permute-start(bf16[408,512]{1,0:T(8,128)(2,1)S(1)} %pad_maximum_fusion.12), channel_id=1, source_target_pairs={{0,1},{1,0},{2,3},{3,2},{4,5},{5,4},{6,7},{7,6},{8,9},{9,8},{10,11... | collective-permute-start | bytes 1253384 | tf_op jit(solution)/shard_map/while/body/ppermute | solution.py:46
  40.5 8.9 %collective-permute-start.19 = (bf16[680,512]{1,0:T(8,128)(2,1)S(1)}, bf16[680,512]{1,0:T(8,128)(2,1)S(1)}, u32[]{:S(2)}, u32[]{:S(2)}) collective-permute-start(bf16[680,512]{1,0:T(8,128)(2,1)S(1)} %constant_dynamic-update-slice_fusion.32), channel_id=1, source_target_pairs={{0,1},{1,0},{2,3},{3,2},{4,5},{5,4},{6,7},{7,6},{8,9},{9,8},{10,11... | collective-permute-start | bytes 2088968 | tf_op jit(solution)/shard_map/while/body/ppermute | solution.py:46
  41.1 10.8 %collective-permute-start.16 = (bf16[680,512]{1,0:T(8,128)(2,1)S(1)}, bf16[680,512]{1,0:T(8,128)(2,1)S(1)}, u32[]{:S(2)}, u32[]{:S(2)}) collective-permute-start(bf16[680,512]{1,0:T(8,128)(2,1)S(1)} %constant_dynamic-update-slice_fusion.27), channel_id=1, source_target_pairs={{0,1},{1,0},{2,3},{3,2},{4,5},{5,4},{6,7},{7,6},{8,9},{9,8},{10,11... | collective-permute-start | bytes 2088968 | tf_op jit(solution)/shard_map/while/body/ppermute | solution.py:46
  41.3 5.7 %collective-permute-start.4 = (bf16[136,512]{1,0:T(8,128)(2,1)S(1)}, bf16[136,512]{1,0:T(8,128)(2,1)S(1)}, u32[]{:S(2)}, u32[]{:S(2)}) collective-permute-start(bf16[136,512]{1,0:T(8,128)(2,1)S(1)} %collective-permute-done.3), channel_id=1, source_target_pairs={{0,14},{2,0},{4,2},{6,4},{8,6},{10,8},{12,10},{14,12},{1,15},{3,1}... | collective-permute-start | bytes 417800 | tf_op jit(solution)/shard_map/while/body/ppermute | solution.py:55
  47.0 2.3 %collective-permute-start.5 = (bf16[136,512]{1,0:T(8,128)(2,1)S(1)}, bf16[136,512]{1,0:T(8,128)(2,1)S(1)}, u32[]{:S(2)}, u32[]{:S(2)}) collective-permute-start(bf16[136,512]{1,0:T(8,128)(2,1)S(1)} %collective-permute-done.4), channel_id=1, source_target_pairs={{0,1},{1,0},{2,3},{3,2},{4,5},{5,4},{6,7},{7,6},{8,9},{9,8},{10,11... | collective-permute-start | bytes 417800 | tf_op jit(solution)/shard_map/while/body/ppermute | solution.py:46
  54.7 20.7 %copy-start.10 = (s32[1,1,128]{2,1,0:T(1,128)S(1)}, s32[1,1,128]{2,1,0:T(1,128)}, u32[]{:S(2)}) copy-start(s32[1,1,128]{2,1,0:T(1,128)} %get-tuple-element.1084) | copy-start | bytes 1540 | tf_op jit(solution)/shard_map/while
  54.7 20.8 %copy-start.8 = (f32[1,1,128]{2,1,0:T(1,128)S(1)}, f32[1,1,128]{2,1,0:T(1,128)}, u32[]{:S(2)}) copy-start(f32[1,1,128]{2,1,0:T(1,128)} %get-tuple-element.1082) | copy-start | bytes 1540 | tf_op jit(solution)/shard_map/while
  54.7 20.8 %copy-start.4 = (f32[512]{0:T(512)S(1)}, f32[512]{0:T(512)}, u32[]{:S(2)}) copy-start(f32[512]{0:T(512)} %get-tuple-element.1261) | copy-start | bytes 6148 | tf_op jit(solution)/shard_map/while
  54.7 20.8 %copy-start.3 = (f32[1,1,128,512]{3,2,1,0:T(8,128)S(1)}, f32[1,1,128,512]{3,2,1,0:T(8,128)}, u32[]{:S(2)}) copy-start(f32[1,1,128,512]{3,2,1,0:T(8,128)} %get-tuple-element.1101) | copy-start | bytes 786436 | tf_op jit(solution)/shard_map/while
  54.7 20.8 %copy-start.11 = (f32[1,1,128]{2,1,0:T(1,128)S(1)}, f32[1,1,128]{2,1,0:T(1,128)}, u32[]{:S(2)}) copy-start(f32[1,1,128]{2,1,0:T(1,128)} %get-tuple-element.1083) | copy-start | bytes 1540 | tf_op jit(solution)/shard_map/while
  76.5 0.7 copy-start.1
  77.2 6.4 %copy-start.5 = (f32[16]{0:T(128)S(1)}, f32[16]{0:T(128)}, u32[]{:S(2)}) copy-start(f32[16]{0:T(128)} %get-tuple-element.1079) | copy-start | bytes 196 | tf_op jit(solution)/shard_map/while
  77.2 6.4 %copy-start.6 = (f32[16]{0:T(128)S(1)}, f32[16]{0:T(128)}, u32[]{:S(2)}) copy-start(f32[16]{0:T(128)} %get-tuple-element.1077) | copy-start | bytes 196 | tf_op jit(solution)/shard_map/while
  77.2 6.4 %copy-start.7 = (s32[1,1,128]{2,1,0:T(1,128)S(1)}, s32[1,1,128]{2,1,0:T(1,128)}, u32[]{:S(2)}) copy-start(s32[1,1,128]{2,1,0:T(1,128)} %get-tuple-element.1078) | copy-start | bytes 1540 | tf_op jit(solution)/shard_map/while
  77.5 6.2 %collective-permute-start.13 = (bf16[136,512]{1,0:T(8,128)(2,1)S(1)}, bf16[136,512]{1,0:T(8,128)(2,1)S(1)}, u32[]{:S(2)}, u32[]{:S(2)}) collective-permute-start(bf16[136,512]{1,0:T(8,128)(2,1)S(1)} %pad_maximum_fusion.10), channel_id=1, source_target_pairs={{0,14},{2,0},{4,2},{6,4},{8,6},{10,8},{12,10},{14,12},{1,15},{3,1}... | collective-permute-start | bytes 417800 | tf_op jit(solution)/shard_map/while/body/ppermute | solution.py:55
  81.0 5.5 %collective-permute-start.10 = (bf16[136,512]{1,0:T(8,128)(2,1)S(1)}, bf16[136,512]{1,0:T(8,128)(2,1)S(1)}, u32[]{:S(2)}, u32[]{:S(2)}) collective-permute-start(bf16[136,512]{1,0:T(8,128)(2,1)S(1)} %pad_maximum_fusion.10), channel_id=1, source_target_pairs={{0,2},{2,4},{4,6},{6,8},{8,10},{10,12},{12,14},{14,0},{1,3},{3,5},... | collective-permute-start | bytes 417800 | tf_op jit(solution)/shard_map/while/body/ppermute | solution.py:55
  81.0 5.6 %collective-permute-start = (bf16[136,512]{1,0:T(8,128)(2,1)S(1)}, bf16[136,512]{1,0:T(8,128)(2,1)S(1)}, u32[]{:S(2)}, u32[]{:S(2)}) collective-permute-start(bf16[136,512]{1,0:T(8,128)(2,1)S(1)} %pad_maximum_fusion.10), channel_id=1, source_target_pairs={{0,16},{16,0},{1,17},{17,1},{2,18},{18,2},{3,19},{19,3},{4,20},{20... | collective-permute-start | bytes 417800 | tf_op jit(solution)/shard_map/while/body/ppermute | solution.py:50
  83.7 6.0 %collective-permute-start.14 = (bf16[136,512]{1,0:T(8,128)(2,1)S(1)}, bf16[136,512]{1,0:T(8,128)(2,1)S(1)}, u32[]{:S(2)}, u32[]{:S(2)}) collective-permute-start(bf16[136,512]{1,0:T(8,128)(2,1)S(1)} %collective-permute-done.13), channel_id=1, source_target_pairs={{0,14},{2,0},{4,2},{6,4},{8,6},{10,8},{12,10},{14,12},{1,15},{3,1}... | collective-permute-start | bytes 417800 | tf_op jit(solution)/shard_map/while/body/ppermute | solution.py:55
  86.5 5.4 %collective-permute-start.11 = (bf16[136,512]{1,0:T(8,128)(2,1)S(1)}, bf16[136,512]{1,0:T(8,128)(2,1)S(1)}, u32[]{:S(2)}, u32[]{:S(2)}) collective-permute-start(bf16[136,512]{1,0:T(8,128)(2,1)S(1)} %collective-permute-done.10), channel_id=1, source_target_pairs={{0,2},{2,4},{4,6},{6,8},{8,10},{10,12},{12,14},{14,0},{1,3},{3,5},... | collective-permute-start | bytes 417800 | tf_op jit(solution)/shard_map/while/body/ppermute | solution.py:55
  86.6 6.6 %collective-permute-start.6 = (bf16[136,512]{1,0:T(8,128)(2,1)S(1)}, bf16[136,512]{1,0:T(8,128)(2,1)S(1)}, u32[]{:S(2)}, u32[]{:S(2)}) collective-permute-start(bf16[136,512]{1,0:T(8,128)(2,1)S(1)} %collective-permute-done), channel_id=1, source_target_pairs={{0,2},{2,4},{4,6},{6,8},{8,10},{10,12},{12,14},{14,0},{1,3},{3,5},... | collective-permute-start | bytes 417800 | tf_op jit(solution)/shard_map/while/body/ppermute | solution.py:55
  86.7 6.5 %collective-permute-start.1 = (bf16[136,512]{1,0:T(8,128)(2,1)S(1)}, bf16[136,512]{1,0:T(8,128)(2,1)S(1)}, u32[]{:S(2)}, u32[]{:S(2)}) collective-permute-start(bf16[136,512]{1,0:T(8,128)(2,1)S(1)} %collective-permute-done), channel_id=1, source_target_pairs={{0,14},{2,0},{4,2},{6,4},{8,6},{10,8},{12,10},{14,12},{1,15},{3,1}... | collective-permute-start | bytes 417800 | tf_op jit(solution)/shard_map/while/body/ppermute | solution.py:55
  89.7 9.9 %collective-permute-start.15 = (bf16[136,512]{1,0:T(8,128)(2,1)S(1)}, bf16[136,512]{1,0:T(8,128)(2,1)S(1)}, u32[]{:S(2)}, u32[]{:S(2)}) collective-permute-start(bf16[136,512]{1,0:T(8,128)(2,1)S(1)} %collective-permute-done.14), channel_id=1, source_target_pairs={{0,14},{2,0},{4,2},{6,4},{8,6},{10,8},{12,10},{14,12},{1,15},{3,1}... | collective-permute-start | bytes 417800 | tf_op jit(solution)/shard_map/while/body/ppermute | solution.py:55
  91.9 6.2 %collective-permute-start.12 = (bf16[136,512]{1,0:T(8,128)(2,1)S(1)}, bf16[136,512]{1,0:T(8,128)(2,1)S(1)}, u32[]{:S(2)}, u32[]{:S(2)}) collective-permute-start(bf16[136,512]{1,0:T(8,128)(2,1)S(1)} %collective-permute-done.11), channel_id=1, source_target_pairs={{0,2},{2,4},{4,6},{6,8},{8,10},{10,12},{12,14},{14,0},{1,3},{3,5},... | collective-permute-start | bytes 417800 | tf_op jit(solution)/shard_map/while/body/ppermute | solution.py:55
  93.1 6.4 %collective-permute-start.7 = (bf16[136,512]{1,0:T(8,128)(2,1)S(1)}, bf16[136,512]{1,0:T(8,128)(2,1)S(1)}, u32[]{:S(2)}, u32[]{:S(2)}) collective-permute-start(bf16[136,512]{1,0:T(8,128)(2,1)S(1)} %collective-permute-done.6), channel_id=1, source_target_pairs={{0,2},{2,4},{4,6},{6,8},{8,10},{10,12},{12,14},{14,0},{1,3},{3,5},... | collective-permute-start | bytes 417800 | tf_op jit(solution)/shard_map/while/body/ppermute | solution.py:55
  93.2 6.4 %collective-permute-start.2 = (bf16[136,512]{1,0:T(8,128)(2,1)S(1)}, bf16[136,512]{1,0:T(8,128)(2,1)S(1)}, u32[]{:S(2)}, u32[]{:S(2)}) collective-permute-start(bf16[136,512]{1,0:T(8,128)(2,1)S(1)} %collective-permute-done.1), channel_id=1, source_target_pairs={{0,14},{2,0},{4,2},{6,4},{8,6},{10,8},{12,10},{14,12},{1,15},{3,1}... | collective-permute-start | bytes 417800 | tf_op jit(solution)/shard_map/while/body/ppermute | solution.py:55
  98.0 16.0 %collective-permute-start.17 = (bf16[136,512]{1,0:T(8,128)(2,1)S(1)}, bf16[136,512]{1,0:T(8,128)(2,1)S(1)}, u32[]{:S(2)}, u32[]{:S(2)}) collective-permute-start(bf16[136,512]{1,0:T(8,128)(2,1)S(1)} %collective-permute-done.12), channel_id=1, source_target_pairs={{0,2},{2,4},{4,6},{6,8},{8,10},{10,12},{12,14},{14,0},{1,3},{3,5},... | collective-permute-start | bytes 417800 | tf_op jit(solution)/shard_map/while/body/ppermute | solution.py:55
  99.5 7.8 %collective-permute-start.8 = (bf16[136,512]{1,0:T(8,128)(2,1)S(1)}, bf16[136,512]{1,0:T(8,128)(2,1)S(1)}, u32[]{:S(2)}, u32[]{:S(2)}) collective-permute-start(bf16[136,512]{1,0:T(8,128)(2,1)S(1)} %collective-permute-done.7), channel_id=1, source_target_pairs={{0,2},{2,4},{4,6},{6,8},{8,10},{10,12},{12,14},{14,0},{1,3},{3,5},... | collective-permute-start | bytes 417800 | tf_op jit(solution)/shard_map/while/body/ppermute | solution.py:55
  99.6 7.7 %collective-permute-start.3 = (bf16[136,512]{1,0:T(8,128)(2,1)S(1)}, bf16[136,512]{1,0:T(8,128)(2,1)S(1)}, u32[]{:S(2)}, u32[]{:S(2)}) collective-permute-start(bf16[136,512]{1,0:T(8,128)(2,1)S(1)} %collective-permute-done.2), channel_id=1, source_target_pairs={{0,14},{2,0},{4,2},{6,4},{8,6},{10,8},{12,10},{14,12},{1,15},{3,1}... | collective-permute-start | bytes 417800 | tf_op jit(solution)/shard_map/while/body/ppermute | solution.py:55
  102.3 21.0 %copy-start.9 = (bf16[1024,4096]{1,0:T(8,128)(2,1)S(1)}, bf16[1024,4096]{1,0:T(8,128)(2,1)}, u32[]{:S(2)}) copy-start(bf16[1024,4096]{1,0:T(8,128)(2,1)} %get-tuple-element.1227) | copy-start | bytes 25165828 | tf_op jit(solution)/shard_map/while
  107.3 15.8 %collective-permute-start.9 = (bf16[272,512]{1,0:T(8,128)(2,1)S(1)}, bf16[272,512]{1,0:T(8,128)(2,1)S(1)}, u32[]{:S(2)}, u32[]{:S(2)}) collective-permute-start(bf16[272,512]{1,0:T(8,128)(2,1)S(1)} %pad_maximum_fusion.11), channel_id=1, source_target_pairs={{0,1},{1,0},{2,3},{3,2},{4,5},{5,4},{6,7},{7,6},{8,9},{9,8},{10,11... | collective-permute-start | bytes 835592 | tf_op jit(solution)/shard_map/while/body/ppermute | solution.py:46
  114.1 9.0 %collective-permute-start.18 = (bf16[408,512]{1,0:T(8,128)(2,1)S(1)}, bf16[408,512]{1,0:T(8,128)(2,1)S(1)}, u32[]{:S(2)}, u32[]{:S(2)}) collective-permute-start(bf16[408,512]{1,0:T(8,128)(2,1)S(1)} %pad_maximum_fusion.12), channel_id=1, source_target_pairs={{0,1},{1,0},{2,3},{3,2},{4,5},{5,4},{6,7},{7,6},{8,9},{9,8},{10,11... | collective-permute-start | bytes 1253384 | tf_op jit(solution)/shard_map/while/body/ppermute | solution.py:46
  114.3 8.9 %collective-permute-start.19 = (bf16[680,512]{1,0:T(8,128)(2,1)S(1)}, bf16[680,512]{1,0:T(8,128)(2,1)S(1)}, u32[]{:S(2)}, u32[]{:S(2)}) collective-permute-start(bf16[680,512]{1,0:T(8,128)(2,1)S(1)} %constant_dynamic-update-slice_fusion.32), channel_id=1, source_target_pairs={{0,1},{1,0},{2,3},{3,2},{4,5},{5,4},{6,7},{7,6},{8,9},{9,8},{10,11... | collective-permute-start | bytes 2088968 | tf_op jit(solution)/shard_map/while/body/ppermute | solution.py:46
  114.9 10.8 %collective-permute-start.16 = (bf16[680,512]{1,0:T(8,128)(2,1)S(1)}, bf16[680,512]{1,0:T(8,128)(2,1)S(1)}, u32[]{:S(2)}, u32[]{:S(2)}) collective-permute-start(bf16[680,512]{1,0:T(8,128)(2,1)S(1)} %constant_dynamic-update-slice_fusion.27), channel_id=1, source_target_pairs={{0,1},{1,0},{2,3},{3,2},{4,5},{5,4},{6,7},{7,6},{8,9},{9,8},{10,11... | collective-permute-start | bytes 2088968 | tf_op jit(solution)/shard_map/while/body/ppermute | solution.py:46
  115.1 5.7 %collective-permute-start.4 = (bf16[136,512]{1,0:T(8,128)(2,1)S(1)}, bf16[136,512]{1,0:T(8,128)(2,1)S(1)}, u32[]{:S(2)}, u32[]{:S(2)}) collective-permute-start(bf16[136,512]{1,0:T(8,128)(2,1)S(1)} %collective-permute-done.3), channel_id=1, source_target_pairs={{0,14},{2,0},{4,2},{6,4},{8,6},{10,8},{12,10},{14,12},{1,15},{3,1}... | collective-permute-start | bytes 417800 | tf_op jit(solution)/shard_map/while/body/ppermute | solution.py:55
  120.7 2.3 %collective-permute-start.5 = (bf16[136,512]{1,0:T(8,128)(2,1)S(1)}, bf16[136,512]{1,0:T(8,128)(2,1)S(1)}, u32[]{:S(2)}, u32[]{:S(2)}) collective-permute-start(bf16[136,512]{1,0:T(8,128)(2,1)S(1)} %collective-permute-done.4), channel_id=1, source_target_pairs={{0,1},{1,0},{2,3},{3,2},{4,5},{5,4},{6,7},{7,6},{8,9},{9,8},{10,11... | collective-permute-start | bytes 417800 | tf_op jit(solution)/shard_map/while/body/ppermute | solution.py:46
  128.4 18.5 %copy-start.10 = (s32[1,1,128]{2,1,0:T(1,128)S(1)}, s32[1,1,128]{2,1,0:T(1,128)}, u32[]{:S(2)}) copy-start(s32[1,1,128]{2,1,0:T(1,128)} %get-tuple-element.1084) | copy-start | bytes 1540 | tf_op jit(solution)/shard_map/while
  128.5 18.5 %copy-start.8 = (f32[1,1,128]{2,1,0:T(1,128)S(1)}, f32[1,1,128]{2,1,0:T(1,128)}, u32[]{:S(2)}) copy-start(f32[1,1,128]{2,1,0:T(1,128)} %get-tuple-element.1082) | copy-start | bytes 1540 | tf_op jit(solution)/shard_map/while
  128.5 18.6 %copy-start.4 = (f32[512]{0:T(512)S(1)}, f32[512]{0:T(512)}, u32[]{:S(2)}) copy-start(f32[512]{0:T(512)} %get-tuple-element.1261) | copy-start | bytes 6148 | tf_op jit(solution)/shard_map/while
  128.5 18.6 %copy-start.3 = (f32[1,1,128,512]{3,2,1,0:T(8,128)S(1)}, f32[1,1,128,512]{3,2,1,0:T(8,128)}, u32[]{:S(2)}) copy-start(f32[1,1,128,512]{3,2,1,0:T(8,128)} %get-tuple-element.1101) | copy-start | bytes 786436 | tf_op jit(solution)/shard_map/while
  128.5 18.6 %copy-start.11 = (f32[1,1,128]{2,1,0:T(1,128)S(1)}, f32[1,1,128]{2,1,0:T(1,128)}, u32[]{:S(2)}) copy-start(f32[1,1,128]{2,1,0:T(1,128)} %get-tuple-element.1083) | copy-start | bytes 1540 | tf_op jit(solution)/shard_map/while
  148.1 0.7 copy-start.1
  148.8 27.2 %copy-start = (f32[128,512]{1,0:T(8,128)}, f32[128,512]{1,0:T(8,128)S(1)}, u32[]{:S(2)}) copy-start(f32[128,512]{1,0:T(8,128)S(1)} %get-tuple-element.572) | copy-start | bytes 786436
  148.8 27.2 %copy-start.2 = (f32[128,512]{1,0:T(8,128)}, f32[128,512]{1,0:T(8,128)S(1)}, u32[]{:S(2)}) copy-start(f32[128,512]{1,0:T(8,128)S(1)} %get-tuple-element.573) | copy-start | bytes 786436
  148.8 2.4 %collective-permute-start.20 = (f32[512]{0:T(512)S(1)}, f32[512]{0:T(512)S(1)}, u32[]{:S(2)}, u32[]{:S(2)}) collective-permute-start(f32[512]{0:T(512)S(1)} %get-tuple-element.574), channel_id=1, source_target_pairs={{0,1},{1,0},{2,3},{3,2},{4,5},{5,4},{6,7},{7,6},{8,9},{9,8},{10,11... | collective-permute-start | bytes 6152 | tf_op jit(solution)/shard_map/ppermute | solution.py:46

commit v3 on v2

--- a/solution.py
+++ b/solution.py
@@ -102,29 +102,38 @@
         held, _ = lax.optimization_barrier(([block for _, block in blocks], token))
         return [(shift, block) for (shift, _), block in zip(blocks, held)]
 
-    def joined(rows):
-        return rows[0].astype(jnp.float32) + rows[1].astype(jnp.float32)
-
     def gathered(block):
-        found = [joined(block[elements:])]
-
-        def marked(block, by):
+        slips = [
+            jnp.zeros((half, members), jnp.bfloat16),
+            jnp.zeros((half // elements, elements, members), jnp.bfloat16),
+        ]
+
+        def place(side, owner_core, shift, block):
+            owner = 2 * lax.rem(here + shift + depth, depth) + owner_core
+            if side == 0:
+                slips[0] = lax.dynamic_update_slice(slips[0], block, (owner * elements, 0))
+            else:
+                slips[1] = lax.dynamic_update_slice(slips[1], block[None], (owner, 0, 0))
+
+        def hopped(side, shift, block, by):
             block = shifted(block, by)
-            found.append(joined(block[elements:]))
+            place(side, core, shift, block)
             return block
 
         far = swap_far(block)
-        found.append(joined(far[elements:]))
         start = [[(0, block)], [(0, far)]]
+        place(0, core, 0, block)
+        place(1, core, 0, far)
         up, down = [block, far], [block, far]
         hops = [[], []]
         for hop in (1, 2, 3):
+            up[0] = hopped(0, -hop, up[0], 1)
+            down[0] = hopped(0, hop, down[0], -1)
+            down[1] = hopped(1, hop, down[1], -1)
+            up[1] = hopped(1, -hop, up[1], 1)
             for side in (0, 1):
-                up[side] = marked(up[side], 1)
-                down[side] = marked(down[side], -1)
                 hops[side].append([(-hop, up[side]), (hop, down[side])])
-        last = [[(4, marked(up[0], 1))], [(4, marked(down[1], -1))]]
-        mine = [start[side] + sum(hops[side], []) + last[side] for side in (0, 1)]
+        last = [[(4, hopped(0, 4, up[0], 1))], [(4, hopped(1, 4, down[1], -1))]]
         token = (up[0], down[0], up[1], down[1])
         other = [
             swapped(after(start[side] + hops[side][0] + hops[side][1], token))
@@ -132,27 +141,15 @@
         ]
         other[0] += swapped(hops[0][2] + last[0])
         other[1] += swapped(hops[1][2]) + swapped(last[1])
-        found += [joined(block[elements:]) for side in other for _, block in side]
-        return mine, other, found
-
-    def placed(mine, other, blank):
-        slips = blank
-        for owner_core, blocks in ((core, mine), (1 - core, other)):
-            for shift, block in blocks:
-                owner = 2 * lax.rem(here + shift + depth, depth) + owner_core
-                block = block[:elements].reshape(-1, *blank.shape[1:])
-                start = (owner * block.shape[0], *(0 for _ in blank.shape[1:]))
-                slips = lax.dynamic_update_slice(slips, block, start)
-        return slips.reshape(half, members)
-
-    def partial_of(mine, other, side):
-        near_blank = jnp.zeros((half, members), jnp.bfloat16)
-        far_blank = jnp.zeros((half // elements, elements, members), jnp.bfloat16)
-        slips = placed(mine[0], other[0], near_blank)
-        partial = jnp.dot(tile_of(side), slips, preferred_element_type=jnp.float32)
+        for side in (0, 1):
+            for shift, block in other[side]:
+                place(side, 1 - core, shift, block)
+        return slips[0], slips[1].reshape(half, members)
+
+    def partial_of(slips, side):
+        partial = jnp.dot(tile_of(side), slips[0], preferred_element_type=jnp.float32)
         partial = lax.optimization_barrier(partial)
-        slips = placed(mine[1], other[1], far_blank)
-        partial += jnp.dot(tile_of(1 - side), slips, preferred_element_type=jnp.float32)
+        partial += jnp.dot(tile_of(1 - side), slips[1], preferred_element_type=jnp.float32)
         return partial.astype(jnp.bfloat16).reshape(-1, elements, members)
 
     def summed(parts):
@@ -166,51 +163,39 @@
         stress = loading + traction
         return solve_rate(stress, pressure, rate_coef, state_coef, state, creeping == 1)
 
-    spare = 8
-
-    def split_rows(largest):
-        high = largest.astype(jnp.bfloat16)
-        rest = largest - high.astype(jnp.float32)
-        low = rest.astype(jnp.bfloat16)
-        return jnp.concatenate(
-            [high[None], low[None], jnp.zeros((spare - 2, members), jnp.bfloat16)]
-        )
-
     def largest_of(local):
+        local = local.astype(jnp.bfloat16)
         local = jnp.maximum(local, swap_cores(local))
         chips = functools.reduce(lambda n, axis: n * lax.axis_size(axis), CHIPS, 1)
-        everyone = jnp.broadcast_to(local, (chips, members))
-        return jnp.max(lax.all_to_all(everyone, CHIPS, 0, 0, tiled=True), axis=0)
+        everyone = jnp.broadcast_to(local, (chips, *local.shape))
+        everyone = lax.all_to_all(everyone, CHIPS, 0, 0, tiled=True)
+        return jnp.max(everyone, axis=0).astype(jnp.float32)
 
     def step(carry):
-        index, deficit, state, _, local = carry
-        block = jnp.concatenate([deficit.astype(jnp.bfloat16), split_rows(local)])
-        mine, other, found = gathered(block)
+        index, deficit, state, velocity, _, local = carry
+        step_now = jnp.where(index == 0, 0.0, step_size)
+        _, deficit = advance(state, deficit, velocity, step_now)
+        slips = gathered(deficit.astype(jnp.bfloat16))
         side, held, _ = lax.optimization_barrier((near, fault, index))
         coefs = coefs_of(held)
-        parts = partial_of(mine, other, side)
-        rows = split_rows(functools.reduce(jnp.maximum, found))
-        rows = jnp.broadcast_to(rows, (parts.shape[0], *rows.shape))
-        parts = jnp.concatenate([parts, rows], axis=1)
-        held = (coefs, deficit, state, state_variable, index)
+        parts = partial_of(slips, side)
+        held = (coefs, deficit, state, state_variable, velocity, local, index)
         parts, held = lax.optimization_barrier((parts, held))
         parts, held = lax.optimization_barrier((exchanged(parts), held))
-        coefs, deficit, state, begin, index = held
+        coefs, deficit, state, begin, velocity, local, index = held
+        state, _ = advance(state, deficit, velocity, step_size)
         state = jnp.where(index == 0, begin.reshape(elements, members), state)
-        velocity = solved(summed(parts[:, :elements]), state, coefs)
-        local = jnp.max(jnp.abs(velocity), axis=0)
-        found = [joined(parts[row, elements:]) for row in range(parts.shape[0])]
-        largest = functools.reduce(jnp.maximum, found)
-        step_now = jnp.where(index == 0, step_size, STEP_CAP / (1.0 + largest))
-        state, deficit = advance(state, deficit, velocity, step_now)
-        return index + 1, deficit, state, velocity, local
-
-    blank = jnp.zeros((elements, members), jnp.float32)
+        velocity = solved(summed(parts), state, coefs)
+        return index + 1, deficit, state, velocity, local, jnp.max(jnp.abs(velocity), axis=0)
+
+    blank = jnp.zeros((members,), jnp.float32)
     deficit = slip_deficit.reshape(elements, members)
-    carry = (jnp.int32(0), deficit, blank, blank, jnp.zeros((members,), jnp.float32))
+    carry = (jnp.int32(0), deficit, jnp.ones_like(deficit), jnp.zeros_like(deficit), blank, blank)
     carry = lax.while_loop(lambda carry: carry[0] < STEPS, step, carry)
-    _, deficit, state, velocity, local = carry
-    step_next = STEP_CAP / (1.0 + largest_of(local))
+    _, deficit, state, velocity, local_first, local_second = carry
+    largest = largest_of(jnp.stack([local_first, local_second]))
+    state, deficit = advance(state, deficit, velocity, STEP_CAP / (1.0 + largest[0]))
+    step_next = STEP_CAP / (1.0 + largest[1])
     shape = slip_deficit.shape
     return (velocity.reshape(shape), deficit.reshape(shape), state.reshape(shape), step_next)
 

time: 176 us -> 174 us (0.989)
  starting transfers between devices: 66.7 us -> 62.5 us
    ppermute x11, starting transfers between devices: 18.3 us -> 13.1 us  [swap_cores(): return lax.ppermute(x, 'c', ((0, 1), (1, 0)))]
    all_to_all x1, blocking collectives: 23.8 us -> 26 us  [largest_of(): everyone = lax.all_to_all(everyone, CHIPS, 0, 0, tiled=True)]
    ppermute x11, waiting for transfers between devices: 2.78 us -> 0.85 us  [swap_cores(): return lax.ppermute(x, 'c', ((0, 1), (1, 0)))]
  transfers between devices with their start and end apart: 41 -> 41, of which waited for: 14 -> 10; matrix products, arithmetic and copies ran while one was open for 4% -> 4% of each run, Pallas kernels for 0% -> 0%
where the time goes in v3:
time: 174 us
  blocking collectives  64 us (37%)
  starting transfers between devices  62.5 us (36%)
  waiting for transfers between devices  24.8 us (14%)
  matrix products  9.32 us (5%)
  local copies, waits for them, and re-layouts  5.52 us (3%)
  other arithmetic  5.46 us (3%)
    ppermute x28, starting transfers between devices, shifted(): return lax.ppermute(x, 'z', [(z, (z + by) % depth) for z in range(depth)])  42.9 us
    all_to_all x2, blocking collectives, exchanged(): return lax.all_to_all(parts, ROW, 0, 0, tiled=True)  38 us
    all_to_all x1, blocking collectives, largest_of(): everyone = lax.all_to_all(everyone, CHIPS, 0, 0, tiled=True)  26 us
    ppermute x28, waiting for transfers between devices, shifted(): return lax.ppermute(x, 'z', [(z, (z + by) % depth) for z in range(depth)])  23.9 us
    ppermute x11, starting transfers between devices, swap_cores(): return lax.ppermute(x, 'c', ((0, 1), (1, 0)))  13.1 us
    ppermute x2, starting transfers between devices, swap_far(): return lax.ppermute(x, 'yh', ((0, 1), (1, 0)))  6.53 us
    dot_general x2, matrix products, partial_of(): jnp.dot(tile_of(side), slips[0], preferred_element_type=jnp.float32)  4.67 us
    dot_general x2, matrix products, partial_of(): jnp.dot(tile_of(1 - side), slips[1], preferred_element_type=jnp.float32)  4.65 us
  transfers between devices with their start and end apart: 41, of which 10 were waited for; matrix products, arithmetic and copies ran while one was open for 4% of the time, Pallas kernels for 0%

profile of v3, /device:TPU:1, one launch (start us, length us, event | category | flops | bytes accessed | tf_op | source)
XLA Modules:
  0.0 173.6 jit_solution(4098463893853224220)
XLA Ops:
  0.6 1.0 copy.75
  1.6 0.6 broadcast_in_dim.143
  2.2 140.7 %while.20 = (s32[]{:T(128)}, f32[128,512]{1,0:T(8,128)S(1)}, f32[128,512]{1,0:T(8,128)S(1)}, f32[128,512]{1,0:T(8,128)S(1)}, bf16[512]{0:T(512)(128)(2,1)}, /*in...) while((s32[]{:T(128)}, f32[128,512]{1,0:T(8,128)S(1)}, ...), condition=%wide.region_5.6_spmd, body=%wide.region_0.5_spmd.sunk | while | flops 4303235072 | bytes 91000928 | solution.py:194
  2.2 0.1 broadcast.134
  2.4 0.1 constant_dynamic-update-slice_fusion.36
  2.5 3.8 %collective-permute-start.7 = (bf16[128,512]{1,0:T(8,128)(2,1)S(1)}, bf16[128,512]{1,0:T(8,128)(2,1)S(1)}, u32[]{:S(2)}, u32[]{:S(2)}) collective-permute-start(bf16[128,512]{1,0:T(8,128)(2,1)S(1)} %get-tuple-element.1047), channel_id=1, source_target_pairs={{0,16},{16,0},{1,17},{17,1},{2,18},{18,2},{3,19},{19,3},{4,20},{20... | collective-permute-start | bytes 393224 | tf_op jit(solution)/shard_map/while/body/ppermute | solution.py:50
  6.3 1.6 collective-permute-start
  8.0 3.9 %collective-permute-start.1 = (bf16[128,512]{1,0:T(8,128)(2,1)S(1)}, bf16[128,512]{1,0:T(8,128)(2,1)S(1)}, u32[]{:S(2)}, u32[]{:S(2)}) collective-permute-start(bf16[128,512]{1,0:T(8,128)(2,1)S(1)} %get-tuple-element.1047), channel_id=1, source_target_pairs={{0,14},{2,0},{4,2},{6,4},{8,6},{10,8},{12,10},{14,12},{1,15},{3,1}... | collective-permute-start | bytes 393224 | tf_op jit(solution)/shard_map/while/body/ppermute | solution.py:55
  12.1 2.8 %collective-permute-start.11 = (bf16[128,512]{1,0:T(8,128)(2,1)S(1)}, bf16[128,512]{1,0:T(8,128)(2,1)S(1)}, u32[]{:S(2)}, u32[]{:S(2)}) collective-permute-start(bf16[128,512]{1,0:T(8,128)(2,1)S(1)} %collective-permute-done.7), channel_id=1, source_target_pairs={{0,14},{2,0},{4,2},{6,4},{8,6},{10,8},{12,10},{14,12},{1,15},{3,1}... | collective-permute-start | bytes 393224 | tf_op jit(solution)/shard_map/while/body/ppermute | solution.py:55
  14.9 2.7 %collective-permute-start.3 = (bf16[128,512]{1,0:T(8,128)(2,1)S(1)}, bf16[128,512]{1,0:T(8,128)(2,1)S(1)}, u32[]{:S(2)}, u32[]{:S(2)}) collective-permute-start(bf16[128,512]{1,0:T(8,128)(2,1)S(1)} %collective-permute-done.1), channel_id=1, source_target_pairs={{0,14},{2,0},{4,2},{6,4},{8,6},{10,8},{12,10},{14,12},{1,15},{3,1}... | collective-permute-start | bytes 393224 | tf_op jit(solution)/shard_map/while/body/ppermute | solution.py:55
  17.6 0.2 broadcast.135
  17.8 2.5 %collective-permute-done.2 = bf16[128,512]{1,0:T(8,128)(2,1)S(1)} collective-permute-done((bf16[128,512]{1,0:T(8,128)(2,1)S(1)}, bf16[128,512]{1,0:T(8,128)(2,1)S(1)}, u32[]{:S(2)}, u32[]{:S(2)}) %collective-permute-start.2) | collective-permute-done | bytes 131104 | tf_op jit(solution)/shard_map/while/body/ppermute | solution.py:55
  20.4 3.0 %collective-permute-start.5 = (bf16[128,512]{1,0:T(8,128)(2,1)S(1)}, bf16[128,512]{1,0:T(8,128)(2,1)S(1)}, u32[]{:S(2)}, u32[]{:S(2)}) collective-permute-start(bf16[128,512]{1,0:T(8,128)(2,1)S(1)} %collective-permute-done.3), channel_id=1, source_target_pairs={{0,14},{2,0},{4,2},{6,4},{8,6},{10,8},{12,10},{14,12},{1,15},{3,1}... | collective-permute-start | bytes 393224 | tf_op jit(solution)/shard_map/while/body/ppermute | solution.py:55
  23.3 2.7 %collective-permute-start.12 = (bf16[128,512]{1,0:T(8,128)(2,1)S(1)}, bf16[128,512]{1,0:T(8,128)(2,1)S(1)}, u32[]{:S(2)}, u32[]{:S(2)}) collective-permute-start(bf16[128,512]{1,0:T(8,128)(2,1)S(1)} %collective-permute-done.11), channel_id=1, source_target_pairs={{0,14},{2,0},{4,2},{6,4},{8,6},{10,8},{12,10},{14,12},{1,15},{3,1}... | collective-permute-start | bytes 393224 | tf_op jit(solution)/shard_map/while/body/ppermute | solution.py:55
  26.2 3.8 %collective-permute-done.9 = bf16[128,512]{1,0:T(8,128)(2,1)S(1)} collective-permute-done((bf16[128,512]{1,0:T(8,128)(2,1)S(1)}, bf16[128,512]{1,0:T(8,128)(2,1)S(1)}, u32[]{:S(2)}, u32[]{:S(2)}) %collective-permute-start.9) | collective-permute-done | bytes 131104 | tf_op jit(solution)/shard_map/while/body/ppermute | solution.py:55
  30.0 2.7 %collective-permute-start.13 = (bf16[128,512]{1,0:T(8,128)(2,1)S(1)}, bf16[128,512]{1,0:T(8,128)(2,1)S(1)}, u32[]{:S(2)}, u32[]{:S(2)}) collective-permute-start(bf16[128,512]{1,0:T(8,128)(2,1)S(1)} %collective-permute-done.12), channel_id=1, source_target_pairs={{0,14},{2,0},{4,2},{6,4},{8,6},{10,8},{12,10},{14,12},{1,15},{3,1}... | collective-permute-start | bytes 393224 | tf_op jit(solution)/shard_map/while/body/ppermute | solution.py:55
  32.8 3.1 %collective-permute-done.10 = bf16[128,512]{1,0:T(8,128)(2,1)S(1)} collective-permute-done((bf16[128,512]{1,0:T(8,128)(2,1)S(1)}, bf16[128,512]{1,0:T(8,128)(2,1)S(1)}, u32[]{:S(2)}, u32[]{:S(2)}) %collective-permute-start.10) | collective-permute-done | bytes 131104 | tf_op jit(solution)/shard_map/while/body/ppermute | solution.py:55
  35.9 3.7 %collective-permute-start.14 = (bf16[640,512]{1,0:T(8,128)(2,1)S(1)}, bf16[640,512]{1,0:T(8,128)(2,1)S(1)}, u32[]{:S(2)}, u32[]{:S(2)}) collective-permute-start(bf16[640,512]{1,0:T(8,128)(2,1)S(1)} %constant_dynamic-update-slice_fusion.48), channel_id=1, source_target_pairs={{0,1},{1,0},{2,3},{3,2},{4,5},{5,4},{6,7},{7,6},{8,9},{9,8},{10,11... | collective-permute-start | bytes 1966088 | tf_op jit(solution)/shard_map/while/body/ppermute | solution.py:46
  39.7 0.1 collective-permute-start.15
  39.9 0.6 collective-permute-start.17
  40.6 3.0 %collective-permute-start.16 = (bf16[128,512]{1,0:T(8,128)(2,1)S(1)}, bf16[128,512]{1,0:T(8,128)(2,1)S(1)}, u32[]{:S(2)}, u32[]{:S(2)}) collective-permute-start(bf16[128,512]{1,0:T(8,128)(2,1)S(1)} %collective-permute-done.13), channel_id=1, source_target_pairs={{0,14},{2,0},{4,2},{6,4},{8,6},{10,8},{12,10},{14,12},{1,15},{3,1}... | collective-permute-start | bytes 393224 | tf_op jit(solution)/shard_map/while/body/ppermute | solution.py:55
  43.7 2.4 %collective-permute-done.16 = bf16[128,512]{1,0:T(8,128)(2,1)S(1)} collective-permute-done((bf16[128,512]{1,0:T(8,128)(2,1)S(1)}, bf16[128,512]{1,0:T(8,128)(2,1)S(1)}, u32[]{:S(2)}, u32[]{:S(2)}) %collective-permute-start.16) | collective-permute-done | bytes 131104 | tf_op jit(solution)/shard_map/while/body/ppermute | solution.py:55
  46.1 1.3 collective-permute-start.19
  47.6 2.3 %fusion.53 = f32[1024,512]{1,0:T(8,128)S(1)} fusion(bf16[2048,512]{1,0:T(8,128)(2,1)S(1)} %slice_dynamic-update-slice_fusion.23, bf16[1024,4096]{1,0:T(8,128)(2,1)S(1)} %copy-done.8, s32[]{:T(128)S(6)} %select_n.315), kind=kOutput, calls=%fused_computation.2.clone.1 | convolution fusion | flops 2147483648 | bytes 8388612 | tf_op jit(solution)/shard_map/while/body/dot_general | solution.py:150
  50.1 2.3 %add_convert_fusion.2 = bf16[1024,512]{1,0:T(8,128)(2,1)S(1)} fusion(f32[1024,512]{1,0:T(8,128)S(1)} %fusion.53, bf16[2048,512]{1,0:T(8,128)(2,1)S(1)} %bitcast.136, bf16[1024,4096]{1,0:T(8,128)(2,1)S(1)} %copy-done.8, s32[]{:T(128)S(6)} %select_n.316), kind=kOutput, calls=%fused_computation.5.clone.1 | convolution fusion | flops 2148532224 | bytes 9437188 | tf_op jit(solution)/shard_map/while/body/dot_general | solution.py:152
  52.5 20.1 %all_to_all.15 = bf16[8,128,512]{2,1,0:T(8,128)(2,1)S(1)} all-to-all(bf16[8,128,512]{2,1,0:T(8,128)(2,1)S(1)} %bitcast.138), channel_id=1, replica_groups=mesh['x'=4,'yl'=2,'yh'=2,'z'=8,'c'=2] {'x','yl'}, dimensions={0} | all-to-all | bytes 2097152 | tf_op jit(solution)/shard_map/while/body/all_to_all | solution.py:159
  72.7 0.6 copy.72
  73.2 0.1 convert_reduce_fusion.2
  73.5 1.1 abs_reduce_fusion.2
  74.6 0.7 broadcast_select_fusion.2
  75.3 0.1 broadcast.134
  75.4 0.1 constant_dynamic-update-slice_fusion.36
  75.5 2.7 %collective-permute-start.7 = (bf16[128,512]{1,0:T(8,128)(2,1)S(1)}, bf16[128,512]{1,0:T(8,128)(2,1)S(1)}, u32[]{:S(2)}, u32[]{:S(2)}) collective-permute-start(bf16[128,512]{1,0:T(8,128)(2,1)S(1)} %get-tuple-element.1047), channel_id=1, source_target_pairs={{0,16},{16,0},{1,17},{17,1},{2,18},{18,2},{3,19},{19,3},{4,20},{20... | collective-permute-start | bytes 393224 | tf_op jit(solution)/shard_map/while/body/ppermute | solution.py:50
  78.2 0.3 collective-permute-start
  78.5 3.2 %collective-permute-start.1 = (bf16[128,512]{1,0:T(8,128)(2,1)S(1)}, bf16[128,512]{1,0:T(8,128)(2,1)S(1)}, u32[]{:S(2)}, u32[]{:S(2)}) collective-permute-start(bf16[128,512]{1,0:T(8,128)(2,1)S(1)} %get-tuple-element.1047), channel_id=1, source_target_pairs={{0,14},{2,0},{4,2},{6,4},{8,6},{10,8},{12,10},{14,12},{1,15},{3,1}... | collective-permute-start | bytes 393224 | tf_op jit(solution)/shard_map/while/body/ppermute | solution.py:55
  81.8 2.7 %collective-permute-start.11 = (bf16[128,512]{1,0:T(8,128)(2,1)S(1)}, bf16[128,512]{1,0:T(8,128)(2,1)S(1)}, u32[]{:S(2)}, u32[]{:S(2)}) collective-permute-start(bf16[128,512]{1,0:T(8,128)(2,1)S(1)} %collective-permute-done.7), channel_id=1, source_target_pairs={{0,14},{2,0},{4,2},{6,4},{8,6},{10,8},{12,10},{14,12},{1,15},{3,1}... | collective-permute-start | bytes 393224 | tf_op jit(solution)/shard_map/while/body/ppermute | solution.py:55
  84.5 2.7 %collective-permute-start.3 = (bf16[128,512]{1,0:T(8,128)(2,1)S(1)}, bf16[128,512]{1,0:T(8,128)(2,1)S(1)}, u32[]{:S(2)}, u32[]{:S(2)}) collective-permute-start(bf16[128,512]{1,0:T(8,128)(2,1)S(1)} %collective-permute-done.1), channel_id=1, source_target_pairs={{0,14},{2,0},{4,2},{6,4},{8,6},{10,8},{12,10},{14,12},{1,15},{3,1}... | collective-permute-start | bytes 393224 | tf_op jit(solution)/shard_map/while/body/ppermute | solution.py:55
  87.2 0.2 broadcast.135
  87.5 3.1 %collective-permute-done.2 = bf16[128,512]{1,0:T(8,128)(2,1)S(1)} collective-permute-done((bf16[128,512]{1,0:T(8,128)(2,1)S(1)}, bf16[128,512]{1,0:T(8,128)(2,1)S(1)}, u32[]{:S(2)}, u32[]{:S(2)}) %collective-permute-start.2) | collective-permute-done | bytes 131104 | tf_op jit(solution)/shard_map/while/body/ppermute | solution.py:55
  90.6 0.2 collective-permute-done.3
  90.8 2.9 %collective-permute-start.5 = (bf16[128,512]{1,0:T(8,128)(2,1)S(1)}, bf16[128,512]{1,0:T(8,128)(2,1)S(1)}, u32[]{:S(2)}, u32[]{:S(2)}) collective-permute-start(bf16[128,512]{1,0:T(8,128)(2,1)S(1)} %collective-permute-done.3), channel_id=1, source_target_pairs={{0,14},{2,0},{4,2},{6,4},{8,6},{10,8},{12,10},{14,12},{1,15},{3,1}... | collective-permute-start | bytes 393224 | tf_op jit(solution)/shard_map/while/body/ppermute | solution.py:55
  93.7 2.7 %collective-permute-start.12 = (bf16[128,512]{1,0:T(8,128)(2,1)S(1)}, bf16[128,512]{1,0:T(8,128)(2,1)S(1)}, u32[]{:S(2)}, u32[]{:S(2)}) collective-permute-start(bf16[128,512]{1,0:T(8,128)(2,1)S(1)} %collective-permute-done.11), channel_id=1, source_target_pairs={{0,14},{2,0},{4,2},{6,4},{8,6},{10,8},{12,10},{14,12},{1,15},{3,1}... | collective-permute-start | bytes 393224 | tf_op jit(solution)/shard_map/while/body/ppermute | solution.py:55
  96.6 3.5 %collective-permute-done.9 = bf16[128,512]{1,0:T(8,128)(2,1)S(1)} collective-permute-done((bf16[128,512]{1,0:T(8,128)(2,1)S(1)}, bf16[128,512]{1,0:T(8,128)(2,1)S(1)}, u32[]{:S(2)}, u32[]{:S(2)}) %collective-permute-start.9) | collective-permute-done | bytes 131104 | tf_op jit(solution)/shard_map/while/body/ppermute | solution.py:55
  100.1 2.9 %collective-permute-start.13 = (bf16[128,512]{1,0:T(8,128)(2,1)S(1)}, bf16[128,512]{1,0:T(8,128)(2,1)S(1)}, u32[]{:S(2)}, u32[]{:S(2)}) collective-permute-start(bf16[128,512]{1,0:T(8,128)(2,1)S(1)} %collective-permute-done.12), channel_id=1, source_target_pairs={{0,14},{2,0},{4,2},{6,4},{8,6},{10,8},{12,10},{14,12},{1,15},{3,1}... | collective-permute-start | bytes 393224 | tf_op jit(solution)/shard_map/while/body/ppermute | solution.py:55
  103.1 2.9 %collective-permute-done.10 = bf16[128,512]{1,0:T(8,128)(2,1)S(1)} collective-permute-done((bf16[128,512]{1,0:T(8,128)(2,1)S(1)}, bf16[128,512]{1,0:T(8,128)(2,1)S(1)}, u32[]{:S(2)}, u32[]{:S(2)}) %collective-permute-start.10) | collective-permute-done | bytes 131104 | tf_op jit(solution)/shard_map/while/body/ppermute | solution.py:55
  106.1 4.0 %collective-permute-start.14 = (bf16[640,512]{1,0:T(8,128)(2,1)S(1)}, bf16[640,512]{1,0:T(8,128)(2,1)S(1)}, u32[]{:S(2)}, u32[]{:S(2)}) collective-permute-start(bf16[640,512]{1,0:T(8,128)(2,1)S(1)} %constant_dynamic-update-slice_fusion.48), channel_id=1, source_target_pairs={{0,1},{1,0},{2,3},{3,2},{4,5},{5,4},{6,7},{7,6},{8,9},{9,8},{10,11... | collective-permute-start | bytes 1966088 | tf_op jit(solution)/shard_map/while/body/ppermute | solution.py:46
  110.3 0.6 collective-permute-start.17
  111.0 3.0 %collective-permute-start.16 = (bf16[128,512]{1,0:T(8,128)(2,1)S(1)}, bf16[128,512]{1,0:T(8,128)(2,1)S(1)}, u32[]{:S(2)}, u32[]{:S(2)}) collective-permute-start(bf16[128,512]{1,0:T(8,128)(2,1)S(1)} %collective-permute-done.13), channel_id=1, source_target_pairs={{0,14},{2,0},{4,2},{6,4},{8,6},{10,8},{12,10},{14,12},{1,15},{3,1}... | collective-permute-start | bytes 393224 | tf_op jit(solution)/shard_map/while/body/ppermute | solution.py:55
  114.1 2.4 %collective-permute-done.16 = bf16[128,512]{1,0:T(8,128)(2,1)S(1)} collective-permute-done((bf16[128,512]{1,0:T(8,128)(2,1)S(1)}, bf16[128,512]{1,0:T(8,128)(2,1)S(1)}, u32[]{:S(2)}, u32[]{:S(2)}) %collective-permute-start.16) | collective-permute-done | bytes 131104 | tf_op jit(solution)/shard_map/while/body/ppermute | solution.py:55
  116.5 1.3 collective-permute-start.19
  118.0 2.3 %fusion.53 = f32[1024,512]{1,0:T(8,128)S(1)} fusion(bf16[2048,512]{1,0:T(8,128)(2,1)S(1)} %slice_dynamic-update-slice_fusion.23, bf16[1024,4096]{1,0:T(8,128)(2,1)S(1)} %copy-done.8, s32[]{:T(128)S(6)} %select_n.315), kind=kOutput, calls=%fused_computation.2.clone.1 | convolution fusion | flops 2147483648 | bytes 8388612 | tf_op jit(solution)/shard_map/while/body/dot_general | solution.py:150
  120.5 2.3 %add_convert_fusion.2 = bf16[1024,512]{1,0:T(8,128)(2,1)S(1)} fusion(f32[1024,512]{1,0:T(8,128)S(1)} %fusion.53, bf16[2048,512]{1,0:T(8,128)(2,1)S(1)} %bitcast.136, bf16[1024,4096]{1,0:T(8,128)(2,1)S(1)} %copy-done.8, s32[]{:T(128)S(6)} %select_n.316), kind=kOutput, calls=%fused_computation.5.clone.1 | convolution fusion | flops 2148532224 | bytes 9437188 | tf_op jit(solution)/shard_map/while/body/dot_general | solution.py:152
  122.9 17.9 %all_to_all.15 = bf16[8,128,512]{2,1,0:T(8,128)(2,1)S(1)} all-to-all(bf16[8,128,512]{2,1,0:T(8,128)(2,1)S(1)} %bitcast.138), channel_id=1, replica_groups=mesh['x'=4,'yl'=2,'yh'=2,'z'=8,'c'=2] {'x','yl'}, dimensions={0} | all-to-all | bytes 2097152 | tf_op jit(solution)/shard_map/while/body/all_to_all | solution.py:159
  140.8 0.6 copy.72
  141.4 0.1 convert_reduce_fusion.2
  141.6 1.1 abs_reduce_fusion.2
  142.9 0.7 stack.12
  143.6 1.2 collective-permute-start.20
  144.9 0.8 collective-permute-done.20
  145.7 0.1 broadcast_in_dim.144
  145.8 26.0 %all_to_all.14 = bf16[128,2,512]{2,1,0:T(2,128)(2,1)S(1)} all-to-all(bf16[128,2,512]{2,1,0:T(2,128)(2,1)S(1)} %broadcast_in_dim.144), channel_id=1, replica_groups=mesh['x'=4,'yl'=2,'yh'=2,'z'=8,'c'=2] {'x','yl','yh','z'}, dimensions={0} | all-to-all | bytes 524288 | tf_op jit(solution)/shard_map/all_to_all | solution.py:171
  171.8 0.3 reduce_max.21
  172.1 0.6 fusion.31
  172.7 0.9 multiply_bitcast_fusion.1
  (184 shorter events, 2.4 us)
Async XLA Ops:
  2.2 9.7 %copy-start.4 = (f32[16]{0:T(128)S(1)}, f32[16]{0:T(128)}, u32[]{:S(2)}) copy-start(f32[16]{0:T(128)} %get-tuple-element.1060) | copy-start | bytes 196 | tf_op jit(solution)/shard_map/while
  2.2 9.7 %copy-start.5 = (f32[16]{0:T(128)S(1)}, f32[16]{0:T(128)}, u32[]{:S(2)}) copy-start(f32[16]{0:T(128)} %get-tuple-element.1058) | copy-start | bytes 196 | tf_op jit(solution)/shard_map/while
  2.2 9.7 %copy-start.6 = (s32[1,1,128]{2,1,0:T(1,128)S(1)}, s32[1,1,128]{2,1,0:T(1,128)}, u32[]{:S(2)}) copy-start(s32[1,1,128]{2,1,0:T(1,128)} %get-tuple-element.1059) | copy-start | bytes 1540 | tf_op jit(solution)/shard_map/while
  2.5 9.5 %collective-permute-start.7 = (bf16[128,512]{1,0:T(8,128)(2,1)S(1)}, bf16[128,512]{1,0:T(8,128)(2,1)S(1)}, u32[]{:S(2)}, u32[]{:S(2)}) collective-permute-start(bf16[128,512]{1,0:T(8,128)(2,1)S(1)} %get-tuple-element.1047), channel_id=1, source_target_pairs={{0,16},{16,0},{1,17},{17,1},{2,18},{18,2},{3,19},{19,3},{4,20},{20... | collective-permute-start | bytes 393224 | tf_op jit(solution)/shard_map/while/body/ppermute | solution.py:50
  6.3 8.6 %collective-permute-start = (bf16[128,512]{1,0:T(8,128)(2,1)S(1)}, bf16[128,512]{1,0:T(8,128)(2,1)S(1)}, u32[]{:S(2)}, u32[]{:S(2)}) collective-permute-start(bf16[128,512]{1,0:T(8,128)(2,1)S(1)} %get-tuple-element.1047), channel_id=1, source_target_pairs={{0,2},{2,4},{4,6},{6,8},{8,10},{10,12},{12,14},{14,0},{1,3},{3,5},... | collective-permute-start | bytes 393224 | tf_op jit(solution)/shard_map/while/body/ppermute | solution.py:55
  8.0 6.9 %collective-permute-start.1 = (bf16[128,512]{1,0:T(8,128)(2,1)S(1)}, bf16[128,512]{1,0:T(8,128)(2,1)S(1)}, u32[]{:S(2)}, u32[]{:S(2)}) collective-permute-start(bf16[128,512]{1,0:T(8,128)(2,1)S(1)} %get-tuple-element.1047), channel_id=1, source_target_pairs={{0,14},{2,0},{4,2},{6,4},{8,6},{10,8},{12,10},{14,12},{1,15},{3,1}... | collective-permute-start | bytes 393224 | tf_op jit(solution)/shard_map/while/body/ppermute | solution.py:55
  12.0 11.3 %collective-permute-start.8 = (bf16[128,512]{1,0:T(8,128)(2,1)S(1)}, bf16[128,512]{1,0:T(8,128)(2,1)S(1)}, u32[]{:S(2)}, u32[]{:S(2)}) collective-permute-start(bf16[128,512]{1,0:T(8,128)(2,1)S(1)} %collective-permute-done.7), channel_id=1, source_target_pairs={{0,2},{2,4},{4,6},{6,8},{8,10},{10,12},{12,14},{14,0},{1,3},{3,5},... | collective-permute-start | bytes 393224 | tf_op jit(solution)/shard_map/while/body/ppermute | solution.py:55
  12.1 11.2 %collective-permute-start.11 = (bf16[128,512]{1,0:T(8,128)(2,1)S(1)}, bf16[128,512]{1,0:T(8,128)(2,1)S(1)}, u32[]{:S(2)}, u32[]{:S(2)}) collective-permute-start(bf16[128,512]{1,0:T(8,128)(2,1)S(1)} %collective-permute-done.7), channel_id=1, source_target_pairs={{0,14},{2,0},{4,2},{6,4},{8,6},{10,8},{12,10},{14,12},{1,15},{3,1}... | collective-permute-start | bytes 393224 | tf_op jit(solution)/shard_map/while/body/ppermute | solution.py:55
  14.9 5.5 %collective-permute-start.2 = (bf16[128,512]{1,0:T(8,128)(2,1)S(1)}, bf16[128,512]{1,0:T(8,128)(2,1)S(1)}, u32[]{:S(2)}, u32[]{:S(2)}) collective-permute-start(bf16[128,512]{1,0:T(8,128)(2,1)S(1)} %collective-permute-done), channel_id=1, source_target_pairs={{0,2},{2,4},{4,6},{6,8},{8,10},{10,12},{12,14},{14,0},{1,3},{3,5},... | collective-permute-start | bytes 393224 | tf_op jit(solution)/shard_map/while/body/ppermute | solution.py:55
  14.9 5.5 %collective-permute-start.3 = (bf16[128,512]{1,0:T(8,128)(2,1)S(1)}, bf16[128,512]{1,0:T(8,128)(2,1)S(1)}, u32[]{:S(2)}, u32[]{:S(2)}) collective-permute-start(bf16[128,512]{1,0:T(8,128)(2,1)S(1)} %collective-permute-done.1), channel_id=1, source_target_pairs={{0,14},{2,0},{4,2},{6,4},{8,6},{10,8},{12,10},{14,12},{1,15},{3,1}... | collective-permute-start | bytes 393224 | tf_op jit(solution)/shard_map/while/body/ppermute | solution.py:55
  20.3 5.7 %collective-permute-start.4 = (bf16[128,512]{1,0:T(8,128)(2,1)S(1)}, bf16[128,512]{1,0:T(8,128)(2,1)S(1)}, u32[]{:S(2)}, u32[]{:S(2)}) collective-permute-start(bf16[128,512]{1,0:T(8,128)(2,1)S(1)} %collective-permute-done.2), channel_id=1, source_target_pairs={{0,2},{2,4},{4,6},{6,8},{8,10},{10,12},{12,14},{14,0},{1,3},{3,5},... | collective-permute-start | bytes 393224 | tf_op jit(solution)/shard_map/while/body/ppermute | solution.py:55
  20.4 12.4 %collective-permute-start.5 = (bf16[128,512]{1,0:T(8,128)(2,1)S(1)}, bf16[128,512]{1,0:T(8,128)(2,1)S(1)}, u32[]{:S(2)}, u32[]{:S(2)}) collective-permute-start(bf16[128,512]{1,0:T(8,128)(2,1)S(1)} %collective-permute-done.3), channel_id=1, source_target_pairs={{0,14},{2,0},{4,2},{6,4},{8,6},{10,8},{12,10},{14,12},{1,15},{3,1}... | collective-permute-start | bytes 393224 | tf_op jit(solution)/shard_map/while/body/ppermute | solution.py:55
  23.3 6.7 %collective-permute-start.9 = (bf16[128,512]{1,0:T(8,128)(2,1)S(1)}, bf16[128,512]{1,0:T(8,128)(2,1)S(1)}, u32[]{:S(2)}, u32[]{:S(2)}) collective-permute-start(bf16[128,512]{1,0:T(8,128)(2,1)S(1)} %collective-permute-done.8), channel_id=1, source_target_pairs={{0,2},{2,4},{4,6},{6,8},{8,10},{10,12},{12,14},{14,0},{1,3},{3,5},... | collective-permute-start | bytes 393224 | tf_op jit(solution)/shard_map/while/body/ppermute | solution.py:55
  23.3 6.7 %collective-permute-start.12 = (bf16[128,512]{1,0:T(8,128)(2,1)S(1)}, bf16[128,512]{1,0:T(8,128)(2,1)S(1)}, u32[]{:S(2)}, u32[]{:S(2)}) collective-permute-start(bf16[128,512]{1,0:T(8,128)(2,1)S(1)} %collective-permute-done.11), channel_id=1, source_target_pairs={{0,14},{2,0},{4,2},{6,4},{8,6},{10,8},{12,10},{14,12},{1,15},{3,1}... | collective-permute-start | bytes 393224 | tf_op jit(solution)/shard_map/while/body/ppermute | solution.py:55
  26.1 21.5 %copy-start.8 = (bf16[1024,4096]{1,0:T(8,128)(2,1)S(1)}, bf16[1024,4096]{1,0:T(8,128)(2,1)}, u32[]{:S(2)}) copy-start(bf16[1024,4096]{1,0:T(8,128)(2,1)} %get-tuple-element.1215) | copy-start | bytes 25165828 | tf_op jit(solution)/shard_map/while
  26.1 13.6 %collective-permute-start.6 = (bf16[128,512]{1,0:T(8,128)(2,1)S(1)}, bf16[128,512]{1,0:T(8,128)(2,1)S(1)}, u32[]{:S(2)}, u32[]{:S(2)}) collective-permute-start(bf16[128,512]{1,0:T(8,128)(2,1)S(1)} %collective-permute-done.4), channel_id=1, source_target_pairs={{0,2},{2,4},{4,6},{6,8},{8,10},{10,12},{12,14},{14,0},{1,3},{3,5},... | collective-permute-start | bytes 393224 | tf_op jit(solution)/shard_map/while/body/ppermute | solution.py:55
  30.0 5.8 %collective-permute-start.10 = (bf16[128,512]{1,0:T(8,128)(2,1)S(1)}, bf16[128,512]{1,0:T(8,128)(2,1)S(1)}, u32[]{:S(2)}, u32[]{:S(2)}) collective-permute-start(bf16[128,512]{1,0:T(8,128)(2,1)S(1)} %collective-permute-done.9), channel_id=1, source_target_pairs={{0,2},{2,4},{4,6},{6,8},{8,10},{10,12},{12,14},{14,0},{1,3},{3,5},... | collective-permute-start | bytes 393224 | tf_op jit(solution)/shard_map/while/body/ppermute | solution.py:55
  30.0 5.8 %collective-permute-start.13 = (bf16[128,512]{1,0:T(8,128)(2,1)S(1)}, bf16[128,512]{1,0:T(8,128)(2,1)S(1)}, u32[]{:S(2)}, u32[]{:S(2)}) collective-permute-start(bf16[128,512]{1,0:T(8,128)(2,1)S(1)} %collective-permute-done.12), channel_id=1, source_target_pairs={{0,14},{2,0},{4,2},{6,4},{8,6},{10,8},{12,10},{14,12},{1,15},{3,1}... | collective-permute-start | bytes 393224 | tf_op jit(solution)/shard_map/while/body/ppermute | solution.py:55
  35.9 11.4 %collective-permute-start.14 = (bf16[640,512]{1,0:T(8,128)(2,1)S(1)}, bf16[640,512]{1,0:T(8,128)(2,1)S(1)}, u32[]{:S(2)}, u32[]{:S(2)}) collective-permute-start(bf16[640,512]{1,0:T(8,128)(2,1)S(1)} %constant_dynamic-update-slice_fusion.48), channel_id=1, source_target_pairs={{0,1},{1,0},{2,3},{3,2},{4,5},{5,4},{6,7},{7,6},{8,9},{9,8},{10,11... | collective-permute-start | bytes 1966088 | tf_op jit(solution)/shard_map/while/body/ppermute | solution.py:46
  39.7 7.8 %collective-permute-start.15 = (bf16[384,512]{1,0:T(8,128)(2,1)S(1)}, bf16[384,512]{1,0:T(8,128)(2,1)S(1)}, u32[]{:S(2)}, u32[]{:S(2)}) collective-permute-start(bf16[384,512]{1,0:T(8,128)(2,1)S(1)} %pad_maximum_fusion.5), channel_id=1, source_target_pairs={{0,1},{1,0},{2,3},{3,2},{4,5},{5,4},{6,7},{7,6},{8,9},{9,8},{10,11... | collective-permute-start | bytes 1179656 | tf_op jit(solution)/shard_map/while/body/ppermute | solution.py:46
  39.9 10.0 %collective-permute-start.17 = (bf16[640,512]{1,0:T(8,128)(2,1)S(1)}, bf16[640,512]{1,0:T(8,128)(2,1)S(1)}, u32[]{:S(2)}, u32[]{:S(2)}) collective-permute-start(bf16[640,512]{1,0:T(8,128)(2,1)S(1)} %constant_dynamic-update-slice_fusion.53), channel_id=1, source_target_pairs={{0,1},{1,0},{2,3},{3,2},{4,5},{5,4},{6,7},{7,6},{8,9},{9,8},{10,11... | collective-permute-start | bytes 1966088 | tf_op jit(solution)/shard_map/while/body/ppermute | solution.py:46
  40.5 9.6 %collective-permute-start.18 = (bf16[256,512]{1,0:T(8,128)(2,1)S(1)}, bf16[256,512]{1,0:T(8,128)(2,1)S(1)}, u32[]{:S(2)}, u32[]{:S(2)}) collective-permute-start(bf16[256,512]{1,0:T(8,128)(2,1)S(1)} %pad_maximum_fusion.6), channel_id=1, source_target_pairs={{0,1},{1,0},{2,3},{3,2},{4,5},{5,4},{6,7},{7,6},{8,9},{9,8},{10,11... | collective-permute-start | bytes 786440 | tf_op jit(solution)/shard_map/while/body/ppermute | solution.py:46
  40.6 5.5 %collective-permute-start.16 = (bf16[128,512]{1,0:T(8,128)(2,1)S(1)}, bf16[128,512]{1,0:T(8,128)(2,1)S(1)}, u32[]{:S(2)}, u32[]{:S(2)}) collective-permute-start(bf16[128,512]{1,0:T(8,128)(2,1)S(1)} %collective-permute-done.13), channel_id=1, source_target_pairs={{0,14},{2,0},{4,2},{6,4},{8,6},{10,8},{12,10},{14,12},{1,15},{3,1}... | collective-permute-start | bytes 393224 | tf_op jit(solution)/shard_map/while/body/ppermute | solution.py:55
  46.1 4.0 %collective-permute-start.19 = (bf16[128,512]{1,0:T(8,128)(2,1)S(1)}, bf16[128,512]{1,0:T(8,128)(2,1)S(1)}, u32[]{:S(2)}, u32[]{:S(2)}) collective-permute-start(bf16[128,512]{1,0:T(8,128)(2,1)S(1)} %collective-permute-done.16), channel_id=1, source_target_pairs={{0,1},{1,0},{2,3},{3,2},{4,5},{5,4},{6,7},{7,6},{8,9},{9,8},{10,11... | collective-permute-start | bytes 393224 | tf_op jit(solution)/shard_map/while/body/ppermute | solution.py:46
  52.5 20.9 %copy-start.9 = (s32[1,1,128]{2,1,0:T(1,128)S(1)}, s32[1,1,128]{2,1,0:T(1,128)}, u32[]{:S(2)}) copy-start(s32[1,1,128]{2,1,0:T(1,128)} %get-tuple-element.1065) | copy-start | bytes 1540 | tf_op jit(solution)/shard_map/while
  52.5 20.9 %copy-start.7 = (f32[1,1,128]{2,1,0:T(1,128)S(1)}, f32[1,1,128]{2,1,0:T(1,128)}, u32[]{:S(2)}) copy-start(f32[1,1,128]{2,1,0:T(1,128)} %get-tuple-element.1063) | copy-start | bytes 1540 | tf_op jit(solution)/shard_map/while
  52.5 20.9 %copy-start.1 = (f32[1,1,128,512]{3,2,1,0:T(8,128)S(1)}, f32[1,1,128,512]{3,2,1,0:T(8,128)}, u32[]{:S(2)}) copy-start(f32[1,1,128,512]{3,2,1,0:T(8,128)} %get-tuple-element.1091) | copy-start | bytes 786436 | tf_op jit(solution)/shard_map/while
  52.5 20.9 %copy-start.2 = (f32[512]{0:T(512)S(1)}, f32[512]{0:T(512)}, u32[]{:S(2)}) copy-start(f32[512]{0:T(512)} %get-tuple-element.1216) | copy-start | bytes 6148 | tf_op jit(solution)/shard_map/while
  52.5 20.9 %copy-start.3 = (f32[1,1,128]{2,1,0:T(1,128)S(1)}, f32[1,1,128]{2,1,0:T(1,128)}, u32[]{:S(2)}) copy-start(f32[1,1,128]{2,1,0:T(1,128)} %get-tuple-element.1064) | copy-start | bytes 1540 | tf_op jit(solution)/shard_map/while
  74.5 7.1 %copy-start.4 = (f32[16]{0:T(128)S(1)}, f32[16]{0:T(128)}, u32[]{:S(2)}) copy-start(f32[16]{0:T(128)} %get-tuple-element.1060) | copy-start | bytes 196 | tf_op jit(solution)/shard_map/while
  74.6 7.1 %copy-start.5 = (f32[16]{0:T(128)S(1)}, f32[16]{0:T(128)}, u32[]{:S(2)}) copy-start(f32[16]{0:T(128)} %get-tuple-element.1058) | copy-start | bytes 196 | tf_op jit(solution)/shard_map/while
  74.6 7.1 %copy-start.6 = (s32[1,1,128]{2,1,0:T(1,128)S(1)}, s32[1,1,128]{2,1,0:T(1,128)}, u32[]{:S(2)}) copy-start(s32[1,1,128]{2,1,0:T(1,128)} %get-tuple-element.1059) | copy-start | bytes 1540 | tf_op jit(solution)/shard_map/while
  75.5 6.2 %collective-permute-start.7 = (bf16[128,512]{1,0:T(8,128)(2,1)S(1)}, bf16[128,512]{1,0:T(8,128)(2,1)S(1)}, u32[]{:S(2)}, u32[]{:S(2)}) collective-permute-start(bf16[128,512]{1,0:T(8,128)(2,1)S(1)} %get-tuple-element.1047), channel_id=1, source_target_pairs={{0,16},{16,0},{1,17},{17,1},{2,18},{18,2},{3,19},{19,3},{4,20},{20... | collective-permute-start | bytes 393224 | tf_op jit(solution)/shard_map/while/body/ppermute | solution.py:50
  78.2 6.3 %collective-permute-start = (bf16[128,512]{1,0:T(8,128)(2,1)S(1)}, bf16[128,512]{1,0:T(8,128)(2,1)S(1)}, u32[]{:S(2)}, u32[]{:S(2)}) collective-permute-start(bf16[128,512]{1,0:T(8,128)(2,1)S(1)} %get-tuple-element.1047), channel_id=1, source_target_pairs={{0,2},{2,4},{4,6},{6,8},{8,10},{10,12},{12,14},{14,0},{1,3},{3,5},... | collective-permute-start | bytes 393224 | tf_op jit(solution)/shard_map/while/body/ppermute | solution.py:55
  78.5 6.0 %collective-permute-start.1 = (bf16[128,512]{1,0:T(8,128)(2,1)S(1)}, bf16[128,512]{1,0:T(8,128)(2,1)S(1)}, u32[]{:S(2)}, u32[]{:S(2)}) collective-permute-start(bf16[128,512]{1,0:T(8,128)(2,1)S(1)} %get-tuple-element.1047), channel_id=1, source_target_pairs={{0,14},{2,0},{4,2},{6,4},{8,6},{10,8},{12,10},{14,12},{1,15},{3,1}... | collective-permute-start | bytes 393224 | tf_op jit(solution)/shard_map/while/body/ppermute | solution.py:55
  81.8 12.0 %collective-permute-start.8 = (bf16[128,512]{1,0:T(8,128)(2,1)S(1)}, bf16[128,512]{1,0:T(8,128)(2,1)S(1)}, u32[]{:S(2)}, u32[]{:S(2)}) collective-permute-start(bf16[128,512]{1,0:T(8,128)(2,1)S(1)} %collective-permute-done.7), channel_id=1, source_target_pairs={{0,2},{2,4},{4,6},{6,8},{8,10},{10,12},{12,14},{14,0},{1,3},{3,5},... | collective-permute-start | bytes 393224 | tf_op jit(solution)/shard_map/while/body/ppermute | solution.py:55
  81.8 11.9 %collective-permute-start.11 = (bf16[128,512]{1,0:T(8,128)(2,1)S(1)}, bf16[128,512]{1,0:T(8,128)(2,1)S(1)}, u32[]{:S(2)}, u32[]{:S(2)}) collective-permute-start(bf16[128,512]{1,0:T(8,128)(2,1)S(1)} %collective-permute-done.7), channel_id=1, source_target_pairs={{0,14},{2,0},{4,2},{6,4},{8,6},{10,8},{12,10},{14,12},{1,15},{3,1}... | collective-permute-start | bytes 393224 | tf_op jit(solution)/shard_map/while/body/ppermute | solution.py:55
  84.5 6.1 %collective-permute-start.2 = (bf16[128,512]{1,0:T(8,128)(2,1)S(1)}, bf16[128,512]{1,0:T(8,128)(2,1)S(1)}, u32[]{:S(2)}, u32[]{:S(2)}) collective-permute-start(bf16[128,512]{1,0:T(8,128)(2,1)S(1)} %collective-permute-done), channel_id=1, source_target_pairs={{0,2},{2,4},{4,6},{6,8},{8,10},{10,12},{12,14},{14,0},{1,3},{3,5},... | collective-permute-start | bytes 393224 | tf_op jit(solution)/shard_map/while/body/ppermute | solution.py:55
  84.5 6.3 %collective-permute-start.3 = (bf16[128,512]{1,0:T(8,128)(2,1)S(1)}, bf16[128,512]{1,0:T(8,128)(2,1)S(1)}, u32[]{:S(2)}, u32[]{:S(2)}) collective-permute-start(bf16[128,512]{1,0:T(8,128)(2,1)S(1)} %collective-permute-done.1), channel_id=1, source_target_pairs={{0,14},{2,0},{4,2},{6,4},{8,6},{10,8},{12,10},{14,12},{1,15},{3,1}... | collective-permute-start | bytes 393224 | tf_op jit(solution)/shard_map/while/body/ppermute | solution.py:55
  90.6 5.9 %collective-permute-start.4 = (bf16[128,512]{1,0:T(8,128)(2,1)S(1)}, bf16[128,512]{1,0:T(8,128)(2,1)S(1)}, u32[]{:S(2)}, u32[]{:S(2)}) collective-permute-start(bf16[128,512]{1,0:T(8,128)(2,1)S(1)} %collective-permute-done.2), channel_id=1, source_target_pairs={{0,2},{2,4},{4,6},{6,8},{8,10},{10,12},{12,14},{14,0},{1,3},{3,5},... | collective-permute-start | bytes 393224 | tf_op jit(solution)/shard_map/while/body/ppermute | solution.py:55
  90.8 12.3 %collective-permute-start.5 = (bf16[128,512]{1,0:T(8,128)(2,1)S(1)}, bf16[128,512]{1,0:T(8,128)(2,1)S(1)}, u32[]{:S(2)}, u32[]{:S(2)}) collective-permute-start(bf16[128,512]{1,0:T(8,128)(2,1)S(1)} %collective-permute-done.3), channel_id=1, source_target_pairs={{0,14},{2,0},{4,2},{6,4},{8,6},{10,8},{12,10},{14,12},{1,15},{3,1}... | collective-permute-start | bytes 393224 | tf_op jit(solution)/shard_map/while/body/ppermute | solution.py:55
  93.7 6.4 %collective-permute-start.9 = (bf16[128,512]{1,0:T(8,128)(2,1)S(1)}, bf16[128,512]{1,0:T(8,128)(2,1)S(1)}, u32[]{:S(2)}, u32[]{:S(2)}) collective-permute-start(bf16[128,512]{1,0:T(8,128)(2,1)S(1)} %collective-permute-done.8), channel_id=1, source_target_pairs={{0,2},{2,4},{4,6},{6,8},{8,10},{10,12},{12,14},{14,0},{1,3},{3,5},... | collective-permute-start | bytes 393224 | tf_op jit(solution)/shard_map/while/body/ppermute | solution.py:55
  93.7 6.4 %collective-permute-start.12 = (bf16[128,512]{1,0:T(8,128)(2,1)S(1)}, bf16[128,512]{1,0:T(8,128)(2,1)S(1)}, u32[]{:S(2)}, u32[]{:S(2)}) collective-permute-start(bf16[128,512]{1,0:T(8,128)(2,1)S(1)} %collective-permute-done.11), channel_id=1, source_target_pairs={{0,14},{2,0},{4,2},{6,4},{8,6},{10,8},{12,10},{14,12},{1,15},{3,1}... | collective-permute-start | bytes 393224 | tf_op jit(solution)/shard_map/while/body/ppermute | solution.py:55
  96.5 21.5 %copy-start.8 = (bf16[1024,4096]{1,0:T(8,128)(2,1)S(1)}, bf16[1024,4096]{1,0:T(8,128)(2,1)}, u32[]{:S(2)}) copy-start(bf16[1024,4096]{1,0:T(8,128)(2,1)} %get-tuple-element.1215) | copy-start | bytes 25165828 | tf_op jit(solution)/shard_map/while
  96.5 13.6 %collective-permute-start.6 = (bf16[128,512]{1,0:T(8,128)(2,1)S(1)}, bf16[128,512]{1,0:T(8,128)(2,1)S(1)}, u32[]{:S(2)}, u32[]{:S(2)}) collective-permute-start(bf16[128,512]{1,0:T(8,128)(2,1)S(1)} %collective-permute-done.4), channel_id=1, source_target_pairs={{0,2},{2,4},{4,6},{6,8},{8,10},{10,12},{12,14},{14,0},{1,3},{3,5},... | collective-permute-start | bytes 393224 | tf_op jit(solution)/shard_map/while/body/ppermute | solution.py:55
  100.1 5.9 %collective-permute-start.10 = (bf16[128,512]{1,0:T(8,128)(2,1)S(1)}, bf16[128,512]{1,0:T(8,128)(2,1)S(1)}, u32[]{:S(2)}, u32[]{:S(2)}) collective-permute-start(bf16[128,512]{1,0:T(8,128)(2,1)S(1)} %collective-permute-done.9), channel_id=1, source_target_pairs={{0,2},{2,4},{4,6},{6,8},{8,10},{10,12},{12,14},{14,0},{1,3},{3,5},... | collective-permute-start | bytes 393224 | tf_op jit(solution)/shard_map/while/body/ppermute | solution.py:55
  100.1 5.9 %collective-permute-start.13 = (bf16[128,512]{1,0:T(8,128)(2,1)S(1)}, bf16[128,512]{1,0:T(8,128)(2,1)S(1)}, u32[]{:S(2)}, u32[]{:S(2)}) collective-permute-start(bf16[128,512]{1,0:T(8,128)(2,1)S(1)} %collective-permute-done.12), channel_id=1, source_target_pairs={{0,14},{2,0},{4,2},{6,4},{8,6},{10,8},{12,10},{14,12},{1,15},{3,1}... | collective-permute-start | bytes 393224 | tf_op jit(solution)/shard_map/while/body/ppermute | solution.py:55
  106.1 11.7 %collective-permute-start.14 = (bf16[640,512]{1,0:T(8,128)(2,1)S(1)}, bf16[640,512]{1,0:T(8,128)(2,1)S(1)}, u32[]{:S(2)}, u32[]{:S(2)}) collective-permute-start(bf16[640,512]{1,0:T(8,128)(2,1)S(1)} %constant_dynamic-update-slice_fusion.48), channel_id=1, source_target_pairs={{0,1},{1,0},{2,3},{3,2},{4,5},{5,4},{6,7},{7,6},{8,9},{9,8},{10,11... | collective-permute-start | bytes 1966088 | tf_op jit(solution)/shard_map/while/body/ppermute | solution.py:46
  110.1 7.8 %collective-permute-start.15 = (bf16[384,512]{1,0:T(8,128)(2,1)S(1)}, bf16[384,512]{1,0:T(8,128)(2,1)S(1)}, u32[]{:S(2)}, u32[]{:S(2)}) collective-permute-start(bf16[384,512]{1,0:T(8,128)(2,1)S(1)} %pad_maximum_fusion.5), channel_id=1, source_target_pairs={{0,1},{1,0},{2,3},{3,2},{4,5},{5,4},{6,7},{7,6},{8,9},{9,8},{10,11... | collective-permute-start | bytes 1179656 | tf_op jit(solution)/shard_map/while/body/ppermute | solution.py:46
  110.3 10.0 %collective-permute-start.17 = (bf16[640,512]{1,0:T(8,128)(2,1)S(1)}, bf16[640,512]{1,0:T(8,128)(2,1)S(1)}, u32[]{:S(2)}, u32[]{:S(2)}) collective-permute-start(bf16[640,512]{1,0:T(8,128)(2,1)S(1)} %constant_dynamic-update-slice_fusion.53), channel_id=1, source_target_pairs={{0,1},{1,0},{2,3},{3,2},{4,5},{5,4},{6,7},{7,6},{8,9},{9,8},{10,11... | collective-permute-start | bytes 1966088 | tf_op jit(solution)/shard_map/while/body/ppermute | solution.py:46
  110.9 9.6 %collective-permute-start.18 = (bf16[256,512]{1,0:T(8,128)(2,1)S(1)}, bf16[256,512]{1,0:T(8,128)(2,1)S(1)}, u32[]{:S(2)}, u32[]{:S(2)}) collective-permute-start(bf16[256,512]{1,0:T(8,128)(2,1)S(1)} %pad_maximum_fusion.6), channel_id=1, source_target_pairs={{0,1},{1,0},{2,3},{3,2},{4,5},{5,4},{6,7},{7,6},{8,9},{9,8},{10,11... | collective-permute-start | bytes 786440 | tf_op jit(solution)/shard_map/while/body/ppermute | solution.py:46
  111.0 5.5 %collective-permute-start.16 = (bf16[128,512]{1,0:T(8,128)(2,1)S(1)}, bf16[128,512]{1,0:T(8,128)(2,1)S(1)}, u32[]{:S(2)}, u32[]{:S(2)}) collective-permute-start(bf16[128,512]{1,0:T(8,128)(2,1)S(1)} %collective-permute-done.13), channel_id=1, source_target_pairs={{0,14},{2,0},{4,2},{6,4},{8,6},{10,8},{12,10},{14,12},{1,15},{3,1}... | collective-permute-start | bytes 393224 | tf_op jit(solution)/shard_map/while/body/ppermute | solution.py:55
  116.5 4.0 %collective-permute-start.19 = (bf16[128,512]{1,0:T(8,128)(2,1)S(1)}, bf16[128,512]{1,0:T(8,128)(2,1)S(1)}, u32[]{:S(2)}, u32[]{:S(2)}) collective-permute-start(bf16[128,512]{1,0:T(8,128)(2,1)S(1)} %collective-permute-done.16), channel_id=1, source_target_pairs={{0,1},{1,0},{2,3},{3,2},{4,5},{5,4},{6,7},{7,6},{8,9},{9,8},{10,11... | collective-permute-start | bytes 393224 | tf_op jit(solution)/shard_map/while/body/ppermute | solution.py:46
  122.9 18.7 %copy-start.9 = (s32[1,1,128]{2,1,0:T(1,128)S(1)}, s32[1,1,128]{2,1,0:T(1,128)}, u32[]{:S(2)}) copy-start(s32[1,1,128]{2,1,0:T(1,128)} %get-tuple-element.1065) | copy-start | bytes 1540 | tf_op jit(solution)/shard_map/while
  122.9 18.7 %copy-start.7 = (f32[1,1,128]{2,1,0:T(1,128)S(1)}, f32[1,1,128]{2,1,0:T(1,128)}, u32[]{:S(2)}) copy-start(f32[1,1,128]{2,1,0:T(1,128)} %get-tuple-element.1063) | copy-start | bytes 1540 | tf_op jit(solution)/shard_map/while
  122.9 18.7 %copy-start.1 = (f32[1,1,128,512]{3,2,1,0:T(8,128)S(1)}, f32[1,1,128,512]{3,2,1,0:T(8,128)}, u32[]{:S(2)}) copy-start(f32[1,1,128,512]{3,2,1,0:T(8,128)} %get-tuple-element.1091) | copy-start | bytes 786436 | tf_op jit(solution)/shard_map/while
  122.9 18.7 %copy-start.2 = (f32[512]{0:T(512)S(1)}, f32[512]{0:T(512)}, u32[]{:S(2)}) copy-start(f32[512]{0:T(512)} %get-tuple-element.1216) | copy-start | bytes 6148 | tf_op jit(solution)/shard_map/while
  122.9 18.7 %copy-start.3 = (f32[1,1,128]{2,1,0:T(1,128)S(1)}, f32[1,1,128]{2,1,0:T(1,128)}, u32[]{:S(2)}) copy-start(f32[1,1,128]{2,1,0:T(1,128)} %get-tuple-element.1064) | copy-start | bytes 1540 | tf_op jit(solution)/shard_map/while
  142.9 30.7 %copy-start = (f32[128,512]{1,0:T(8,128)}, f32[128,512]{1,0:T(8,128)S(1)}, u32[]{:S(2)}) copy-start(f32[128,512]{1,0:T(8,128)S(1)} %get-tuple-element.592) | copy-start | bytes 786436
  143.6 2.0 %collective-permute-start.20 = (bf16[2,512]{1,0:T(2,128)(2,1)S(1)}, bf16[2,512]{1,0:T(2,128)(2,1)S(1)}, u32[]{:S(2)}, u32[]{:S(2)}) collective-permute-start(bf16[2,512]{1,0:T(2,128)(2,1)S(1)} %pad_maximum_fusion.2), channel_id=1, source_target_pairs={{0,1},{1,0},{2,3},{3,2},{4,5},{5,4},{6,7},{7,6},{8,9},{9,8},{10,11... | collective-permute-start | bytes 6152 | tf_op jit(solution)/shard_map/ppermute | solution.py:46
